TPU v7x, 512 devices: a whole 4x8x8 slice. The times are simulated.
512 devices in a mesh: row: 32 (over x_lo, z, core), col: 16 (over x_hi, y).
Axes of the slice: x: 4 (x_hi: 2, x_lo: 2; x = x_hi * 2 + x_lo), y: 8, z: 8, core: 2. Of those that a mesh axis runs over, the one named last changes fastest.
Arguments:
- starting_state: float32 [65536, 256], P(('row', 'col')), may hold values from -1 to 1
- features: float32 [65536, 128], P(('row', 'col')), may hold values from -6 to 6
- cotangent: float32 [65536, 256], P(('row', 'col')), may hold values from -6 to 6
- degrees: int32 [65536], P(('row', 'col')), may hold values from 8 to 64
- tile_values: bfloat16 [32, 16, 64, 128, 128], P('row', 'col'), may hold values from 0 to 1, as said below
- tile_rows: int32 [32, 16, 64], P('row', 'col'), may hold values from 0 to 15, as said below
- tile_cols: int32 [32, 16, 64], P('row', 'col'), may hold values from 0 to 31, as said below
- tile_live: int32 [32, 16, 64], P('row', 'col'), may hold values from 0 to 1, as said below
- weight: float32 [256, 256], replicated, may hold values from -0.375 to 0.375
- input_map: float32 [128, 256], replicated, may hold values from -0.5 to 0.5
Outputs:
- states: float32 [65536, 256], P(('row', 'col'))
- adjoint: float32 [65536, 256], P(('row', 'col'))
- weight_grad: float32 [256, 256], replicated
- input_grad: float32 [128, 256], replicated
Inputs may be any that keep to these rules, and one draw needn't show every extreme that they name: `tile_rows`: together with tile_cols, the slots of one device name distinct tiles. `tile_cols`: together with tile_rows, the slots of one device name distinct tiles. `tile_live`: on each device the live slots come first; every device has at least a quarter of its 64 slots live (and at least one), and some device has all 64 live. `tile_values`: roughly half of the entries of each tile are nonzero; nonzero weights lie in (0, 1].
All inputs are finite; a program needn't handle non-finite values.
Results may differ from a plain program's by a relative error of at most 0.012.
Values may be sent and summed in bfloat16 or wider, within the bound.
No kernel may reach another device: no remote copies, remote signals or barrier semaphores. Data moves between devices by JAX's collectives and lax.ppermute only.
A program may use at most 64 MiB of HBM per device.

v0:
```python
import math

import jax
import jax.numpy as jnp
from jax import lax
from jax.sharding import PartitionSpec as P

PRECISION_HIGH = lax.Precision.HIGHEST


def laid_out(parts, dim):
    parts = jnp.moveaxis(parts, 0, dim)
    dims = parts.shape
    return parts.reshape(*dims[:dim], dims[dim] * dims[dim + 1], *dims[dim + 2 :])


def copy_for_each(x, axis):
    devices = lax.axis_size(axis)
    return lax.all_to_all(jnp.broadcast_to(x[None], (devices, *x.shape)), axis, 0, 0, tiled=True)


def collect(x, axis, dim):
    return laid_out(copy_for_each(x, axis), dim)


def split_up(x, dim, devices):
    before, after = (x.shape[:dim], x.shape[dim + 1 :])
    return jnp.moveaxis(x.reshape(*before, devices, -1, *after), dim, 0)


def sent_and_summed(x, axis, dim):
    devices = lax.axis_size(axis)
    parts = lax.all_to_all(split_up(x, dim, devices), axis, 0, 0, tiled=True)
    return jnp.sum(parts.astype(jnp.float32), axis=0)


def in_one(arrays, axis):
    ravelled, at, gathered = (jnp.concatenate([a.reshape(-1) for a in arrays]), 0, [])
    so_far = lax.psum(ravelled, axis)
    for a in arrays:
        gathered.append(so_far[at : at + a.size].reshape(a.shape))
        at += a.size
    return tuple(gathered)


def spread_forward(values, rows_here, cols_here, live_here, gathered, first_tile, out_count):
    blocks = gathered.reshape(-1, values.shape[1], gathered.shape[1])
    picked = jnp.take(blocks, rows_here, axis=0)
    matrix_products = jnp.einsum("tab,taf->tbf", values, picked, preferred_element_type=jnp.float32)
    inside = (live_here == 1) & (cols_here >= 0) & (cols_here < out_count)
    labels = jnp.where(inside, cols_here, out_count)
    return jax.ops.segment_sum(matrix_products, labels, num_segments=out_count)


def spread_adjoint(values, rows_here, cols_here, live_here, gathered, first_tile, out_count):
    blocks = gathered.reshape(-1, values.shape[1], gathered.shape[1])
    picked = jnp.take(blocks, cols_here, axis=0)
    matrix_products = jnp.einsum("tab,tbf->taf", values, picked, preferred_element_type=jnp.float32)
    offset = rows_here - first_tile
    inside = (live_here == 1) & (offset >= 0) & (offset < out_count)
    labels = jnp.where(inside, offset, out_count)
    return jax.ops.segment_sum(matrix_products, labels, num_segments=out_count)


def tile_sum(kernel, values, rows_here, cols_here, live_here, gathered, first_tile, out_count):
    group_size = min(16, values.shape[0])
    live_count = jnp.sum(live_here)
    turn_count = (live_count + group_size - 1) // group_size

    def single_rotation(turn, totals):
        first_slot = turn * group_size
        return totals + kernel(
            lax.dynamic_slice_in_dim(values, first_slot, group_size, 0),
            lax.dynamic_slice_in_dim(rows_here, first_slot, group_size, 0),
            lax.dynamic_slice_in_dim(cols_here, first_slot, group_size, 0),
            lax.dynamic_slice_in_dim(live_here, first_slot, group_size, 0),
            gathered,
            first_tile,
            out_count,
        )

    initial = jnp.zeros((out_count, values.shape[1], gathered.shape[1]), jnp.float32)
    return lax.fori_loop(0, turn_count, single_rotation, initial)


def on_device(
    starting_state,
    features,
    cotangent,
    degrees,
    tile_values,
    tile_rows,
    tile_cols,
    tile_live,
    weight,
    input_map,
):
    values = tile_values[0, 0]
    rows_here = tile_rows[0, 0]
    cols_here = tile_cols[0, 0]
    live_here = tile_live[0, 0]
    node_count = starting_state.shape[0]
    width = starting_state.shape[1]
    block = values.shape[1]
    row_devices = lax.axis_size("row")
    col_devices = lax.axis_size("col")
    tile_row_count = col_devices * node_count // block
    reciprocal_square_root = lax.rsqrt(degrees.astype(jnp.float32))[:, None]
    driving = jnp.dot(features, input_map, precision=PRECISION_HIGH)
    states = starting_state
    scaled = (reciprocal_square_root * states).astype(jnp.bfloat16)
    gathered = collect(scaled, "col", 0)
    tile_count = node_count * lax.axis_size("row") // block
    part_sum = tile_sum(
        spread_forward,
        values,
        rows_here,
        cols_here,
        live_here,
        gathered,
        jnp.int32(0) // block,
        tile_count,
    )
    rounded = lax.optimization_barrier(
        part_sum.reshape(node_count * lax.axis_size("row"), width).astype(jnp.bfloat16)
    )
    own_rows = sent_and_summed(rounded.astype(jnp.float32).astype(jnp.bfloat16), "row", 0)
    summed = reciprocal_square_root * own_rows
    states = jnp.tanh(jnp.dot(summed, weight, precision=PRECISION_HIGH) + driving)
    slopes = 1.0 - states * states
    adjoint = cotangent
    scaled = (reciprocal_square_root * (slopes * adjoint)).astype(jnp.bfloat16)
    gathered = collect(scaled, "row", 0)
    partial_result_value = tile_sum(
        spread_adjoint, values, rows_here, cols_here, live_here, gathered, 0, tile_row_count
    )
    partial_result_value = partial_result_value.reshape(col_devices * node_count, width).astype(
        jnp.bfloat16
    )
    pulled = reciprocal_square_root * sent_and_summed(partial_result_value, "col", 0)
    adjoint = cotangent + jnp.dot(pulled, weight.T, precision=PRECISION_HIGH)
    masked = slopes * adjoint
    factor = 1.0 / math.sqrt(node_count * row_devices * col_devices)
    weight_part = jnp.dot(summed.T, masked, precision=PRECISION_HIGH)
    input_part = jnp.dot(features.T, masked, precision=PRECISION_HIGH)
    weight_grad, input_grad = in_one((weight_part, input_part), ("row", "col"))
    return (states, adjoint, weight_grad * factor, input_grad * factor)


def solution(mesh):
    return jax.shard_map(
        on_device,
        mesh=mesh,
        in_specs=(
            P(("row", "col"), None),
            P(("row", "col"), None),
            P(("row", "col"), None),
            P(("row", "col")),
            P("row", "col", None, None, None),
            P("row", "col", None),
            P("row", "col", None),
            P("row", "col", None),
            P(),
            P(),
        ),
        out_specs=(P(("row", "col"), None), P(("row", "col"), None), P(), P()),
        check_vma=False,
    )
```

profile of v0, /device:TPU:1, one launch (start us, length us, event | category | flops | bytes accessed | tf_op | source)
XLA Modules:
  0.0 551.0 jit_solution(5858859240928437864)
XLA Ops:
  10.0 10.3 %all-to-all-start = ((bf16[16,128,256]{2,1,0:T(8,128)(2,1)}), bf16[16,128,256]{2,1,0:T(8,128)(2,1)}, u32[]{:S(2)}, u32[]{:S(2)}) async-start(bf16[16,128,256]{2,1,0:T(8,128)(2,1)} %broadcast_in_dim.46), calls=%async_computation | async-start | bytes 2097152 | tf_op jit(solution)/shard_map/all_to_all | solution.py:19
  21.6 25.8 %all-to-all-done = bf16[16,128,256]{2,1,0:T(8,128)(2,1)} async-done(((bf16[16,128,256]{2,1,0:T(8,128)(2,1)}), bf16[16,128,256]{2,1,0:T(8,128)(2,1)}, u32[]{:S(2)}, u32[]{:S(2)}) %all-to-all-start) | async-done | bytes 1048608 | tf_op jit(solution)/shard_map/all_to_all | solution.py:19
  47.3 2.4 broadcast.56
  49.8 24.2 %while.20 = (s32[]{:T(128)}, f32[32,128,256]{2,1,0:T(8,128)}, s32[]{:T(128)}, s32[64]{0:T(128)S(1)}, s32[64]{0:T(128)S(1)}, /*index=5*/bf16[64,128,128]{2,1,0:T(...) while((s32[]{:T(128)}, f32[32,128,256]{2,1,0:T(8,128)}, ...), condition=%wide.region_3.4_spmd, body=%wide.region_1.3_spmd.sunk | while | flops 135267520 | bytes 12063439 | solution.py:83
  49.9 1.8 gather_fusion
  53.4 4.4 scatter_fusion
  57.9 1.8 gather_fusion
  61.4 4.5 scatter_fusion
  65.9 1.8 gather_fusion
  69.4 4.6 scatter_fusion
  74.0 3.8 convert_element_type.29
  77.8 13.0 %all-to-all-start.1 = ((bf16[32,128,256]{2,1,0:T(8,128)(2,1)}), bf16[32,128,256]{2,1,0:T(8,128)(2,1)S(1)}, u32[]{:S(2)}, u32[]{:S(2)}) async-start(bf16[32,128,256]{2,1,0:T(8,128)(2,1)} %bitcast.5), calls=%async_computation.1 | async-start | bytes 4194304 | tf_op jit(solution)/shard_map/all_to_all | solution.py:33
  91.1 49.0 %all-to-all-done.1 = bf16[32,128,256]{2,1,0:T(8,128)(2,1)S(1)} async-done(((bf16[32,128,256]{2,1,0:T(8,128)(2,1)}), bf16[32,128,256]{2,1,0:T(8,128)(2,1)S(1)}, u32[]{:S(2)}, u32[]{:S(2)}) %all-to-all-start.1) | async-done | bytes 2097184 | tf_op jit(solution)/shard_map/all_to_all | solution.py:33
  142.3 5.7 %all-to-all-start.2 = ((bf16[32,128,256]{2,1,0:T(8,128)(2,1)}), bf16[32,128,256]{2,1,0:T(8,128)(2,1)}, u32[]{:S(2)}, u32[]{:S(2)}) async-start(bf16[32,128,256]{2,1,0:T(8,128)(2,1)} %broadcast_in_dim.47), calls=%async_computation.2 | async-start | bytes 4194304 | tf_op jit(solution)/shard_map/all_to_all | solution.py:19
  148.1 49.4 %all-to-all-done.2 = bf16[32,128,256]{2,1,0:T(8,128)(2,1)} async-done(((bf16[32,128,256]{2,1,0:T(8,128)(2,1)}), bf16[32,128,256]{2,1,0:T(8,128)(2,1)}, u32[]{:S(2)}, u32[]{:S(2)}) %all-to-all-start.2) | async-done | bytes 2097184 | tf_op jit(solution)/shard_map/all_to_all | solution.py:19
  199.0 25.2 %while.21 = (s32[]{:T(128)}, f32[16,128,256]{2,1,0:T(8,128)}, s32[]{:T(128)}, s32[64]{0:T(128)S(1)}, s32[64]{0:T(128)S(1)}, /*index=5*/bf16[64,128,128]{2,1,0:T(...) while((s32[]{:T(128)}, f32[16,128,256]{2,1,0:T(8,128)}, ...), condition=%wide.region_7.8_spmd, body=%wide.region_5.7_spmd.sunk | while | flops 135267520 | bytes 12063439 | solution.py:83
  199.1 2.2 gather_fusion.1
  202.9 4.4 scatter_fusion.1
  207.4 2.2 gather_fusion.1
  211.2 4.4 scatter_fusion.1
  215.7 2.2 gather_fusion.1
  219.5 4.6 scatter_fusion.1
  225.9 43.6 %all_to_all.20 = bf16[16,128,256]{2,1,0:T(8,128)(2,1)S(1)} all-to-all(bf16[16,128,256]{2,1,0:T(8,128)(2,1)S(1)} %convert_element_type.33), channel_id=1, replica_groups=mesh['row'=32,'col'=16] {'col'}, dimensions={0} | all-to-all | bytes 2097152 | tf_op jit(solution)/shard_map/all_to_all | solution.py:33
  272.2 268.7 %all-reduce.2.cloned.1.call-done = f32[98304]{0:T(1024)} async-done(((f32[98304]{0:T(1024)}), f32[98304]{0:T(1024)}) %all-reduce.2.cloned.1.call-update) | async-done | bytes 393232 | tf_op jit(solution)/shard_map/psum | solution.py:39
  (78 shorter events, 25.4 us)
Async XLA Ops:
  7.2 133.2 %copy-start = (f32[256,256]{1,0:T(8,128)S(1)}, f32[256,256]{1,0:T(8,128)}, u32[]{:S(2)}) copy-start(f32[256,256]{1,0:T(8,128)} %param.22) | copy-start | bytes 786436
  7.2 13.1 %copy-start.10 = (s32[1,1,64]{2,1,0:T(1,128)S(1)}, s32[1,1,64]{2,1,0:T(1,128)}, u32[]{:S(2)}) copy-start(s32[1,1,64]{2,1,0:T(1,128)} %param.21) | copy-start | bytes 772
  7.9 132.5 %copy-start.13 = (f32[128]{0:T(128)}, f32[128]{0:T(128)S(1)}, u32[]{:S(2)}) copy-start(f32[128]{0:T(128)S(1)} %convert_rsqrt_fusion) | copy-start | bytes 1540
  10.0 37.4 %all-to-all-start = ((bf16[16,128,256]{2,1,0:T(8,128)(2,1)}), bf16[16,128,256]{2,1,0:T(8,128)(2,1)}, u32[]{:S(2)}, u32[]{:S(2)}) async-start(bf16[16,128,256]{2,1,0:T(8,128)(2,1)} %broadcast_in_dim.46), calls=%async_computation | async-start | bytes 2097152 | tf_op jit(solution)/shard_map/all_to_all | solution.py:19
  47.3 2.5 copy-start.11
  47.3 2.5 copy-start.12
  77.8 13.0 %copy-start.7 = (f32[128,128]{1,0:T(8,128)S(1)}, f32[128,128]{1,0:T(8,128)}, u32[]{:S(2)}) copy-start(f32[128,128]{1,0:T(8,128)} %param.15) | copy-start | bytes 196612
  77.8 13.0 %copy-start.9 = (f32[128,256]{1,0:T(8,128)S(1)}, f32[128,256]{1,0:T(8,128)}, u32[]{:S(2)}) copy-start(f32[128,256]{1,0:T(8,128)} %param.23) | copy-start | bytes 393220
  77.8 62.3 %all-to-all-start.1 = ((bf16[32,128,256]{2,1,0:T(8,128)(2,1)}), bf16[32,128,256]{2,1,0:T(8,128)(2,1)S(1)}, u32[]{:S(2)}, u32[]{:S(2)}) async-start(bf16[32,128,256]{2,1,0:T(8,128)(2,1)} %bitcast.5), calls=%async_computation.1 | async-start | bytes 4194304 | tf_op jit(solution)/shard_map/all_to_all | solution.py:33
  90.9 49.5 %copy-start.5 = (f32[128,256]{1,0:T(8,128)S(1)}, f32[128,256]{1,0:T(8,128)}, u32[]{:S(2)}) copy-start(f32[128,256]{1,0:T(8,128)} %param.16) | copy-start | bytes 393220
  140.4 1.9 copy-start.2
  140.8 129.9 %copy-start.1 = (f32[128,256]{1,0:T(8,128)}, f32[128,256]{1,0:T(8,128)S(1)}, u32[]{:S(2)}) copy-start(f32[128,256]{1,0:T(8,128)S(1)} %get-tuple-element.145) | copy-start | bytes 393220
  142.3 55.1 %all-to-all-start.2 = ((bf16[32,128,256]{2,1,0:T(8,128)(2,1)}), bf16[32,128,256]{2,1,0:T(8,128)(2,1)}, u32[]{:S(2)}, u32[]{:S(2)}) async-start(bf16[32,128,256]{2,1,0:T(8,128)(2,1)} %broadcast_in_dim.47), calls=%async_computation.2 | async-start | bytes 4194304 | tf_op jit(solution)/shard_map/all_to_all | solution.py:19
  148.0 392.8 %all-reduce.2.cloned.1.call-start = ((), (), s32[]{:S(2)}) async-start(), calls=%async_computation.4 | async-start | bytes 786432 | tf_op jit(solution)/shard_map/psum | solution.py:39
  225.8 43.8 %copy-start.6 = (f32[128,256]{1,0:T(8,128)S(1)}, f32[128,256]{1,0:T(8,128)}, u32[]{:S(2)}) copy-start(f32[128,256]{1,0:T(8,128)} %param.16) | copy-start | bytes 393220
  225.9 43.8 %copy-start.14 = (f32[128]{0:T(128)S(1)}, f32[128]{0:T(128)}, u32[]{:S(2)}) copy-start(f32[128]{0:T(128)} %copy-done.13) | copy-start | bytes 1540
  225.9 44.3 %copy-start.3 = (f32[128,256]{1,0:T(8,128)S(1)}, f32[128,256]{1,0:T(8,128)}, u32[]{:S(2)}) copy-start(f32[128,256]{1,0:T(8,128)} %copy-done.2) | copy-start | bytes 393220
  225.9 44.8 %copy-start.8 = (f32[128,128]{1,0:T(8,128)S(1)}, f32[128,128]{1,0:T(8,128)}, u32[]{:S(2)}) copy-start(f32[128,128]{1,0:T(8,128)} %param.15) | copy-start | bytes 196612
  270.1 272.5 %copy-start.4 = (f32[128,256]{1,0:T(8,128)}, f32[128,256]{1,0:T(8,128)S(1)}, u32[]{:S(2)}) copy-start(f32[128,256]{1,0:T(8,128)S(1)} %convolution_add_fusion) | copy-start | bytes 393220
Sparse Core Ops, SparseCore 0:
  272.3 268.5 all-reduce.1
where the time goes:
time: 553 us; the launch traced here: 551 us
  waiting for transfers between devices  393 us (71%)
  blocking collectives  43.6 us (8%)
  other arithmetic  38.8 us (7%)
  starting transfers between devices  29 us (5%)
  local copies, waits for them, and re-layouts  20.6 us (4%)
  between operations  15 us (3%)
  matrix products  11.2 us (2%)
    psum x1, waiting for transfers between devices, in_one(): so_far = lax.psum(ravelled, axis)  269 us
    all_to_all x2, waiting for transfers between devices, copy_for_each(): lax.all_to_all(jnp.broadcast_to(x[None], (devices, *x.shape)), axis, 0, 0...  75.1 us
    all_to_all x1, waiting for transfers between devices, sent_and_summed(): parts = lax.all_to_all(split_up(x, dim, devices), axis, 0, 0, tiled=True)  49 us
    all_to_all x1, blocking collectives, sent_and_summed(): parts = lax.all_to_all(split_up(x, dim, devices), axis, 0, 0, tiled=True)  43.6 us
    all_to_all x2, starting transfers between devices, copy_for_each(): lax.all_to_all(jnp.broadcast_to(x[None], (devices, *x.shape)), axis, 0, 0...  15.9 us
    scatter-add x3, other arithmetic, spread_forward(): return jax.ops.segment_sum(matrix_products, labels, num_segments=out_count)  13.5 us
    scatter-add x3, other arithmetic, spread_adjoint(): return jax.ops.segment_sum(matrix_products, labels, num_segments=out_count)  13.3 us
    all_to_all x1, starting transfers between devices, sent_and_summed(): parts = lax.all_to_all(split_up(x, dim, devices), axis, 0, 0, tiled=True)  13 us
  transfers between devices with their start and end apart: 4, of which 4 were waited for; matrix products, arithmetic and copies ran while one was open for 0% of the time, Pallas kernels for 0%

commit v1 on v0

v1 whole, which is shorter than its diff:
```python
import functools
import math

import jax
import jax.numpy as jnp
from jax import lax
from jax.experimental import pallas as pl
from jax.experimental.pallas import tpu as pltpu
from jax.sharding import Mesh, PartitionSpec as P

HIGH = lax.Precision.HIGHEST
BF16 = jnp.bfloat16
F32 = jnp.float32
CHIP = ("xl", "z")
COL = ("xh", "y")
ROW = ("xl", "z", "core")
UNROLL = 4
VMEM = pl.BlockSpec(memory_space=pltpu.VMEM)
SMEM = pl.BlockSpec(memory_space=pltpu.SMEM)
ANY = pl.BlockSpec(memory_space=pl.ANY)


def shape(dims, dtype):
    return jax.ShapeDtypeStruct(dims, dtype)


def first_kernel(state, inv_col, out):
    scaled = jnp.transpose(state[...] * inv_col[...]).astype(BF16)
    for q in range(out.shape[0]):
        out[q] = scaled


def live_count(live):
    return lax.fori_loop(0, live.shape[0], lambda t, n: n + live[t], jnp.int32(0))


def place(c, core, half):
    return ((c & 1) ^ core) * half + (c >> 1)


def forward_kernel(rows, cols, live, core_ref, values, blocks, keep, send, acc):
    core = core_ref[0]
    half = keep.shape[0]
    acc[...] = jnp.zeros_like(acc)

    def group(g, carry):
        products, slots = [], []
        for u in range(UNROLL):
            t = g * UNROLL + u
            slot = place(cols[t], core, half)
            slots.append(jnp.where(live[t] == 1, slot, 2 * half))
            products.append(
                jnp.dot(blocks[rows[t]], values[t], preferred_element_type=F32)
            )
        for slot, product in zip(slots, products):
            acc[slot] += product
        return carry

    lax.fori_loop(0, (live_count(live) + UNROLL - 1) // UNROLL, group, 0)
    keep[...] = acc[0:half].astype(BF16)
    send[...] = acc[half : 2 * half].astype(BF16)


def adjoint_kernel(rows, cols, live, core_ref, values, own, other, out, blocks, acc, sem):
    core = core_ref[0]
    half = own.shape[0]
    count = out.shape[0]
    copies = [
        pltpu.make_async_copy(own, blocks.at[pl.ds(0, half)], sem.at[0]),
        pltpu.make_async_copy(other, blocks.at[pl.ds(half, half)], sem.at[1]),
    ]
    for copy in copies:
        copy.start()
    acc[...] = jnp.zeros_like(acc)
    groups = (live_count(live) + UNROLL - 1) // UNROLL
    for copy in copies:
        copy.wait()

    def group(g, carry):
        products, slots = [], []
        for u in range(UNROLL):
            t = g * UNROLL + u
            slots.append(jnp.where(live[t] == 1, rows[t], count))
            block = blocks[place(cols[t], core, half)]
            products.append(jnp.dot(values[t], block, preferred_element_type=F32))
        for slot, product in zip(slots, products):
            acc[slot] += product
        return carry

    lax.fori_loop(0, groups, group, 0)
    out[...] = acc[0:count].astype(BF16)


def state_kernel(parts, inv_row, inv_col, weight, features, input_map, cotangent, states, summed_t, out):
    total = parts[0].astype(F32)
    for q in range(1, parts.shape[0]):
        total += parts[q].astype(F32)
    total = total * inv_row[...]
    summed_t[...] = total
    driving = jnp.dot(features[...], input_map[...], precision=HIGH, preferred_element_type=F32)
    moved = lax.dot_general(
        jnp.transpose(total), weight[...], (((1,), (0,)), ((), ())), precision=HIGH, preferred_element_type=F32
    )
    state = jnp.tanh(moved + driving)
    states[...] = state
    slopes = 1.0 - state * state
    scaled = (inv_col[...] * (slopes * cotangent[...])).astype(BF16)
    for q in range(out.shape[0]):
        out[q] = scaled


def grad_kernel(core_ref, parts, inv_col, cotangent, weight, states, summed_t, features, adjoint, keep, send, *, factor):
    total = parts[0].astype(F32)
    for q in range(1, parts.shape[0]):
        total += parts[q].astype(F32)
    pulled = total * inv_col[...]
    moved = lax.dot_general(
        pulled, weight[...], (((1,), (1,)), ((), ())), precision=HIGH, preferred_element_type=F32
    )
    result = cotangent[...] + moved
    adjoint[...] = result
    state = states[...]
    masked = (1.0 - state * state) * result * factor
    weight_part = jnp.dot(summed_t[...], masked, precision=HIGH, preferred_element_type=F32)
    input_part = jnp.dot(
        jnp.transpose(features[...]), masked, precision=HIGH, preferred_element_type=F32
    )
    first = core_ref[0] == 0
    width = weight_part.shape[0]
    half = weight_part.shape[1] // 2
    for at, part in ((0, weight_part), (width, input_part)):
        left, right = part[:, :half], part[:, half:]
        keep[at : at + part.shape[0], :] = jnp.where(first, left, right)
        send[at : at + part.shape[0], :] = jnp.where(first, right, left)


def sum_kernel(parts, out):
    total = parts[0].astype(F32)
    for q in range(1, parts.shape[0]):
        total += parts[q].astype(F32)
    total = total.astype(out.dtype)
    for q in range(out.shape[0]):
        out[q] = total


def last_kernel(core_ref, own, other, weight_grad, input_grad):
    first = core_ref[0] == 0
    width = weight_grad.shape[0]
    half = own.shape[1]
    for at, out in ((0, weight_grad), (width, input_grad)):
        mine = own[at : at + out.shape[0], :].astype(F32)
        theirs = other[at : at + out.shape[0], :].astype(F32)
        out[:, :half] = jnp.where(first, mine, theirs)
        out[:, half:] = jnp.where(first, theirs, mine)


def call(kernel, outs, specs, scratch=(), name=None):
    return pl.pallas_call(
        kernel,
        out_shape=outs,
        in_specs=specs,
        out_specs=jax.tree.map(lambda _: VMEM, outs),
        scratch_shapes=list(scratch),
        name=name,
    )


def swap(x):
    return lax.ppermute(x, "core", [(0, 1), (1, 0)])


def exchange(x, axes):
    return lax.all_to_all(x, axes, 0, 0, tiled=True)


def on_device(
    starting_state,
    features,
    cotangent,
    degrees,
    tile_values,
    tile_rows,
    tile_cols,
    tile_live,
    weight,
    input_map,
):
    values = tile_values[0, 0]
    rows, cols, live = tile_rows[0, 0], tile_cols[0, 0], tile_live[0, 0]
    nodes, width = starting_state.shape
    inputs = features.shape[1]
    chips = lax.axis_size("xl") * lax.axis_size("z")
    col_devices = lax.axis_size("xh") * lax.axis_size("y")
    core = lax.axis_index("core").astype(jnp.int32).reshape(1)
    inverse = lax.rsqrt(degrees.astype(F32))
    inv_row, inv_col = inverse.reshape(1, nodes), inverse.reshape(nodes, 1)
    block = values.shape[1]

    spread = call(
        first_kernel, shape((col_devices, width, nodes), BF16), [VMEM] * 2, name="first"
    )(starting_state, inv_col)
    gathered = exchange(spread, COL)
    keep, send = call(
        forward_kernel,
        (shape((chips, width, block), BF16),) * 2,
        [SMEM] * 4 + [VMEM] * 2,
        [pltpu.VMEM((2 * chips + 1, width, block), F32)],
        name="forward",
    )(rows, cols, live, core, values, gathered)
    parts = exchange((keep.astype(F32) + swap(send).astype(F32)).astype(BF16), CHIP)
    states, summed_t, spread = call(
        state_kernel,
        (shape((nodes, width), F32), shape((width, nodes), F32), shape((chips, nodes, width), BF16)),
        [VMEM] * 7,
        name="state",
    )(parts, inv_row, inv_col, weight, features, input_map, cotangent)
    own = exchange(spread, CHIP)
    other = swap(own)
    partial = call(
        adjoint_kernel,
        shape((col_devices, block, width), BF16),
        [SMEM] * 4 + [VMEM] + [ANY] * 2,
        [
            pltpu.VMEM((2 * chips, block, width), BF16),
            pltpu.VMEM((col_devices + 1, block, width), F32),
            pltpu.SemaphoreType.DMA((2,)),
        ],
        name="adjoint",
    )(rows, cols, live, core, values, own, other)
    parts = exchange(partial, COL)
    factor = 1.0 / math.sqrt(nodes * 2 * chips * col_devices)
    total = width + inputs
    adjoint, keep, send = call(
        functools.partial(grad_kernel, factor=factor),
        (shape((nodes, width), F32), shape((total, width // 2), F32), shape((total, width // 2), F32)),
        [SMEM] + [VMEM] * 7,
        name="grad",
    )(core, parts, inv_col, cotangent, weight, states, summed_t, features)
    piece = (total // chips, width // 2)
    halves = (keep + swap(send)).reshape(chips, *piece)
    parts = exchange(halves, CHIP)
    spread = call(sum_kernel, shape((col_devices, *piece), F32), [VMEM], name="sum_chip")(parts)
    parts = exchange(spread, COL)
    spread = call(sum_kernel, shape((chips, *piece), BF16), [VMEM], name="sum_col")(parts)
    own = exchange(spread, CHIP).reshape(total, width // 2)
    other = swap(own)
    weight_grad, input_grad = call(
        last_kernel,
        (shape((width, width), F32), shape((inputs, width), F32)),
        [SMEM] + [VMEM] * 2,
        name="last",
    )(core, own, other)
    return states, adjoint, weight_grad, input_grad


def solution(mesh):
    sizes = mesh.devices.shape
    fine = Mesh(
        mesh.devices.reshape(2, sizes[0] // 4, 2, 2, sizes[1] // 2),
        ("xl", "z", "core", "xh", "y"),
    )
    every = ROW + COL
    return jax.shard_map(
        on_device,
        mesh=fine,
        in_specs=(
            P(every, None),
            P(every, None),
            P(every, None),
            P(every),
            P(ROW, COL, None, None, None),
            P(ROW, COL, None),
            P(ROW, COL, None),
            P(ROW, COL, None),
            P(),
            P(),
        ),
        out_specs=(P(every, None), P(every, None), P(), P()),
        check_vma=False,
    )
```

time: 553 us -> 237 us (0.43)
  waiting for transfers between devices: 393 us -> 34 us
  blocking collectives: 43.6 us -> 139 us
  other arithmetic: 38.8 us -> 3.63 us
  Pallas kernels: 0 us -> 25 us
  local copies, waits for them, and re-layouts: 20.6 us -> 3.33 us
  between operations: 15 us -> 0.7 us
  matrix products: 11.2 us -> 0 us
    psum x1 -> x0, waiting for transfers between devices: 269 us -> none  [in_one(): so_far = lax.psum(ravelled, axis)]
    all_to_all x3 -> x1, waiting for transfers between devices: 124 us -> 27 us  [exchange(): return lax.all_to_all(x, axes, 0, 0, tiled=True)]
    all_to_all x1 -> x6, blocking collectives: 43.6 us -> 139 us  [exchange(): return lax.all_to_all(x, axes, 0, 0, tiled=True)]
    scatter-add x6 -> x0, other arithmetic: 26.9 us -> none  [the longest x3 13.5 us: spread_forward(): return jax.ops.segment_sum(matrix_products, labels, num_segments=out_count)]
    pallas_call x0 -> x8, Pallas kernels: none -> 25 us  [the longest x1 5.83 us: on_device(): call(adjoint_kernel, shape((col_devices, block, width), BF16), [SMEM] * 4...]
    ppermute x0 -> x4, starting transfers between devices: none -> 19.5 us  [swap(): return lax.ppermute(x, 'core', [(0, 1), (1, 0)])]
    all_to_all x3 -> x1, starting transfers between devices: 28.9 us -> 10.2 us  [exchange(): return lax.all_to_all(x, axes, 0, 0, tiled=True)]
    gather x6 -> x0, local copies, waits for them, and re-layouts: 12.1 us -> none  [the longest x3 6.61 us: spread_adjoint(): picked = jnp.take(blocks, cols_here, axis=0)]
  transfers between devices with their start and end apart: 4 -> 5, of which waited for: 4 -> 5; matrix products, arithmetic and copies ran while one was open for 0% -> 0% of each run, Pallas kernels for 0% -> 0%
where the time goes in v1:
time: 237 us; the launch traced here: 235 us
  blocking collectives  139 us (59%)
  waiting for transfers between devices  34 us (14%)
  starting transfers between devices  29.7 us (13%)
  Pallas kernels  25 us (11%)
  other arithmetic  3.63 us (2%)
  local copies, waits for them, and re-layouts  3.33 us (1%)
    all_to_all x6, blocking collectives, exchange(): return lax.all_to_all(x, axes, 0, 0, tiled=True)  139 us
    all_to_all x1, waiting for transfers between devices, exchange(): return lax.all_to_all(x, axes, 0, 0, tiled=True)  27 us
    ppermute x4, starting transfers between devices, swap(): return lax.ppermute(x, 'core', [(0, 1), (1, 0)])  19.5 us
    all_to_all x1, starting transfers between devices, exchange(): return lax.all_to_all(x, axes, 0, 0, tiled=True)  10.2 us
    ppermute x4, waiting for transfers between devices, swap(): return lax.ppermute(x, 'core', [(0, 1), (1, 0)])  6.92 us
    pallas_call x1, Pallas kernels, on_device(): call(adjoint_kernel, shape((col_devices, block, width), BF16), [SMEM] * 4...  5.83 us
    pallas_call x1, Pallas kernels, on_device(): call(forward_kernel, (shape((chips, width, block), BF16),) * 2, [SMEM] *...  5.49 us
  transfers between devices with their start and end apart: 5, of which 5 were waited for; matrix products, arithmetic and copies ran while one was open for 0% of the time, Pallas kernels for 0%

profile of v1, /device:TPU:1, one launch (start us, length us, event | category | flops | bytes accessed | tf_op | source)
XLA Modules:
  0.0 235.2 jit_solution(2328764858739032878)
XLA Ops:
  2.5 2.1 first.1
  4.7 10.2 %all-to-all-start = ((bf16[16,256,128]{2,1,0:T(8,128)(2,1)}), bf16[16,256,128]{2,1,0:T(8,128)(2,1)S(1)}, u32[]{:S(2)}, u32[]{:S(2)}) async-start(bf16[16,256,128]{2,1,0:T(8,128)(2,1)} %first.1), calls=%async_computation | async-start | bytes 2097152 | tf_op jit(solution)/shard_map/all_to_all | solution.py:173
  14.9 27.0 %all-to-all-done.blocks = bf16[16,256,128]{2,1,0:T(8,128)(2,1)S(1)} async-done(((bf16[16,256,128]{2,1,0:T(8,128)(2,1)}), bf16[16,256,128]{2,1,0:T(8,128)(2,1)S(1)}, u32[]{:S(2)}, u32[]{:S(2)}) %all-to-all-start) | async-done | bytes 1048608 | tf_op jit(solution)/shard_map/all_to_all | solution.py:173
  42.9 5.5 %forward.1 = (bf16[16,256,128]{2,1,0:T(8,128)(2,1)}, bf16[16,256,128]{2,1,0:T(8,128)(2,1)}) custom-call(s32[64]{0:T(128)} %bitcast.16, s32[64]{0:T(128)} %bitcast.18, s32[64]{0:T(128)} %bitcast.20, s32[1]{0:T(128)} %bitcast.3.core_ref, bf16[64,128,128]{2,1,0:T(8,128)(2,1)} %bitcast.11, bf16[16,256,128]{2,1,0:T(8,128)(2,1)} %copy-done.1), custom_call_target="tpu_custom_call" | custom-call | tf_op jit(solution)/shard_map/forward/pallas_call | solution.py:203
  48.4 4.4 %collective-permute-start = (bf16[16,256,128]{2,1,0:T(8,128)(2,1)}, bf16[16,256,128]{2,1,0:T(8,128)(2,1)S(1)}, u32[]{:S(2)}, u32[]{:S(2)}) collective-permute-start(bf16[16,256,128]{2,1,0:T(8,128)(2,1)} %get-tuple-element.15), channel_id=1, source_target_pairs={{0,16},{16,0},{1,17},{17,1},{2,18},{18,2},{3,19},{19,3},{4,20},{20... | collective-permute-start | bytes 3145736 | tf_op jit(solution)/shard_map/ppermute | solution.py:169
  52.9 2.5 %collective-permute-done = bf16[16,256,128]{2,1,0:T(8,128)(2,1)S(1)} collective-permute-done((bf16[16,256,128]{2,1,0:T(8,128)(2,1)}, bf16[16,256,128]{2,1,0:T(8,128)(2,1)S(1)}, u32[]{:S(2)}, u32[]{:S(2)}) %collective-permute-start) | collective-permute-done | bytes 1048608 | tf_op jit(solution)/shard_map/ppermute | solution.py:169
  55.3 1.5 add_convert_fusion
  56.8 35.8 %all_to_all.35.parts = bf16[16,256,128]{2,1,0:T(8,128)(2,1)} all-to-all(bf16[16,256,128]{2,1,0:T(8,128)(2,1)S(1)} %add_convert_fusion), channel_id=1, replica_groups=mesh['xl'=2,'z'=8,'core'=2,'xh'=2,'y'=8] {'xl','z'}, dimensions={0} | all-to-all | bytes 2097152 | tf_op jit(solution)/shard_map/all_to_all | solution.py:173
  92.6 3.1 %state.3 = (f32[128,256]{1,0:T(8,128)}, f32[256,128]{1,0:T(8,128)}, bf16[16,128,256]{2,1,0:T(8,128)(2,1)}) custom-call(bf16[16,256,128]{2,1,0:T(8,128)(2,1)} %all_to_all.35.parts, f32[1,128]{1,0:T(1,128)} %get-tuple-element.24.inv_row, f32[128,1]{1,0:T(8,128)} %copy.14.inv_col, f32[256,256]{1,0:T(8,128)} %weight.3, f32[128,128]{1,0:T(8,128)} %features.3, ...), custom_call_target="tpu_custom_call" | custom-call | tf_op jit(solution)/shard_map/state/pallas_call | solution.py:211
  95.7 32.0 %all_to_all.36.own = bf16[16,128,256]{2,1,0:T(8,128)(2,1)S(1)} all-to-all(bf16[16,128,256]{2,1,0:T(8,128)(2,1)} %get-tuple-element.17), channel_id=1, replica_groups=mesh['xl'=2,'z'=8,'core'=2,'xh'=2,'y'=8] {'xl','z'}, dimensions={0} | all-to-all | bytes 2097152 | tf_op jit(solution)/shard_map/all_to_all | solution.py:173
  127.6 4.5 %collective-permute-start.1 = (bf16[16,128,256]{2,1,0:T(8,128)(2,1)S(1)}, bf16[16,128,256]{2,1,0:T(8,128)(2,1)S(1)}, u32[]{:S(2)}, u32[]{:S(2)}) collective-permute-start(bf16[16,128,256]{2,1,0:T(8,128)(2,1)S(1)} %all_to_all.36.own), channel_id=1, source_target_pairs={{0,16},{16,0},{1,17},{17,1},{2,18},{18,2},{3,19},{19,3},{4,20},{20... | collective-permute-start | bytes 3145736 | tf_op jit(solution)/shard_map/ppermute | solution.py:169
  132.1 2.3 collective-permute-done.1.other
  135.4 5.8 %adjoint.1 = bf16[16,128,256]{2,1,0:T(8,128)(2,1)} custom-call(s32[64]{0:T(128)} %bitcast.17, s32[64]{0:T(128)} %bitcast.19, s32[64]{0:T(128)} %bitcast.21, s32[1]{0:T(128)} %bitcast.3.core_ref, bf16[64,128,128]{2,1,0:T(8,128)(2,1)} %bitcast.12, bf16[16,128,256]{2,1,0:T(8,128)(2,1)} %copy-done, bf16[16,128,256]{2,1,0:T(8,128)(2,1)} %copy-done.2), custom_call_target="tpu_custom_call" | custom-call | tf_op jit(solution)/shard_map/adjoint/pallas_call | solution.py:219
  141.2 32.6 %all_to_all.37.parts = bf16[16,128,256]{2,1,0:T(8,128)(2,1)} all-to-all(bf16[16,128,256]{2,1,0:T(8,128)(2,1)} %adjoint.1), channel_id=1, replica_groups=mesh['xl'=2,'z'=8,'core'=2,'xh'=2,'y'=8] {'xh','y'}, dimensions={0} | all-to-all | bytes 2097152 | tf_op jit(solution)/shard_map/all_to_all | solution.py:173
  173.8 3.5 %grad.1 = (f32[128,256]{1,0:T(8,128)}, f32[384,128]{1,0:T(8,128)}, f32[384,128]{1,0:T(8,128)}) custom-call(s32[1]{0:T(128)} %bitcast.3.core_ref, bf16[16,128,256]{2,1,0:T(8,128)(2,1)} %all_to_all.37.parts, f32[128,1]{1,0:T(8,128)} %copy.14.inv_col, f32[128,256]{1,0:T(8,128)} %cotangent.3, f32[256,256]{1,0:T(8,128)} %weight.3, ...), custom_call_target="tpu_custom_call" | custom-call | tf_op jit(solution)/shard_map/grad/pallas_call | solution.py:233
  177.3 4.4 %collective-permute-start.2 = (f32[384,128]{1,0:T(8,128)}, f32[384,128]{1,0:T(8,128)S(1)}, u32[]{:S(2)}, u32[]{:S(2)}) collective-permute-start(f32[384,128]{1,0:T(8,128)} %get-tuple-element.21), channel_id=1, source_target_pairs={{0,16},{16,0},{1,17},{17,1},{2,18},{18,2},{3,19},{19,3},{4,20},{20... | collective-permute-start | bytes 589832 | tf_op jit(solution)/shard_map/ppermute | solution.py:169
  181.7 1.3 collective-permute-done.2
  183.9 12.4 %all_to_all.38.parts = f32[16,24,128]{2,1,0:T(8,128)} all-to-all(f32[16,24,128]{2,1,0:T(8,128)S(1)} %bitcast.13), channel_id=1, replica_groups=mesh['xl'=2,'z'=8,'core'=2,'xh'=2,'y'=8] {'xl','z'}, dimensions={0} | all-to-all | bytes 393216 | tf_op jit(solution)/shard_map/all_to_all | solution.py:173
  196.4 1.6 sum_chip.1
  198.0 13.8 %all_to_all.39.parts = f32[16,24,128]{2,1,0:T(8,128)} all-to-all(f32[16,24,128]{2,1,0:T(8,128)} %sum_chip.1), channel_id=1, replica_groups=mesh['xl'=2,'z'=8,'core'=2,'xh'=2,'y'=8] {'xh','y'}, dimensions={0} | all-to-all | bytes 393216 | tf_op jit(solution)/shard_map/all_to_all | solution.py:173
  211.8 1.6 sum_col.1
  213.3 12.4 %all_to_all.40 = bf16[16,24,128]{2,1,0:T(8,128)(2,1)S(1)} all-to-all(bf16[16,24,128]{2,1,0:T(8,128)(2,1)} %sum_col.1), channel_id=1, replica_groups=mesh['xl'=2,'z'=8,'core'=2,'xh'=2,'y'=8] {'xl','z'}, dimensions={0} | all-to-all | bytes 196608 | tf_op jit(solution)/shard_map/all_to_all | solution.py:173
  225.8 6.2 %collective-permute-start.3 = (bf16[384,128]{1,0:T(8,128)(2,1)S(1)}, bf16[384,128]{1,0:T(8,128)(2,1)S(1)}, u32[]{:S(2)}, u32[]{:S(2)}) collective-permute-start(bf16[384,128]{1,0:T(8,128)(2,1)S(1)} %bitcast.14), channel_id=1, source_target_pairs={{0,16},{16,0},{1,17},{17,1},{2,18},{18,2},{3,19},{19,3},{4,20},{20... | collective-permute-start | bytes 294920 | tf_op jit(solution)/shard_map/ppermute | solution.py:169
  233.5 1.7 last.1
  (14 shorter events, 6.4 us)
Async XLA Ops:
  4.7 37.3 %all-to-all-start = ((bf16[16,256,128]{2,1,0:T(8,128)(2,1)}), bf16[16,256,128]{2,1,0:T(8,128)(2,1)S(1)}, u32[]{:S(2)}, u32[]{:S(2)}) async-start(bf16[16,256,128]{2,1,0:T(8,128)(2,1)} %first.1), calls=%async_computation | async-start | bytes 2097152 | tf_op jit(solution)/shard_map/all_to_all | solution.py:173
  41.9 1.0 copy-start.1
  48.4 6.9 %collective-permute-start = (bf16[16,256,128]{2,1,0:T(8,128)(2,1)}, bf16[16,256,128]{2,1,0:T(8,128)(2,1)S(1)}, u32[]{:S(2)}, u32[]{:S(2)}) collective-permute-start(bf16[16,256,128]{2,1,0:T(8,128)(2,1)} %get-tuple-element.15), channel_id=1, source_target_pairs={{0,16},{16,0},{1,17},{17,1},{2,18},{18,2},{3,19},{19,3},{4,20},{20... | collective-permute-start | bytes 3145736 | tf_op jit(solution)/shard_map/ppermute | solution.py:169
  127.6 6.8 %copy-start = (bf16[16,128,256]{2,1,0:T(8,128)(2,1)}, bf16[16,128,256]{2,1,0:T(8,128)(2,1)S(1)}, u32[]{:S(2)}) copy-start(bf16[16,128,256]{2,1,0:T(8,128)(2,1)S(1)} %all_to_all.36.own) | copy-start | bytes 3145732
  127.6 6.7 %collective-permute-start.1 = (bf16[16,128,256]{2,1,0:T(8,128)(2,1)S(1)}, bf16[16,128,256]{2,1,0:T(8,128)(2,1)S(1)}, u32[]{:S(2)}, u32[]{:S(2)}) collective-permute-start(bf16[16,128,256]{2,1,0:T(8,128)(2,1)S(1)} %all_to_all.36.own), channel_id=1, source_target_pairs={{0,16},{16,0},{1,17},{17,1},{2,18},{18,2},{3,19},{19,3},{4,20},{20... | collective-permute-start | bytes 3145736 | tf_op jit(solution)/shard_map/ppermute | solution.py:169
  134.4 1.0 copy-start.2
  177.3 5.7 %collective-permute-start.2 = (f32[384,128]{1,0:T(8,128)}, f32[384,128]{1,0:T(8,128)S(1)}, u32[]{:S(2)}, u32[]{:S(2)}) collective-permute-start(f32[384,128]{1,0:T(8,128)} %get-tuple-element.21), channel_id=1, source_target_pairs={{0,16},{16,0},{1,17},{17,1},{2,18},{18,2},{3,19},{19,3},{4,20},{20... | collective-permute-start | bytes 589832 | tf_op jit(solution)/shard_map/ppermute | solution.py:169
  225.8 7.1 %copy-start.3 = (bf16[16,24,128]{2,1,0:T(8,128)(2,1)}, bf16[16,24,128]{2,1,0:T(8,128)(2,1)S(1)}, u32[]{:S(2)}) copy-start(bf16[16,24,128]{2,1,0:T(8,128)(2,1)S(1)} %all_to_all.40) | copy-start | bytes 294916
  225.8 7.1 %collective-permute-start.3 = (bf16[384,128]{1,0:T(8,128)(2,1)S(1)}, bf16[384,128]{1,0:T(8,128)(2,1)S(1)}, u32[]{:S(2)}, u32[]{:S(2)}) collective-permute-start(bf16[384,128]{1,0:T(8,128)(2,1)S(1)} %bitcast.14), channel_id=1, source_target_pairs={{0,16},{16,0},{1,17},{17,1},{2,18},{18,2},{3,19},{19,3},{4,20},{20... | collective-permute-start | bytes 294920 | tf_op jit(solution)/shard_map/ppermute | solution.py:169
  232.8 0.6 copy-start.4

commit v2 on v1

--- a/solution.py
+++ b/solution.py
@@ -15,6 +15,7 @@
 COL = ("xh", "y")
 ROW = ("xl", "z", "core")
 UNROLL = 4
+CHUNKS = 1
 VMEM = pl.BlockSpec(memory_space=pltpu.VMEM)
 SMEM = pl.BlockSpec(memory_space=pltpu.SMEM)
 ANY = pl.BlockSpec(memory_space=pl.ANY)
@@ -24,10 +25,25 @@
     return jax.ShapeDtypeStruct(dims, dtype)
 
 
-def first_kernel(state, inv_col, out):
-    scaled = jnp.transpose(state[...] * inv_col[...]).astype(BF16)
-    for q in range(out.shape[0]):
-        out[q] = scaled
+def chunk_of(width, h):
+    size = width // CHUNKS
+    return slice(h * size, (h + 1) * size)
+
+
+def first_kernel(state, degrees, *outs):
+    inverse = lax.rsqrt(degrees[...].astype(F32))
+    scaled = (jnp.transpose(state[...]) * inverse).astype(BF16)
+    for h, out in enumerate(outs):
+        piece = scaled[chunk_of(scaled.shape[0], h), :]
+        for q in range(out.shape[0]):
+            out[q] = piece
+
+
+def summed_up(parts):
+    total = parts[0].astype(F32)
+    for q in range(1, parts.shape[0]):
+        total += parts[q].astype(F32)
+    return total
 
 
 def live_count(live):
@@ -91,11 +107,11 @@
     out[...] = acc[0:count].astype(BF16)
 
 
-def state_kernel(parts, inv_row, inv_col, weight, features, input_map, cotangent, states, summed_t, out):
-    total = parts[0].astype(F32)
-    for q in range(1, parts.shape[0]):
-        total += parts[q].astype(F32)
-    total = total * inv_row[...]
+def state_kernel(*refs):
+    parts = refs[:CHUNKS]
+    inv_row, inv_col, weight, features, input_map, cotangent, states, summed_t = refs[CHUNKS : CHUNKS + 8]
+    outs = refs[CHUNKS + 8 :]
+    total = jnp.concatenate([summed_up(p) for p in parts], axis=0) * inv_row[...]
     summed_t[...] = total
     driving = jnp.dot(features[...], input_map[...], precision=HIGH, preferred_element_type=F32)
     moved = lax.dot_general(
@@ -105,14 +121,16 @@
     states[...] = state
     slopes = 1.0 - state * state
     scaled = (inv_col[...] * (slopes * cotangent[...])).astype(BF16)
-    for q in range(out.shape[0]):
-        out[q] = scaled
-
-
-def grad_kernel(core_ref, parts, inv_col, cotangent, weight, states, summed_t, features, adjoint, keep, send, *, factor):
-    total = parts[0].astype(F32)
-    for q in range(1, parts.shape[0]):
-        total += parts[q].astype(F32)
+    for h, out in enumerate(outs):
+        piece = scaled[:, chunk_of(scaled.shape[1], h)]
+        for q in range(out.shape[0]):
+            out[q] = piece
+
+
+def grad_kernel(core_ref, *refs, factor):
+    parts = refs[:CHUNKS]
+    inv_col, cotangent, weight, states, summed_t, features, adjoint, keep, send = refs[CHUNKS:]
+    total = jnp.concatenate([summed_up(p) for p in parts], axis=1)
     pulled = total * inv_col[...]
     moved = lax.dot_general(
         pulled, weight[...], (((1,), (1,)), ((), ())), precision=HIGH, preferred_element_type=F32
@@ -130,15 +148,12 @@
     half = weight_part.shape[1] // 2
     for at, part in ((0, weight_part), (width, input_part)):
         left, right = part[:, :half], part[:, half:]
-        keep[at : at + part.shape[0], :] = jnp.where(first, left, right)
-        send[at : at + part.shape[0], :] = jnp.where(first, right, left)
+        keep[at : at + part.shape[0], :] = jnp.where(first, left, right).astype(keep.dtype)
+        send[at : at + part.shape[0], :] = jnp.where(first, right, left).astype(send.dtype)
 
 
 def sum_kernel(parts, out):
-    total = parts[0].astype(F32)
-    for q in range(1, parts.shape[0]):
-        total += parts[q].astype(F32)
-    total = total.astype(out.dtype)
+    total = summed_up(parts).astype(out.dtype)
     for q in range(out.shape[0]):
         out[q] = total
 
@@ -154,7 +169,7 @@
         out[:, half:] = jnp.where(first, theirs, mine)
 
 
-def call(kernel, outs, specs, scratch=(), name=None):
+def call(kernel, outs, specs, scratch=(), name=None, mib=12, flops=10**8):
     return pl.pallas_call(
         kernel,
         out_shape=outs,
@@ -162,6 +177,8 @@
         out_specs=jax.tree.map(lambda _: VMEM, outs),
         scratch_shapes=list(scratch),
         name=name,
+        compiler_params=pltpu.CompilerParams(vmem_limit_bytes=mib * 2**20),
+        cost_estimate=pl.CostEstimate(flops=flops, bytes_accessed=2**21, transcendentals=0),
     )
 
 
@@ -195,51 +212,63 @@
     inverse = lax.rsqrt(degrees.astype(F32))
     inv_row, inv_col = inverse.reshape(1, nodes), inverse.reshape(nodes, 1)
     block = values.shape[1]
-
-    spread = call(
-        first_kernel, shape((col_devices, width, nodes), BF16), [VMEM] * 2, name="first"
-    )(starting_state, inv_col)
-    gathered = exchange(spread, COL)
-    keep, send = call(
+    size = width // CHUNKS
+    tile_flops = 2 * values.shape[0] * block * block * size
+
+    spreads = call(
+        first_kernel, (shape((col_devices, size, nodes), BF16),) * CHUNKS, [VMEM] * 2, name="first"
+    )(starting_state, degrees.reshape(1, nodes))
+    forward = call(
         forward_kernel,
-        (shape((chips, width, block), BF16),) * 2,
+        (shape((chips, size, block), BF16),) * 2,
         [SMEM] * 4 + [VMEM] * 2,
-        [pltpu.VMEM((2 * chips + 1, width, block), F32)],
+        [pltpu.VMEM((2 * chips + 1, size, block), F32)],
         name="forward",
-    )(rows, cols, live, core, values, gathered)
-    parts = exchange((keep.astype(F32) + swap(send).astype(F32)).astype(BF16), CHIP)
-    states, summed_t, spread = call(
+        mib=20,
+        flops=tile_flops,
+    )
+    gathered = [exchange(spread, COL) for spread in spreads]
+    parts = []
+    for x in gathered:
+        keep, send = forward(rows, cols, live, core, values, x)
+        parts.append(exchange((keep.astype(F32) + swap(send).astype(F32)).astype(BF16), CHIP))
+    states, summed_t, *spreads = call(
         state_kernel,
-        (shape((nodes, width), F32), shape((width, nodes), F32), shape((chips, nodes, width), BF16)),
-        [VMEM] * 7,
+        (shape((nodes, width), F32), shape((width, nodes), F32))
+        + (shape((chips, nodes, size), BF16),) * CHUNKS,
+        [VMEM] * (CHUNKS + 6),
         name="state",
-    )(parts, inv_row, inv_col, weight, features, input_map, cotangent)
-    own = exchange(spread, CHIP)
-    other = swap(own)
-    partial = call(
+    )(*parts, inv_row, inv_col, weight, features, input_map, cotangent)
+    adjoint_sum = call(
         adjoint_kernel,
-        shape((col_devices, block, width), BF16),
+        shape((col_devices, block, size), BF16),
         [SMEM] * 4 + [VMEM] + [ANY] * 2,
         [
-            pltpu.VMEM((2 * chips, block, width), BF16),
-            pltpu.VMEM((col_devices + 1, block, width), F32),
+            pltpu.VMEM((2 * chips, block, size), BF16),
+            pltpu.VMEM((col_devices + 1, block, size), F32),
             pltpu.SemaphoreType.DMA((2,)),
         ],
         name="adjoint",
-    )(rows, cols, live, core, values, own, other)
-    parts = exchange(partial, COL)
+        mib=20,
+        flops=tile_flops,
+    )
+    gathered = [exchange(spread, CHIP) for spread in spreads]
+    parts = []
+    for own in gathered:
+        partial = adjoint_sum(rows, cols, live, core, values, own, swap(own))
+        parts.append(exchange(partial, COL))
     factor = 1.0 / math.sqrt(nodes * 2 * chips * col_devices)
     total = width + inputs
     adjoint, keep, send = call(
         functools.partial(grad_kernel, factor=factor),
-        (shape((nodes, width), F32), shape((total, width // 2), F32), shape((total, width // 2), F32)),
-        [SMEM] + [VMEM] * 7,
+        (shape((nodes, width), F32),) + (shape((total, width // 2), BF16),) * 2,
+        [SMEM] + [VMEM] * (CHUNKS + 6),
         name="grad",
-    )(core, parts, inv_col, cotangent, weight, states, summed_t, features)
+    )(core, *parts, inv_col, cotangent, weight, states, summed_t, features)
     piece = (total // chips, width // 2)
-    halves = (keep + swap(send)).reshape(chips, *piece)
+    halves = (keep.astype(F32) + swap(send).astype(F32)).astype(BF16).reshape(chips, *piece)
     parts = exchange(halves, CHIP)
-    spread = call(sum_kernel, shape((col_devices, *piece), F32), [VMEM], name="sum_chip")(parts)
+    spread = call(sum_kernel, shape((col_devices, *piece), BF16), [VMEM], name="sum_chip")(parts)
     parts = exchange(spread, COL)
     spread = call(sum_kernel, shape((chips, *piece), BF16), [VMEM], name="sum_col")(parts)
     own = exchange(spread, CHIP).reshape(total, width // 2)

time: 237 us -> 216 us (0.911)
  blocking collectives: 139 us -> 97.4 us
  waiting for transfers between devices: 34 us -> 57.7 us
  Pallas kernels: 25 us -> 11.4 us
  starting transfers between devices: 29.7 us -> 41.7 us
    all_to_all x6 -> x5, blocking collectives: 139 us -> 97.4 us  [exchange(): return lax.all_to_all(x, axes, 0, 0, tiled=True)]
    all_to_all x1 -> x2, waiting for transfers between devices: 27 us -> 51.3 us  [exchange(): return lax.all_to_all(x, axes, 0, 0, tiled=True)]
    all_to_all x1 -> x2, starting transfers between devices: 10.2 us -> 21.7 us  [exchange(): return lax.all_to_all(x, axes, 0, 0, tiled=True)]
    pallas_call x4, Pallas kernels: 15.1 us -> 8.01 us  [the longest x1 3.42 us: on_device(): keep, send = forward(rows, cols, live, core, values, x)]
  transfers between devices with their start and end apart: 5 -> 6, of which waited for: 5 -> 6; matrix products, arithmetic and copies ran while one was open for 0% -> 1% of each run, Pallas kernels for 0% -> 0%
where the time goes in v2:
time: 216 us; the launch traced here: 215 us
  blocking collectives  97.4 us (45%)
  waiting for transfers between devices  57.7 us (27%)
  starting transfers between devices  41.7 us (19%)
  Pallas kernels  11.4 us (5%)
  local copies, waits for them, and re-layouts  4.31 us (2%)
    all_to_all x5, blocking collectives, exchange(): return lax.all_to_all(x, axes, 0, 0, tiled=True)  97.4 us
    all_to_all x2, waiting for transfers between devices, exchange(): return lax.all_to_all(x, axes, 0, 0, tiled=True)  51.3 us
    all_to_all x2, starting transfers between devices, exchange(): return lax.all_to_all(x, axes, 0, 0, tiled=True)  21.7 us
    ppermute x4, starting transfers between devices, swap(): return lax.ppermute(x, 'core', [(0, 1), (1, 0)])  20 us
    ppermute x4, waiting for transfers between devices, swap(): return lax.ppermute(x, 'core', [(0, 1), (1, 0)])  6.37 us
  transfers between devices with their start and end apart: 6, of which 6 were waited for; matrix products, arithmetic and copies ran while one was open for 1% of the time, Pallas kernels for 0%

profile of v2, /device:TPU:1, one launch (start us, length us, event | category | flops | bytes accessed | tf_op | source)
XLA Modules:
  0.0 215.1 jit_solution(7835233178357308594)
XLA Ops:
  0.7 1.0 copy-done.5
  2.4 1.2 first.1
  3.6 10.2 %all-to-all-start = ((bf16[16,256,128]{2,1,0:T(8,128)(2,1)}), bf16[16,256,128]{2,1,0:T(8,128)(2,1)S(1)}, u32[]{:S(2)}, u32[]{:S(2)}) async-start(bf16[16,256,128]{2,1,0:T(8,128)(2,1)} %first.1), calls=%async_computation | async-start | bytes 2097152 | tf_op jit(solution)/shard_map/all_to_all | solution.py:190
  13.8 27.0 %all-to-all-done.blocks = bf16[16,256,128]{2,1,0:T(8,128)(2,1)S(1)} async-done(((bf16[16,256,128]{2,1,0:T(8,128)(2,1)}), bf16[16,256,128]{2,1,0:T(8,128)(2,1)S(1)}, u32[]{:S(2)}, u32[]{:S(2)}) %all-to-all-start) | async-done | bytes 1048608 | tf_op jit(solution)/shard_map/all_to_all | solution.py:190
  40.8 3.4 %forward.1 = (bf16[16,256,128]{2,1,0:T(8,128)(2,1)S(1)}, bf16[16,256,128]{2,1,0:T(8,128)(2,1)S(1)}) custom-call(s32[64]{0:T(128)S(1)} %bitcast.16, s32[64]{0:T(128)S(1)} %bitcast.18, s32[64]{0:T(128)S(1)} %bitcast.20, s32[1]{0:T(128)} %bitcast.3.core_ref, bf16[64,128,128]{2,1,0:T(8,128)(2,1)S(1)} %bitcast.12, bf16[16,256,128]{2,1,0:T(8,128)(2,1)S(1)} %all-to-all-done.blocks), custom_call_target="tpu_custom_call" | custom-call | flops 536870912 | bytes 2097152 | tf_op jit(solution)/shard_map/forward/pallas_call | solution.py:233
  44.3 4.0 %collective-permute-start = (bf16[16,256,128]{2,1,0:T(8,128)(2,1)S(1)}, bf16[16,256,128]{2,1,0:T(8,128)(2,1)S(1)}, u32[]{:S(2)}, u32[]{:S(2)}) collective-permute-start(bf16[16,256,128]{2,1,0:T(8,128)(2,1)S(1)} %get-tuple-element.15), channel_id=1, source_target_pairs={{0,16},{16,0},{1,17},{17,1},{2,18},{18,2},{3,19},{19,3},{4,20},{20... | collective-permute-start | bytes 3145736 | tf_op jit(solution)/shard_map/ppermute | solution.py:186
  48.3 2.3 %collective-permute-done = bf16[16,256,128]{2,1,0:T(8,128)(2,1)S(1)} collective-permute-done((bf16[16,256,128]{2,1,0:T(8,128)(2,1)S(1)}, bf16[16,256,128]{2,1,0:T(8,128)(2,1)S(1)}, u32[]{:S(2)}, u32[]{:S(2)}) %collective-permute-start) | collective-permute-done | bytes 1048608 | tf_op jit(solution)/shard_map/ppermute | solution.py:186
  50.5 1.3 add_convert_fusion
  51.8 11.5 %all-to-all-start.1 = ((bf16[16,256,128]{2,1,0:T(8,128)(2,1)}), bf16[16,256,128]{2,1,0:T(8,128)(2,1)S(1)}, u32[]{:S(2)}, u32[]{:S(2)}) async-start(bf16[16,256,128]{2,1,0:T(8,128)(2,1)} %add_convert_fusion), calls=%async_computation.1 | async-start | bytes 2097152 | tf_op jit(solution)/shard_map/all_to_all | solution.py:190
  64.6 24.3 %all-to-all-done.1.refs_0_ = bf16[16,256,128]{2,1,0:T(8,128)(2,1)S(1)} async-done(((bf16[16,256,128]{2,1,0:T(8,128)(2,1)}), bf16[16,256,128]{2,1,0:T(8,128)(2,1)S(1)}, u32[]{:S(2)}, u32[]{:S(2)}) %all-to-all-start.1) | async-done | bytes 1048608 | tf_op jit(solution)/shard_map/all_to_all | solution.py:190
  90.7 1.3 state.3
  92.0 30.7 %all_to_all.35.own = bf16[16,128,256]{2,1,0:T(8,128)(2,1)S(1)} all-to-all(bf16[16,128,256]{2,1,0:T(8,128)(2,1)S(1)} %get-tuple-element.17), channel_id=1, replica_groups=mesh['xl'=2,'z'=8,'core'=2,'xh'=2,'y'=8] {'xl','z'}, dimensions={0} | all-to-all | bytes 2097152 | tf_op jit(solution)/shard_map/all_to_all | solution.py:190
  122.7 4.7 %collective-permute-start.1 = (bf16[16,128,256]{2,1,0:T(8,128)(2,1)S(1)}, bf16[16,128,256]{2,1,0:T(8,128)(2,1)S(1)}, u32[]{:S(2)}, u32[]{:S(2)}) collective-permute-start(bf16[16,128,256]{2,1,0:T(8,128)(2,1)S(1)} %all_to_all.35.own), channel_id=1, source_target_pairs={{0,16},{16,0},{1,17},{17,1},{2,18},{18,2},{3,19},{19,3},{4,20},{20... | collective-permute-start | bytes 3145736 | tf_op jit(solution)/shard_map/ppermute | solution.py:186
  127.4 2.3 %collective-permute-done.1.other = bf16[16,128,256]{2,1,0:T(8,128)(2,1)S(1)} collective-permute-done((bf16[16,128,256]{2,1,0:T(8,128)(2,1)S(1)}, bf16[16,128,256]{2,1,0:T(8,128)(2,1)S(1)}, u32[]{:S(2)}, u32[]{:S(2)}) %collective-permute-start.1) | collective-permute-done | bytes 1048608 | tf_op jit(solution)/shard_map/ppermute | solution.py:186
  129.7 3.4 %adjoint.1 = bf16[16,128,256]{2,1,0:T(8,128)(2,1)S(1)} custom-call(s32[64]{0:T(128)S(1)} %bitcast.17, s32[64]{0:T(128)S(1)} %bitcast.19, s32[64]{0:T(128)S(1)} %bitcast.21, s32[1]{0:T(128)} %bitcast.3.core_ref, bf16[64,128,128]{2,1,0:T(8,128)(2,1)S(1)} %bitcast.13, bf16[16,128,256]{2,1,0:T(8,128)(2,1)S(1)} %all_to_all.35.own, ...), custom_call_target="tpu_custom_call" | custom-call | flops 536870912 | bytes 2097152 | tf_op jit(solution)/shard_map/adjoint/pallas_call | solution.py:258
  133.1 30.8 %all_to_all.36.refs_0_ = bf16[16,128,256]{2,1,0:T(8,128)(2,1)S(1)} all-to-all(bf16[16,128,256]{2,1,0:T(8,128)(2,1)S(1)} %adjoint.1), channel_id=1, replica_groups=mesh['xl'=2,'z'=8,'core'=2,'xh'=2,'y'=8] {'xh','y'}, dimensions={0} | all-to-all | bytes 2097152 | tf_op jit(solution)/shard_map/all_to_all | solution.py:190
  163.9 1.3 grad.1
  165.2 5.0 %collective-permute-start.2 = (bf16[384,128]{1,0:T(8,128)(2,1)S(1)}, bf16[384,128]{1,0:T(8,128)(2,1)S(1)}, u32[]{:S(2)}, u32[]{:S(2)}) collective-permute-start(bf16[384,128]{1,0:T(8,128)(2,1)S(1)} %get-tuple-element.21), channel_id=1, source_target_pairs={{0,16},{16,0},{1,17},{17,1},{2,18},{18,2},{3,19},{19,3},{4,20},{20... | collective-permute-start | bytes 294920 | tf_op jit(solution)/shard_map/ppermute | solution.py:186
  170.3 0.9 collective-permute-done.2
  171.2 11.9 %all_to_all.37.parts = bf16[16,24,128]{2,1,0:T(8,128)(2,1)S(1)} all-to-all(bf16[16,24,128]{2,1,0:T(8,128)(2,1)S(1)} %bitcast.23), channel_id=1, replica_groups=mesh['xl'=2,'z'=8,'core'=2,'xh'=2,'y'=8] {'xl','z'}, dimensions={0} | all-to-all | bytes 196608 | tf_op jit(solution)/shard_map/all_to_all | solution.py:190
  183.1 14.1 %all_to_all.38.parts = bf16[16,24,128]{2,1,0:T(8,128)(2,1)S(1)} all-to-all(bf16[16,24,128]{2,1,0:T(8,128)(2,1)S(1)} %sum_chip.1), channel_id=1, replica_groups=mesh['xl'=2,'z'=8,'core'=2,'xh'=2,'y'=8] {'xh','y'}, dimensions={0} | all-to-all | bytes 196608 | tf_op jit(solution)/shard_map/all_to_all | solution.py:190
  197.2 10.0 %all_to_all.39 = bf16[16,24,128]{2,1,0:T(8,128)(2,1)S(1)} all-to-all(bf16[16,24,128]{2,1,0:T(8,128)(2,1)S(1)} %sum_col.1), channel_id=1, replica_groups=mesh['xl'=2,'z'=8,'core'=2,'xh'=2,'y'=8] {'xl','z'}, dimensions={0} | all-to-all | bytes 196608 | tf_op jit(solution)/shard_map/all_to_all | solution.py:190
  207.2 6.2 %collective-permute-start.3 = (bf16[384,128]{1,0:T(8,128)(2,1)S(1)}, bf16[384,128]{1,0:T(8,128)(2,1)S(1)}, u32[]{:S(2)}, u32[]{:S(2)}) collective-permute-start(bf16[384,128]{1,0:T(8,128)(2,1)S(1)} %bitcast.14), channel_id=1, source_target_pairs={{0,16},{16,0},{1,17},{17,1},{2,18},{18,2},{3,19},{19,3},{4,20},{20... | collective-permute-start | bytes 294920 | tf_op jit(solution)/shard_map/ppermute | solution.py:186
  213.5 0.9 collective-permute-done.3.other
  (31 shorter events, 4.6 us)
Async XLA Ops:
  0.6 40.2 %copy-start = (bf16[1,1,64,128,128]{4,3,2,1,0:T(8,128)(2,1)S(1)}, bf16[1,1,64,128,128]{4,3,2,1,0:T(8,128)(2,1)}, u32[]{:S(2)}) copy-start(bf16[1,1,64,128,128]{4,3,2,1,0:T(8,128)(2,1)} %param.14) | copy-start | bytes 6291460
  0.6 1.1 copy-start.5
  1.7 0.7 copy-start.11
  2.4 38.5 %copy-start.8 = (s32[1,1,64]{2,1,0:T(1,128)S(1)}, s32[1,1,64]{2,1,0:T(1,128)}, u32[]{:S(2)}) copy-start(s32[1,1,64]{2,1,0:T(1,128)} %param.15) | copy-start | bytes 772
  2.4 38.5 %copy-start.9 = (s32[1,1,64]{2,1,0:T(1,128)S(1)}, s32[1,1,64]{2,1,0:T(1,128)}, u32[]{:S(2)}) copy-start(s32[1,1,64]{2,1,0:T(1,128)} %param.16) | copy-start | bytes 772
  2.4 38.5 %copy-start.10 = (s32[1,1,64]{2,1,0:T(1,128)S(1)}, s32[1,1,64]{2,1,0:T(1,128)}, u32[]{:S(2)}) copy-start(s32[1,1,64]{2,1,0:T(1,128)} %param.17) | copy-start | bytes 772
  3.6 37.3 %all-to-all-start = ((bf16[16,256,128]{2,1,0:T(8,128)(2,1)}), bf16[16,256,128]{2,1,0:T(8,128)(2,1)S(1)}, u32[]{:S(2)}, u32[]{:S(2)}) async-start(bf16[16,256,128]{2,1,0:T(8,128)(2,1)} %first.1), calls=%async_computation | async-start | bytes 2097152 | tf_op jit(solution)/shard_map/all_to_all | solution.py:190
  44.3 6.3 %collective-permute-start = (bf16[16,256,128]{2,1,0:T(8,128)(2,1)S(1)}, bf16[16,256,128]{2,1,0:T(8,128)(2,1)S(1)}, u32[]{:S(2)}, u32[]{:S(2)}) collective-permute-start(bf16[16,256,128]{2,1,0:T(8,128)(2,1)S(1)} %get-tuple-element.15), channel_id=1, source_target_pairs={{0,16},{16,0},{1,17},{17,1},{2,18},{18,2},{3,19},{19,3},{4,20},{20... | collective-permute-start | bytes 3145736 | tf_op jit(solution)/shard_map/ppermute | solution.py:186
  50.5 12.8 %copy-start.12 = (s32[128]{0:T(128)S(1)}, s32[128]{0:T(128)}, u32[]{:S(2)}) copy-start(s32[128]{0:T(128)} %param.13) | copy-start | bytes 1540
  50.5 38.4 %copy-start.1 = (f32[256,256]{1,0:T(8,128)S(1)}, f32[256,256]{1,0:T(8,128)}, u32[]{:S(2)}) copy-start(f32[256,256]{1,0:T(8,128)} %refs_3_.3) | copy-start | bytes 786436
  50.5 38.4 %copy-start.4 = (f32[128,128]{1,0:T(8,128)S(1)}, f32[128,128]{1,0:T(8,128)}, u32[]{:S(2)}) copy-start(f32[128,128]{1,0:T(8,128)} %refs_6_.3) | copy-start | bytes 196612
  51.8 37.1 %all-to-all-start.1 = ((bf16[16,256,128]{2,1,0:T(8,128)(2,1)}), bf16[16,256,128]{2,1,0:T(8,128)(2,1)S(1)}, u32[]{:S(2)}, u32[]{:S(2)}) async-start(bf16[16,256,128]{2,1,0:T(8,128)(2,1)} %add_convert_fusion), calls=%async_computation.1 | async-start | bytes 2097152 | tf_op jit(solution)/shard_map/all_to_all | solution.py:190
  88.9 0.9 copy-start.2
  89.8 0.9 copy-start.6
  122.7 7.0 %collective-permute-start.1 = (bf16[16,128,256]{2,1,0:T(8,128)(2,1)S(1)}, bf16[16,128,256]{2,1,0:T(8,128)(2,1)S(1)}, u32[]{:S(2)}, u32[]{:S(2)}) collective-permute-start(bf16[16,128,256]{2,1,0:T(8,128)(2,1)S(1)} %all_to_all.35.own), channel_id=1, source_target_pairs={{0,16},{16,0},{1,17},{17,1},{2,18},{18,2},{3,19},{19,3},{4,20},{20... | collective-permute-start | bytes 3145736 | tf_op jit(solution)/shard_map/ppermute | solution.py:186
  133.1 30.8 %copy-start.3 = (f32[128,256]{1,0:T(8,128)S(1)}, f32[128,256]{1,0:T(8,128)}, u32[]{:S(2)}) copy-start(f32[128,256]{1,0:T(8,128)} %refs_2_.1) | copy-start | bytes 393220
  133.1 30.8 %copy-start.7 = (f32[128,256]{1,0:T(8,128)S(1)}, f32[128,256]{1,0:T(8,128)}, u32[]{:S(2)}) copy-start(f32[128,256]{1,0:T(8,128)} %get-tuple-element.10.refs_4_) | copy-start | bytes 393220
  165.2 6.0 %collective-permute-start.2 = (bf16[384,128]{1,0:T(8,128)(2,1)S(1)}, bf16[384,128]{1,0:T(8,128)(2,1)S(1)}, u32[]{:S(2)}, u32[]{:S(2)}) collective-permute-start(bf16[384,128]{1,0:T(8,128)(2,1)S(1)} %get-tuple-element.21), channel_id=1, source_target_pairs={{0,16},{16,0},{1,17},{17,1},{2,18},{18,2},{3,19},{19,3},{4,20},{20... | collective-permute-start | bytes 294920 | tf_op jit(solution)/shard_map/ppermute | solution.py:186
  207.2 7.2 %collective-permute-start.3 = (bf16[384,128]{1,0:T(8,128)(2,1)S(1)}, bf16[384,128]{1,0:T(8,128)(2,1)S(1)}, u32[]{:S(2)}, u32[]{:S(2)}) collective-permute-start(bf16[384,128]{1,0:T(8,128)(2,1)S(1)} %bitcast.14), channel_id=1, source_target_pairs={{0,16},{16,0},{1,17},{17,1},{2,18},{18,2},{3,19},{19,3},{4,20},{20... | collective-permute-start | bytes 294920 | tf_op jit(solution)/shard_map/ppermute | solution.py:186

commit v3 on v1

v3 whole, which is shorter than its diff:
```python
import functools
import math

import jax
import jax.numpy as jnp
from jax import lax
from jax.experimental import pallas as pl
from jax.experimental.pallas import tpu as pltpu
from jax.sharding import Mesh, PartitionSpec as P

HIGH = lax.Precision.HIGHEST
BF16 = jnp.bfloat16
F32 = jnp.float32
CHIP = ("xl", "z")
COL = ("xh", "y")
ROW = ("xl", "z", "core")
UNROLL = 4
FIRST_MIB = 56
VMEM = pl.BlockSpec(memory_space=pltpu.VMEM)
SMEM = pl.BlockSpec(memory_space=pltpu.SMEM)


def shape(dims, dtype):
    return jax.ShapeDtypeStruct(dims, dtype)


def summed_up(parts):
    total = parts[0].astype(F32)
    for q in range(1, parts.shape[0]):
        total += parts[q].astype(F32)
    return total


def first_kernel(state, degrees, out):
    inverse = lax.rsqrt(degrees[...].astype(F32))
    scaled = (jnp.transpose(state[...]) * inverse).astype(BF16)
    for q in range(out.shape[0]):
        out[q] = scaled


def prep_kernel(
    rows, cols, live, core_ref, degrees, features, input_map, cotangent,
    tiles, rows_of, cols_of, counts, inv_row, inv_wide, driving, features_t, cotangent_scaled,
):
    core = core_ref[0]
    slots = live.shape[0]

    def clear(t, carry):
        for side in range(2):
            tiles[side, t] = 0
            rows_of[side, t] = 0
            cols_of[side, t] = 0
        return carry

    lax.fori_loop(0, tiles.shape[1], clear, 0)

    def sort(t, ends):
        side = (cols[t] & 1) ^ core
        at = jnp.where(side == 0, ends[0], ends[1])
        use = live[t] == 1

        @pl.when(use)
        def _():
            tiles[side, at] = t
            rows_of[side, at] = rows[t]
            cols_of[side, at] = cols[t] >> 1

        one = use.astype(jnp.int32)
        return ends[0] + jnp.where(side == 0, one, 0), ends[1] + jnp.where(side == 1, one, 0)

    own, other = lax.fori_loop(0, slots, sort, (jnp.int32(0), jnp.int32(0)))
    counts[0] = own
    counts[1] = other
    inverse = lax.rsqrt(degrees[...].astype(F32))
    inv_row[...] = inverse
    wide = jnp.transpose(jnp.broadcast_to(inverse, inv_wide.shape))
    inv_wide[...] = wide
    features_t[...] = jnp.transpose(features[...])
    driving[...] = jnp.dot(
        features[...], input_map[...], precision=HIGH, preferred_element_type=F32
    )
    cotangent_scaled[...] = cotangent[...] * wide[:, :1]


def add_tiles(side, counts, tiles, slots_of, blocks_of, product_of, acc):
    count = counts[side]
    spare = acc.shape[0] - 1

    def group(g, carry):
        products, slots = [], []
        for u in range(UNROLL):
            t = g * UNROLL + u
            slots.append(jnp.where(t < count, slots_of[side, t], spare))
            products.append(product_of(tiles[side, t], blocks_of[side, t]))
        for slot, product in zip(slots, products):
            acc[slot] += product
        return carry

    lax.fori_loop(0, (count + UNROLL - 1) // UNROLL, group, 0)


def forward_kernel(counts, tiles, rows_of, cols_of, values, blocks, out, acc, *, side):
    acc[...] = jnp.zeros_like(acc)

    def product_of(tile, block):
        return jnp.dot(blocks[block], values[tile], preferred_element_type=F32)

    add_tiles(side, counts, tiles, cols_of, rows_of, product_of, acc)
    out[...] = acc[0 : out.shape[0]].astype(BF16)


def adjoint_own_kernel(counts, tiles, rows_of, cols_of, values, blocks, acc):
    acc[...] = jnp.zeros_like(acc)

    def product_of(tile, block):
        return jnp.dot(values[tile], blocks[block], preferred_element_type=F32)

    add_tiles(0, counts, tiles, rows_of, cols_of, product_of, acc)


def adjoint_other_kernel(counts, tiles, rows_of, cols_of, values, blocks, start, out, acc):
    acc[...] = start[...]

    def product_of(tile, block):
        return jnp.dot(values[tile], blocks[block], preferred_element_type=F32)

    add_tiles(1, counts, tiles, rows_of, cols_of, product_of, acc)
    out[...] = acc[0 : out.shape[0]].astype(BF16)


def state_kernel(parts, inv_row, weight, driving, cotangent_scaled, states, summed_t, out):
    total = summed_up(parts) * inv_row[...]
    summed_t[...] = total
    moved = jnp.dot(jnp.transpose(total), weight[...], precision=HIGH, preferred_element_type=F32)
    state = jnp.tanh(moved + driving[...])
    states[...] = state
    slopes = 1.0 - state * state
    scaled = (slopes * cotangent_scaled[...]).astype(BF16)
    for q in range(out.shape[0]):
        out[q] = scaled


def grad_kernel(
    core_ref, parts, inv_wide, cotangent, weight, states, summed_t, features_t, adjoint, keep, send, *, factor
):
    pulled = summed_up(parts) * inv_wide[:, :1]
    moved = lax.dot_general(
        pulled, weight[...], (((1,), (1,)), ((), ())), precision=HIGH, preferred_element_type=F32
    )
    result = cotangent[...] + moved
    adjoint[...] = result
    state = states[...]
    masked = (1.0 - state * state) * result * factor
    weight_part = jnp.dot(summed_t[...], masked, precision=HIGH, preferred_element_type=F32)
    input_part = jnp.dot(features_t[...], masked, precision=HIGH, preferred_element_type=F32)
    first = core_ref[0] == 0
    width = weight_part.shape[0]
    half = weight_part.shape[1] // 2
    for at, part in ((0, weight_part), (width, input_part)):
        left, right = part[:, :half], part[:, half:]
        keep[at : at + part.shape[0], :] = jnp.where(first, left, right).astype(keep.dtype)
        send[at : at + part.shape[0], :] = jnp.where(first, right, left).astype(send.dtype)


def sum_kernel(parts, out):
    total = summed_up(parts).astype(out.dtype)
    for q in range(out.shape[0]):
        out[q] = total


def last_kernel(core_ref, own, other, weight_grad, input_grad):
    first = core_ref[0] == 0
    width = weight_grad.shape[0]
    half = own.shape[1]
    for at, out in ((0, weight_grad), (width, input_grad)):
        mine = own[at : at + out.shape[0], :].astype(F32)
        theirs = other[at : at + out.shape[0], :].astype(F32)
        out[:, :half] = jnp.where(first, mine, theirs)
        out[:, half:] = jnp.where(first, theirs, mine)


def call(kernel, outs, specs, scratch=(), name=None, mib=12, flops=10**8, out_specs=None):
    return pl.pallas_call(
        kernel,
        out_shape=outs,
        in_specs=specs,
        out_specs=jax.tree.map(lambda _: VMEM, outs) if out_specs is None else out_specs,
        scratch_shapes=list(scratch),
        name=name,
        compiler_params=pltpu.CompilerParams(vmem_limit_bytes=mib * 2**20),
        cost_estimate=pl.CostEstimate(flops=flops, bytes_accessed=2**21, transcendentals=0),
    )


def swap(x):
    return lax.ppermute(x, "core", [(0, 1), (1, 0)])


def exchange(x, axes):
    return lax.all_to_all(x, axes, 0, 0, tiled=True)


def on_device(
    starting_state,
    features,
    cotangent,
    degrees,
    tile_values,
    tile_rows,
    tile_cols,
    tile_live,
    weight,
    input_map,
):
    values = tile_values[0, 0]
    rows, cols, live = tile_rows[0, 0], tile_cols[0, 0], tile_live[0, 0]
    nodes, width = starting_state.shape
    inputs = features.shape[1]
    chips = lax.axis_size("xl") * lax.axis_size("z")
    col_devices = lax.axis_size("xh") * lax.axis_size("y")
    core = lax.axis_index("core").astype(jnp.int32).reshape(1)
    degree_row = degrees.reshape(1, nodes)
    block = values.shape[1]
    room = values.shape[0] + UNROLL
    tile_flops = values.shape[0] * block * block * width

    spread = call(
        first_kernel, shape((col_devices, width, nodes), BF16), [VMEM] * 2, name="first", mib=FIRST_MIB
    )(starting_state, degree_row)
    gathered = exchange(spread, COL)
    lists = (shape((2, room), jnp.int32),) * 3 + (shape((2,), jnp.int32),)
    tiles, rows_of, cols_of, counts, inv_row, inv_wide, driving, features_t, cotangent_scaled = call(
        prep_kernel,
        lists
        + (
            shape((1, nodes), F32),
            shape((nodes, nodes), F32),
            shape((nodes, width), F32),
            shape((inputs, nodes), F32),
            shape((nodes, width), F32),
        ),
        [SMEM] * 4 + [VMEM] * 4,
        name="prep",
        out_specs=(SMEM,) * 4 + (VMEM,) * 5,
    )(rows, cols, live, core, degree_row, features, input_map, cotangent)
    order = (counts, tiles, rows_of, cols_of, values)

    def forward(side):
        return call(
            functools.partial(forward_kernel, side=side),
            shape((chips, width, block), BF16),
            [SMEM] * 4 + [VMEM] * 2,
            [pltpu.VMEM((chips + 1, width, block), F32)],
            name=f"forward{side}",
            flops=tile_flops,
        )(*order, gathered)

    received = swap(forward(1))
    parts = exchange((forward(0).astype(F32) + received.astype(F32)).astype(BF16), CHIP)
    states, summed_t, spread = call(
        state_kernel,
        (shape((nodes, width), F32), shape((width, nodes), F32), shape((chips, nodes, width), BF16)),
        [VMEM] * 5,
        name="state",
    )(parts, inv_row, weight, driving, cotangent_scaled)
    own = exchange(spread, CHIP)
    other = swap(own)
    total = (col_devices + 1, block, width)
    part_sum = call(
        adjoint_own_kernel,
        shape(total, F32),
        [SMEM] * 4 + [VMEM] * 2,
        name="adjoint0",
        flops=tile_flops,
    )(*order, own)
    partial = call(
        adjoint_other_kernel,
        shape((col_devices, block, width), BF16),
        [SMEM] * 4 + [VMEM] * 3,
        [pltpu.VMEM(total, F32)],
        name="adjoint1",
        flops=tile_flops,
    )(*order, other, part_sum)
    parts = exchange(partial, COL)
    factor = 1.0 / math.sqrt(nodes * 2 * chips * col_devices)
    total = width + inputs
    adjoint, keep, send = call(
        functools.partial(grad_kernel, factor=factor),
        (shape((nodes, width), F32),) + (shape((total, width // 2), BF16),) * 2,
        [SMEM] + [VMEM] * 7,
        name="grad",
    )(core, parts, inv_wide, cotangent, weight, states, summed_t, features_t)
    piece = (total // chips, width // 2)
    halves = (keep.astype(F32) + swap(send).astype(F32)).astype(BF16).reshape(chips, *piece)
    parts = exchange(halves, CHIP)
    spread = call(sum_kernel, shape((col_devices, *piece), BF16), [VMEM], name="sum_chip")(parts)
    parts = exchange(spread, COL)
    spread = call(sum_kernel, shape((chips, *piece), BF16), [VMEM], name="sum_col")(parts)
    own = exchange(spread, CHIP).reshape(total, width // 2)
    other = swap(own)
    weight_grad, input_grad = call(
        last_kernel,
        (shape((width, width), F32), shape((inputs, width), F32)),
        [SMEM] + [VMEM] * 2,
        name="last",
    )(core, own, other)
    return states, adjoint, weight_grad, input_grad


def solution(mesh):
    sizes = mesh.devices.shape
    fine = Mesh(
        mesh.devices.reshape(2, sizes[0] // 4, 2, 2, sizes[1] // 2),
        ("xl", "z", "core", "xh", "y"),
    )
    every = ROW + COL
    return jax.shard_map(
        on_device,
        mesh=fine,
        in_specs=(
            P(every, None),
            P(every, None),
            P(every, None),
            P(every),
            P(ROW, COL, None, None, None),
            P(ROW, COL, None),
            P(ROW, COL, None),
            P(ROW, COL, None),
            P(),
            P(),
        ),
        out_specs=(P(every, None), P(every, None), P(), P()),
        check_vma=False,
    )
```

time: 237 us -> 208 us (0.88)
  waiting for transfers between devices: 34 us -> 19.9 us
  Pallas kernels: 25 us -> 17.8 us
  blocking collectives: 139 us -> 133 us
  other arithmetic: 3.63 us -> 0.31 us
  local copies, waits for them, and re-layouts: 3.33 us -> 6.16 us
    all_to_all x1, waiting for transfers between devices: 27 us -> 17.8 us  [exchange(): return lax.all_to_all(x, axes, 0, 0, tiled=True)]
    all_to_all x6, blocking collectives: 139 us -> 133 us  [exchange(): return lax.all_to_all(x, axes, 0, 0, tiled=True)]
    ppermute x4, waiting for transfers between devices: 6.92 us -> 2.04 us  [swap(): return lax.ppermute(x, 'core', [(0, 1), (1, 0)])]
    unnamed x10 -> x32, local copies, waits for them, and re-layouts: 2.6 us -> 6.16 us
    pallas_call x3 -> x6, Pallas kernels: 13 us -> 12.3 us  [the longest x2 4.64 us: forward(): call(functools.partial(forward_kernel, side=side), shape((chips, width, b...]
  transfers between devices with their start and end apart: 5 -> 5, of which waited for: 5 -> 4; matrix products, arithmetic and copies ran while one was open for 0% -> 0% of each run, Pallas kernels for 0% -> 4%
where the time goes in v3:
time: 208 us; the launch traced here: 207 us
  blocking collectives  133 us (64%)
  starting transfers between devices  29 us (14%)
  waiting for transfers between devices  19.9 us (10%)
  Pallas kernels  17.8 us (9%)
  local copies, waits for them, and re-layouts  6.16 us (3%)
    all_to_all x6, blocking collectives, exchange(): return lax.all_to_all(x, axes, 0, 0, tiled=True)  133 us
    ppermute x4, starting transfers between devices, swap(): return lax.ppermute(x, 'core', [(0, 1), (1, 0)])  18.8 us
    all_to_all x1, waiting for transfers between devices, exchange(): return lax.all_to_all(x, axes, 0, 0, tiled=True)  17.8 us
    all_to_all x1, starting transfers between devices, exchange(): return lax.all_to_all(x, axes, 0, 0, tiled=True)  10.2 us
    unnamed x32, local copies, waits for them, and re-layouts  6.16 us
    pallas_call x2, Pallas kernels, forward(): call(functools.partial(forward_kernel, side=side), shape((chips, width, b...  4.64 us
  transfers between devices with their start and end apart: 5, of which 4 were waited for; matrix products, arithmetic and copies ran while one was open for 0% of the time, Pallas kernels for 4%

profile of v3, /device:TPU:1, one launch (start us, length us, event | category | flops | bytes accessed | tf_op | source)
XLA Modules:
  0.0 207.0 jit_solution(9061762428993891355)
XLA Ops:
  0.7 2.3 %first.1 = bf16[16,256,128]{2,1,0:T(8,128)(2,1)} custom-call(f32[128,256]{1,0:T(8,128)} %state.2, s32[1,128]{1,0:T(1,128)} %bitcast.14), custom_call_target="tpu_custom_call" | custom-call | flops 100000000 | bytes 2097152 | tf_op jit(solution)/shard_map/first/pallas_call | solution.py:227
  2.9 10.2 %all-to-all-start = ((bf16[16,256,128]{2,1,0:T(8,128)(2,1)}), bf16[16,256,128]{2,1,0:T(8,128)(2,1)S(1)}, u32[]{:S(2)}, u32[]{:S(2)}) async-start(bf16[16,256,128]{2,1,0:T(8,128)(2,1)} %first.1), calls=%async_computation | async-start | bytes 2097152 | tf_op jit(solution)/shard_map/all_to_all | solution.py:200
  13.8 0.9 copy-done.11
  14.7 0.8 copy-done.12
  17.5 3.0 %prep.1 = (s32[2,68]{1,0:T(2,128)S(1)}, s32[2,68]{1,0:T(2,128)S(1)}, s32[2,68]{1,0:T(2,128)S(1)}, s32[2]{0:T(128)S(1)}, f32[1,128]{1,0:T(1,128)S(1)}, /*index=5*...) custom-call(s32[64]{0:T(128)S(1)} %bitcast.16, s32[64]{0:T(128)S(1)} %bitcast.17, ...), custom_call_target="tpu_custom_call" | custom-call | flops 100000000 | bytes 2097152 | tf_op jit(solution)/shard_map/prep/pallas_call | solution.py:232
  22.3 17.8 %all-to-all-done.blocks = bf16[16,256,128]{2,1,0:T(8,128)(2,1)S(1)} async-done(((bf16[16,256,128]{2,1,0:T(8,128)(2,1)}), bf16[16,256,128]{2,1,0:T(8,128)(2,1)S(1)}, u32[]{:S(2)}, u32[]{:S(2)}) %all-to-all-start) | async-done | bytes 1048608 | tf_op jit(solution)/shard_map/all_to_all | solution.py:200
  40.2 2.4 %forward1.1 = bf16[16,256,128]{2,1,0:T(8,128)(2,1)S(1)} custom-call(s32[2]{0:T(128)S(1)} %get-tuple-element.21.counts, s32[2,68]{1,0:T(2,128)S(1)} %get-tuple-element.22.tiles, s32[2,68]{1,0:T(2,128)S(1)} %get-tuple-element.23.rows_of, s32[2,68]{1,0:T(2,128)S(1)} %get-tuple-element.24.cols_of, bf16[64,128,128]{2,1,0:T(8,128)(2,1)S(1)} %bitcast.8, ...), custom_call_target="tpu_custom_call" | custom-call | flops 268435456 | bytes 2097152 | tf_op jit(solution)/shard_map/forward1/pallas_call | solution.py:249
  42.6 4.0 %collective-permute-start = (bf16[16,256,128]{2,1,0:T(8,128)(2,1)S(1)}, bf16[16,256,128]{2,1,0:T(8,128)(2,1)S(1)}, u32[]{:S(2)}, u32[]{:S(2)}) collective-permute-start(bf16[16,256,128]{2,1,0:T(8,128)(2,1)S(1)} %forward1.1), channel_id=1, source_target_pairs={{0,16},{16,0},{1,17},{17,1},{2,18},{18,2},{3,19},{19,3},{4,20},{20... | collective-permute-start | bytes 3145736 | tf_op jit(solution)/shard_map/ppermute | solution.py:196
  46.6 2.2 %forward0.1 = bf16[16,256,128]{2,1,0:T(8,128)(2,1)S(1)} custom-call(s32[2]{0:T(128)S(1)} %get-tuple-element.21.counts, s32[2,68]{1,0:T(2,128)S(1)} %get-tuple-element.22.tiles, s32[2,68]{1,0:T(2,128)S(1)} %get-tuple-element.23.rows_of, s32[2,68]{1,0:T(2,128)S(1)} %get-tuple-element.24.cols_of, bf16[64,128,128]{2,1,0:T(8,128)(2,1)S(1)} %bitcast.9, ...), custom_call_target="tpu_custom_call" | custom-call | flops 268435456 | bytes 2097152 | tf_op jit(solution)/shard_map/forward0/pallas_call | solution.py:249
  49.2 35.8 %all_to_all.35.parts = bf16[16,256,128]{2,1,0:T(8,128)(2,1)S(1)} all-to-all(bf16[16,256,128]{2,1,0:T(8,128)(2,1)S(1)} %add_convert_fusion), channel_id=1, replica_groups=mesh['xl'=2,'z'=8,'core'=2,'xh'=2,'y'=8] {'xl','z'}, dimensions={0} | all-to-all | bytes 2097152 | tf_op jit(solution)/shard_map/all_to_all | solution.py:200
  85.0 1.2 state.3
  86.1 31.3 %all_to_all.36.blocks = bf16[16,128,256]{2,1,0:T(8,128)(2,1)S(1)} all-to-all(bf16[16,128,256]{2,1,0:T(8,128)(2,1)S(1)} %get-tuple-element.29), channel_id=1, replica_groups=mesh['xl'=2,'z'=8,'core'=2,'xh'=2,'y'=8] {'xl','z'}, dimensions={0} | all-to-all | bytes 2097152 | tf_op jit(solution)/shard_map/all_to_all | solution.py:200
  117.4 4.7 %collective-permute-start.1 = (bf16[16,128,256]{2,1,0:T(8,128)(2,1)S(1)}, bf16[16,128,256]{2,1,0:T(8,128)(2,1)S(1)}, u32[]{:S(2)}, u32[]{:S(2)}) collective-permute-start(bf16[16,128,256]{2,1,0:T(8,128)(2,1)S(1)} %all_to_all.36.blocks), channel_id=1, source_target_pairs={{0,16},{16,0},{1,17},{17,1},{2,18},{18,2},{3,19},{19,3},{4,20},{20... | collective-permute-start | bytes 3145736 | tf_op jit(solution)/shard_map/ppermute | solution.py:196
  122.2 2.1 %adjoint0.1.start = f32[17,128,256]{2,1,0:T(8,128)S(1)} custom-call(s32[2]{0:T(128)S(1)} %get-tuple-element.21.counts, s32[2,68]{1,0:T(2,128)S(1)} %get-tuple-element.22.tiles, s32[2,68]{1,0:T(2,128)S(1)} %get-tuple-element.23.rows_of, s32[2,68]{1,0:T(2,128)S(1)} %get-tuple-element.24.cols_of, bf16[64,128,128]{2,1,0:T(8,128)(2,1)S(1)} %bitcast.10, ...), custom_call_target="tpu_custom_call" | custom-call | flops 268435456 | bytes 2097152 | tf_op jit(solution)/shard_map/adjoint0/pallas_call | solution.py:269
  124.4 2.4 %adjoint1.1 = bf16[16,128,256]{2,1,0:T(8,128)(2,1)S(1)} custom-call(s32[2]{0:T(128)S(1)} %get-tuple-element.21.counts, s32[2,68]{1,0:T(2,128)S(1)} %get-tuple-element.22.tiles, s32[2,68]{1,0:T(2,128)S(1)} %get-tuple-element.23.rows_of, s32[2,68]{1,0:T(2,128)S(1)} %get-tuple-element.24.cols_of, bf16[64,128,128]{2,1,0:T(8,128)(2,1)S(1)} %bitcast.11, ...), custom_call_target="tpu_custom_call" | custom-call | flops 268435456 | bytes 2097152 | tf_op jit(solution)/shard_map/adjoint1/pallas_call | solution.py:276
  126.9 31.3 %all_to_all.37.parts = bf16[16,128,256]{2,1,0:T(8,128)(2,1)S(1)} all-to-all(bf16[16,128,256]{2,1,0:T(8,128)(2,1)S(1)} %adjoint1.1), channel_id=1, replica_groups=mesh['xl'=2,'z'=8,'core'=2,'xh'=2,'y'=8] {'xh','y'}, dimensions={0} | all-to-all | bytes 2097152 | tf_op jit(solution)/shard_map/all_to_all | solution.py:200
  158.2 1.3 grad.1
  159.5 3.8 %collective-permute-start.2 = (bf16[384,128]{1,0:T(8,128)(2,1)S(1)}, bf16[384,128]{1,0:T(8,128)(2,1)S(1)}, u32[]{:S(2)}, u32[]{:S(2)}) collective-permute-start(bf16[384,128]{1,0:T(8,128)(2,1)S(1)} %get-tuple-element.35), channel_id=1, source_target_pairs={{0,16},{16,0},{1,17},{17,1},{2,18},{18,2},{3,19},{19,3},{4,20},{20... | collective-permute-start | bytes 294920 | tf_op jit(solution)/shard_map/ppermute | solution.py:196
  163.4 0.9 collective-permute-done.2
  164.3 11.1 %all_to_all.38.parts = bf16[16,24,128]{2,1,0:T(8,128)(2,1)S(1)} all-to-all(bf16[16,24,128]{2,1,0:T(8,128)(2,1)S(1)} %bitcast.19), channel_id=1, replica_groups=mesh['xl'=2,'z'=8,'core'=2,'xh'=2,'y'=8] {'xl','z'}, dimensions={0} | all-to-all | bytes 196608 | tf_op jit(solution)/shard_map/all_to_all | solution.py:200
  175.5 13.6 %all_to_all.39.parts = bf16[16,24,128]{2,1,0:T(8,128)(2,1)S(1)} all-to-all(bf16[16,24,128]{2,1,0:T(8,128)(2,1)S(1)} %sum_chip.1), channel_id=1, replica_groups=mesh['xl'=2,'z'=8,'core'=2,'xh'=2,'y'=8] {'xh','y'}, dimensions={0} | all-to-all | bytes 196608 | tf_op jit(solution)/shard_map/all_to_all | solution.py:200
  189.1 10.0 %all_to_all.40 = bf16[16,24,128]{2,1,0:T(8,128)(2,1)S(1)} all-to-all(bf16[16,24,128]{2,1,0:T(8,128)(2,1)S(1)} %sum_col.1), channel_id=1, replica_groups=mesh['xl'=2,'z'=8,'core'=2,'xh'=2,'y'=8] {'xl','z'}, dimensions={0} | all-to-all | bytes 196608 | tf_op jit(solution)/shard_map/all_to_all | solution.py:200
  199.0 6.2 %collective-permute-start.3 = (bf16[384,128]{1,0:T(8,128)(2,1)S(1)}, bf16[384,128]{1,0:T(8,128)(2,1)S(1)}, u32[]{:S(2)}, u32[]{:S(2)}) collective-permute-start(bf16[384,128]{1,0:T(8,128)(2,1)S(1)} %bitcast.12), channel_id=1, source_target_pairs={{0,16},{16,0},{1,17},{17,1},{2,18},{18,2},{3,19},{19,3},{4,20},{20... | collective-permute-start | bytes 294920 | tf_op jit(solution)/shard_map/ppermute | solution.py:196
  205.3 0.9 collective-permute-done.3.other
  (37 shorter events, 5.7 us)
Async XLA Ops:
  0.6 12.5 %copy-start.2 = (f32[128,256]{1,0:T(8,128)S(1)}, f32[128,256]{1,0:T(8,128)}, u32[]{:S(2)}) copy-start(f32[128,256]{1,0:T(8,128)} %cotangent.3) | copy-start | bytes 393220
  0.6 39.5 %copy-start = (bf16[1,1,64,128,128]{4,3,2,1,0:T(8,128)(2,1)S(1)}, bf16[1,1,64,128,128]{4,3,2,1,0:T(8,128)(2,1)}, u32[]{:S(2)}) copy-start(bf16[1,1,64,128,128]{4,3,2,1,0:T(8,128)(2,1)} %param.14) | copy-start | bytes 6291460
  2.9 37.3 %all-to-all-start = ((bf16[16,256,128]{2,1,0:T(8,128)(2,1)}), bf16[16,256,128]{2,1,0:T(8,128)(2,1)S(1)}, u32[]{:S(2)}, u32[]{:S(2)}) async-start(bf16[16,256,128]{2,1,0:T(8,128)(2,1)} %first.1), calls=%async_computation | async-start | bytes 2097152 | tf_op jit(solution)/shard_map/all_to_all | solution.py:200
  13.1 0.7 copy-start.8
  13.8 0.9 copy-start.11
  14.7 0.8 copy-start.12
  15.5 0.7 copy-start.13
  16.2 0.7 copy-start.14
  16.8 0.7 copy-start.15
  20.6 0.6 copy-start.4
  21.2 0.6 copy-start.6
  21.8 0.5 copy-start.9
  42.6 6.3 %collective-permute-start = (bf16[16,256,128]{2,1,0:T(8,128)(2,1)S(1)}, bf16[16,256,128]{2,1,0:T(8,128)(2,1)S(1)}, u32[]{:S(2)}, u32[]{:S(2)}) collective-permute-start(bf16[16,256,128]{2,1,0:T(8,128)(2,1)S(1)} %forward1.1), channel_id=1, source_target_pairs={{0,16},{16,0},{1,17},{17,1},{2,18},{18,2},{3,19},{19,3},{4,20},{20... | collective-permute-start | bytes 3145736 | tf_op jit(solution)/shard_map/ppermute | solution.py:196
  48.8 36.1 %copy-start.1 = (f32[256,256]{1,0:T(8,128)S(1)}, f32[256,256]{1,0:T(8,128)}, u32[]{:S(2)}) copy-start(f32[256,256]{1,0:T(8,128)} %weight.3) | copy-start | bytes 786436
  48.8 36.1 %copy-start.10 = (f32[1,128]{1,0:T(1,128)S(1)}, f32[1,128]{1,0:T(1,128)}, u32[]{:S(2)}) copy-start(f32[1,128]{1,0:T(1,128)} %copy-done.9) | copy-start | bytes 1540
  117.4 7.0 %collective-permute-start.1 = (bf16[16,128,256]{2,1,0:T(8,128)(2,1)S(1)}, bf16[16,128,256]{2,1,0:T(8,128)(2,1)S(1)}, u32[]{:S(2)}, u32[]{:S(2)}) collective-permute-start(bf16[16,128,256]{2,1,0:T(8,128)(2,1)S(1)} %all_to_all.36.blocks), channel_id=1, source_target_pairs={{0,16},{16,0},{1,17},{17,1},{2,18},{18,2},{3,19},{19,3},{4,20},{20... | collective-permute-start | bytes 3145736 | tf_op jit(solution)/shard_map/ppermute | solution.py:196
  126.9 31.3 %copy-start.3 = (f32[128,256]{1,0:T(8,128)S(1)}, f32[128,256]{1,0:T(8,128)}, u32[]{:S(2)}) copy-start(f32[128,256]{1,0:T(8,128)} %get-tuple-element.17.states) | copy-start | bytes 393220
  126.9 31.3 %copy-start.5 = (f32[128,128]{1,0:T(8,128)S(1)}, f32[128,128]{1,0:T(8,128)}, u32[]{:S(2)}) copy-start(f32[128,128]{1,0:T(8,128)} %copy-done.4) | copy-start | bytes 196612
  126.9 31.3 %copy-start.7 = (f32[128,128]{1,0:T(8,128)S(1)}, f32[128,128]{1,0:T(8,128)}, u32[]{:S(2)}) copy-start(f32[128,128]{1,0:T(8,128)} %copy-done.6) | copy-start | bytes 196612
  159.5 4.8 %collective-permute-start.2 = (bf16[384,128]{1,0:T(8,128)(2,1)S(1)}, bf16[384,128]{1,0:T(8,128)(2,1)S(1)}, u32[]{:S(2)}, u32[]{:S(2)}) collective-permute-start(bf16[384,128]{1,0:T(8,128)(2,1)S(1)} %get-tuple-element.35), channel_id=1, source_target_pairs={{0,16},{16,0},{1,17},{17,1},{2,18},{18,2},{3,19},{19,3},{4,20},{20... | collective-permute-start | bytes 294920 | tf_op jit(solution)/shard_map/ppermute | solution.py:196
  199.0 7.2 %collective-permute-start.3 = (bf16[384,128]{1,0:T(8,128)(2,1)S(1)}, bf16[384,128]{1,0:T(8,128)(2,1)S(1)}, u32[]{:S(2)}, u32[]{:S(2)}) collective-permute-start(bf16[384,128]{1,0:T(8,128)(2,1)S(1)} %bitcast.12), channel_id=1, source_target_pairs={{0,16},{16,0},{1,17},{17,1},{2,18},{18,2},{3,19},{19,3},{4,20},{20... | collective-permute-start | bytes 294920 | tf_op jit(solution)/shard_map/ppermute | solution.py:196

commit v4 on v3

--- a/solution.py
+++ b/solution.py
@@ -14,7 +14,8 @@
 CHIP = ("xl", "z")
 COL = ("xh", "y")
 ROW = ("xl", "z", "core")
-UNROLL = 4
+UNROLL = 16
+REST = 4
 FIRST_MIB = 56
 VMEM = pl.BlockSpec(memory_space=pltpu.VMEM)
 SMEM = pl.BlockSpec(memory_space=pltpu.SMEM)
@@ -86,26 +87,43 @@
     count = counts[side]
     spare = acc.shape[0] - 1
 
-    def group(g, carry):
+    def group(size, start, g, carry):
         products, slots = [], []
-        for u in range(UNROLL):
-            t = g * UNROLL + u
+        for u in range(size):
+            t = start + g * size + u
             slots.append(jnp.where(t < count, slots_of[side, t], spare))
             products.append(product_of(tiles[side, t], blocks_of[side, t]))
         for slot, product in zip(slots, products):
             acc[slot] += product
         return carry
 
-    lax.fori_loop(0, (count + UNROLL - 1) // UNROLL, group, 0)
-
-
-def forward_kernel(counts, tiles, rows_of, cols_of, values, blocks, out, acc, *, side):
+    full = count // UNROLL
+    done = full * UNROLL
+    lax.fori_loop(0, full, functools.partial(group, UNROLL, 0), 0)
+    lax.fori_loop(0, (count - done + REST - 1) // REST, functools.partial(group, REST, done), 0)
+
+
+def forward_own_kernel(counts, tiles, rows_of, cols_of, values, blocks, acc):
     acc[...] = jnp.zeros_like(acc)
 
     def product_of(tile, block):
         return jnp.dot(blocks[block], values[tile], preferred_element_type=F32)
 
-    add_tiles(side, counts, tiles, cols_of, rows_of, product_of, acc)
+    add_tiles(0, counts, tiles, cols_of, rows_of, product_of, acc)
+
+
+def join_kernel(mine, received, out):
+    for q in range(out.shape[0]):
+        out[q] = (mine[q] + received[q].astype(F32)).astype(BF16)
+
+
+def forward_other_kernel(counts, tiles, rows_of, cols_of, values, blocks, out, acc):
+    acc[...] = jnp.zeros_like(acc)
+
+    def product_of(tile, block):
+        return jnp.dot(blocks[block], values[tile], preferred_element_type=F32)
+
+    add_tiles(1, counts, tiles, cols_of, rows_of, product_of, acc)
     out[...] = acc[0 : out.shape[0]].astype(BF16)
 
 
@@ -141,7 +159,7 @@
 
 
 def grad_kernel(
-    core_ref, parts, inv_wide, cotangent, weight, states, summed_t, features_t, adjoint, keep, send, *, factor
+    parts, inv_wide, cotangent, weight, states, summed_t, features_t, adjoint, out, *, factor
 ):
     pulled = summed_up(parts) * inv_wide[:, :1]
     moved = lax.dot_general(
@@ -153,13 +171,13 @@
     masked = (1.0 - state * state) * result * factor
     weight_part = jnp.dot(summed_t[...], masked, precision=HIGH, preferred_element_type=F32)
     input_part = jnp.dot(features_t[...], masked, precision=HIGH, preferred_element_type=F32)
-    first = core_ref[0] == 0
-    width = weight_part.shape[0]
-    half = weight_part.shape[1] // 2
-    for at, part in ((0, weight_part), (width, input_part)):
-        left, right = part[:, :half], part[:, half:]
-        keep[at : at + part.shape[0], :] = jnp.where(first, left, right).astype(keep.dtype)
-        send[at : at + part.shape[0], :] = jnp.where(first, right, left).astype(send.dtype)
+    half = out.shape[1]
+    at = 0
+    for side in range(2):
+        for part in (weight_part, input_part):
+            piece = part[:, side * half : (side + 1) * half]
+            out[at : at + piece.shape[0], :] = piece.astype(out.dtype)
+            at += piece.shape[0]
 
 
 def sum_kernel(parts, out):
@@ -168,15 +186,13 @@
         out[q] = total
 
 
-def last_kernel(core_ref, own, other, weight_grad, input_grad):
-    first = core_ref[0] == 0
-    width = weight_grad.shape[0]
-    half = own.shape[1]
-    for at, out in ((0, weight_grad), (width, input_grad)):
-        mine = own[at : at + out.shape[0], :].astype(F32)
-        theirs = other[at : at + out.shape[0], :].astype(F32)
-        out[:, :half] = jnp.where(first, mine, theirs)
-        out[:, half:] = jnp.where(first, theirs, mine)
+def last_kernel(sums, weight_grad, input_grad):
+    half = sums.shape[1]
+    at = 0
+    for side in range(2):
+        for out in (weight_grad, input_grad):
+            out[:, side * half : (side + 1) * half] = sums[at : at + out.shape[0], :].astype(F32)
+            at += out.shape[0]
 
 
 def call(kernel, outs, specs, scratch=(), name=None, mib=12, flops=10**8, out_specs=None):
@@ -221,7 +237,7 @@
     core = lax.axis_index("core").astype(jnp.int32).reshape(1)
     degree_row = degrees.reshape(1, nodes)
     block = values.shape[1]
-    room = values.shape[0] + UNROLL
+    room = values.shape[0] + REST
     tile_flops = values.shape[0] * block * block * width
 
     spread = call(
@@ -245,18 +261,26 @@
     )(rows, cols, live, core, degree_row, features, input_map, cotangent)
     order = (counts, tiles, rows_of, cols_of, values)
 
-    def forward(side):
-        return call(
-            functools.partial(forward_kernel, side=side),
-            shape((chips, width, block), BF16),
-            [SMEM] * 4 + [VMEM] * 2,
-            [pltpu.VMEM((chips + 1, width, block), F32)],
-            name=f"forward{side}",
-            flops=tile_flops,
-        )(*order, gathered)
-
-    received = swap(forward(1))
-    parts = exchange((forward(0).astype(F32) + received.astype(F32)).astype(BF16), CHIP)
+    sent = call(
+        forward_other_kernel,
+        shape((chips, width, block), BF16),
+        [SMEM] * 4 + [VMEM] * 2,
+        [pltpu.VMEM((chips + 1, width, block), F32)],
+        name="forward1",
+        flops=tile_flops,
+    )(*order, gathered)
+    received = swap(sent)
+    mine = call(
+        forward_own_kernel,
+        shape((chips + 1, width, block), F32),
+        [SMEM] * 4 + [VMEM] * 2,
+        name="forward0",
+        flops=tile_flops,
+    )(*order, gathered)
+    joined = call(join_kernel, shape((chips, width, block), BF16), [VMEM] * 2, name="join")(
+        mine, received
+    )
+    parts = exchange(joined, CHIP)
     states, summed_t, spread = call(
         state_kernel,
         (shape((nodes, width), F32), shape((width, nodes), F32), shape((chips, nodes, width), BF16)),
@@ -284,26 +308,25 @@
     parts = exchange(partial, COL)
     factor = 1.0 / math.sqrt(nodes * 2 * chips * col_devices)
     total = width + inputs
-    adjoint, keep, send = call(
+    members = 2 * chips
+    adjoint, sums = call(
         functools.partial(grad_kernel, factor=factor),
-        (shape((nodes, width), F32),) + (shape((total, width // 2), BF16),) * 2,
-        [SMEM] + [VMEM] * 7,
+        (shape((nodes, width), F32), shape((2 * total, width // 2), BF16)),
+        [VMEM] * 7,
         name="grad",
-    )(core, parts, inv_wide, cotangent, weight, states, summed_t, features_t)
-    piece = (total // chips, width // 2)
-    halves = (keep.astype(F32) + swap(send).astype(F32)).astype(BF16).reshape(chips, *piece)
-    parts = exchange(halves, CHIP)
-    spread = call(sum_kernel, shape((col_devices, *piece), BF16), [VMEM], name="sum_chip")(parts)
+    )(parts, inv_wide, cotangent, weight, states, summed_t, features_t)
+    piece = (2 * total // members, width // 2)
+    parts = exchange(sums.reshape(members, *piece), ROW)
+    spread = call(sum_kernel, shape((col_devices, *piece), BF16), [VMEM], name="sum_row")(parts)
     parts = exchange(spread, COL)
-    spread = call(sum_kernel, shape((chips, *piece), BF16), [VMEM], name="sum_col")(parts)
-    own = exchange(spread, CHIP).reshape(total, width // 2)
-    other = swap(own)
+    spread = call(sum_kernel, shape((members, *piece), BF16), [VMEM], name="sum_col")(parts)
+    sums = exchange(spread, ROW).reshape(2 * total, width // 2)
     weight_grad, input_grad = call(
         last_kernel,
         (shape((width, width), F32), shape((inputs, width), F32)),
-        [SMEM] + [VMEM] * 2,
+        [VMEM],
         name="last",
-    )(core, own, other)
+    )(sums)
     return states, adjoint, weight_grad, input_grad
 
 

time: 208 us -> 206 us (level)
  blocking collectives: 133 us -> 145 us
  starting transfers between devices: 29 us -> 18.9 us
    all_to_all x6, blocking collectives: 133 us -> 145 us  [exchange(): return lax.all_to_all(x, axes, 0, 0, tiled=True)]
    ppermute x4 -> x2, starting transfers between devices: 18.8 us -> 8.73 us  [swap(): return lax.ppermute(x, 'core', [(0, 1), (1, 0)])]
    pallas_call x4 -> x5, Pallas kernels: 4.7 us -> 3.88 us  [the longest x1 1.87 us: on_device(): call(forward_own_kernel, shape((chips + 1, width, block), F32), [SMEM] *...]
  transfers between devices with their start and end apart: 5 -> 3, of which waited for: 4 -> 3; matrix products, arithmetic and copies ran while one was open for 0% -> 0% of each run, Pallas kernels for 4% -> 3%
where the time goes in v4:
time: 206 us; the launch traced here: 205 us
  blocking collectives  145 us (70%)
  starting transfers between devices  18.9 us (9%)
  waiting for transfers between devices  18.5 us (9%)
  Pallas kernels  16.1 us (8%)
  local copies, waits for them, and re-layouts  6.16 us (3%)
    all_to_all x6, blocking collectives, exchange(): return lax.all_to_all(x, axes, 0, 0, tiled=True)  145 us
    all_to_all x1, waiting for transfers between devices, exchange(): return lax.all_to_all(x, axes, 0, 0, tiled=True)  17.8 us
    all_to_all x1, starting transfers between devices, exchange(): return lax.all_to_all(x, axes, 0, 0, tiled=True)  10.2 us
    ppermute x2, starting transfers between devices, swap(): return lax.ppermute(x, 'core', [(0, 1), (1, 0)])  8.73 us
    unnamed x32, local copies, waits for them, and re-layouts  6.16 us
  transfers between devices with their start and end apart: 3, of which 3 were waited for; matrix products, arithmetic and copies ran while one was open for 0% of the time, Pallas kernels for 3%

profile of v4, /device:TPU:1, one launch (start us, length us, event | category | flops | bytes accessed | tf_op | source)
XLA Modules:
  0.0 205.3 jit_solution(14178378128912190052)
XLA Ops:
  0.7 2.2 %first.1 = bf16[16,256,128]{2,1,0:T(8,128)(2,1)} custom-call(f32[128,256]{1,0:T(8,128)} %state.2, s32[1,128]{1,0:T(1,128)} %bitcast.14), custom_call_target="tpu_custom_call" | custom-call | flops 100000000 | bytes 2097152 | tf_op jit(solution)/shard_map/first/pallas_call | solution.py:243
  2.9 10.2 %all-to-all-start = ((bf16[16,256,128]{2,1,0:T(8,128)(2,1)}), bf16[16,256,128]{2,1,0:T(8,128)(2,1)S(1)}, u32[]{:S(2)}, u32[]{:S(2)}) async-start(bf16[16,256,128]{2,1,0:T(8,128)(2,1)} %first.1), calls=%async_computation | async-start | bytes 2097152 | tf_op jit(solution)/shard_map/all_to_all | solution.py:216
  13.8 0.9 copy-done.11
  14.7 0.8 copy-done.12
  15.5 0.7 copy-done.13
  16.2 0.7 copy-done.14
  16.8 0.7 copy-done.15
  17.5 3.0 %prep.1 = (s32[2,68]{1,0:T(2,128)S(1)}, s32[2,68]{1,0:T(2,128)S(1)}, s32[2,68]{1,0:T(2,128)S(1)}, s32[2]{0:T(128)S(1)}, f32[1,128]{1,0:T(1,128)S(1)}, /*index=5*...) custom-call(s32[64]{0:T(128)S(1)} %bitcast.16, s32[64]{0:T(128)S(1)} %bitcast.17, ...), custom_call_target="tpu_custom_call" | custom-call | flops 100000000 | bytes 2097152 | tf_op jit(solution)/shard_map/prep/pallas_call | solution.py:248
  22.3 17.8 %all-to-all-done.blocks = bf16[16,256,128]{2,1,0:T(8,128)(2,1)S(1)} async-done(((bf16[16,256,128]{2,1,0:T(8,128)(2,1)}), bf16[16,256,128]{2,1,0:T(8,128)(2,1)S(1)}, u32[]{:S(2)}, u32[]{:S(2)}) %all-to-all-start) | async-done | bytes 1048608 | tf_op jit(solution)/shard_map/all_to_all | solution.py:216
  40.2 1.8 forward1.1
  41.9 4.2 %collective-permute-start = (bf16[16,256,128]{2,1,0:T(8,128)(2,1)S(1)}, bf16[16,256,128]{2,1,0:T(8,128)(2,1)S(1)}, u32[]{:S(2)}, u32[]{:S(2)}) collective-permute-start(bf16[16,256,128]{2,1,0:T(8,128)(2,1)S(1)} %forward1.1), channel_id=1, source_target_pairs={{0,16},{16,0},{1,17},{17,1},{2,18},{18,2},{3,19},{19,3},{4,20},{20... | collective-permute-start | bytes 3145736 | tf_op jit(solution)/shard_map/ppermute | solution.py:212
  46.1 1.9 forward0.1.mine
  48.6 35.0 %all_to_all.35.parts = bf16[16,256,128]{2,1,0:T(8,128)(2,1)S(1)} all-to-all(bf16[16,256,128]{2,1,0:T(8,128)(2,1)S(1)} %join.1), channel_id=1, replica_groups=mesh['xl'=2,'z'=8,'core'=2,'xh'=2,'y'=8] {'xl','z'}, dimensions={0} | all-to-all | bytes 2097152 | tf_op jit(solution)/shard_map/all_to_all | solution.py:216
  83.6 1.2 state.3
  84.8 31.7 %all_to_all.36.blocks = bf16[16,128,256]{2,1,0:T(8,128)(2,1)S(1)} all-to-all(bf16[16,128,256]{2,1,0:T(8,128)(2,1)S(1)} %get-tuple-element.28), channel_id=1, replica_groups=mesh['xl'=2,'z'=8,'core'=2,'xh'=2,'y'=8] {'xl','z'}, dimensions={0} | all-to-all | bytes 2097152 | tf_op jit(solution)/shard_map/all_to_all | solution.py:216
  116.5 4.5 %collective-permute-start.1 = (bf16[16,128,256]{2,1,0:T(8,128)(2,1)S(1)}, bf16[16,128,256]{2,1,0:T(8,128)(2,1)S(1)}, u32[]{:S(2)}, u32[]{:S(2)}) collective-permute-start(bf16[16,128,256]{2,1,0:T(8,128)(2,1)S(1)} %all_to_all.36.blocks), channel_id=1, source_target_pairs={{0,16},{16,0},{1,17},{17,1},{2,18},{18,2},{3,19},{19,3},{4,20},{20... | collective-permute-start | bytes 3145736 | tf_op jit(solution)/shard_map/ppermute | solution.py:212
  121.0 1.9 adjoint0.1.start
  123.3 1.8 adjoint1.1
  125.1 30.4 %all_to_all.37.parts = bf16[16,128,256]{2,1,0:T(8,128)(2,1)S(1)} all-to-all(bf16[16,128,256]{2,1,0:T(8,128)(2,1)S(1)} %adjoint1.1), channel_id=1, replica_groups=mesh['xl'=2,'z'=8,'core'=2,'xh'=2,'y'=8] {'xh','y'}, dimensions={0} | all-to-all | bytes 2097152 | tf_op jit(solution)/shard_map/all_to_all | solution.py:216
  155.5 1.3 grad.1
  156.8 17.9 %all_to_all.38.parts = bf16[32,24,128]{2,1,0:T(8,128)(2,1)S(1)} all-to-all(bf16[32,24,128]{2,1,0:T(8,128)(2,1)S(1)} %bitcast.12), channel_id=1, replica_groups=mesh['xl'=2,'z'=8,'core'=2,'xh'=2,'y'=8] {'xl','z','core'}, dimensions={0} | all-to-all | bytes 393216 | tf_op jit(solution)/shard_map/all_to_all | solution.py:216
  174.7 13.7 %all_to_all.39.parts = bf16[16,24,128]{2,1,0:T(8,128)(2,1)S(1)} all-to-all(bf16[16,24,128]{2,1,0:T(8,128)(2,1)S(1)} %sum_row.1), channel_id=1, replica_groups=mesh['xl'=2,'z'=8,'core'=2,'xh'=2,'y'=8] {'xh','y'}, dimensions={0} | all-to-all | bytes 196608 | tf_op jit(solution)/shard_map/all_to_all | solution.py:216
  188.5 16.1 %all_to_all.40 = bf16[32,24,128]{2,1,0:T(8,128)(2,1)S(1)} all-to-all(bf16[32,24,128]{2,1,0:T(8,128)(2,1)S(1)} %sum_col.1), channel_id=1, replica_groups=mesh['xl'=2,'z'=8,'core'=2,'xh'=2,'y'=8] {'xl','z','core'}, dimensions={0} | all-to-all | bytes 393216 | tf_op jit(solution)/shard_map/all_to_all | solution.py:216
  204.6 0.8 last.1
  (32 shorter events, 3.4 us)
Async XLA Ops:
  0.6 12.5 %copy-start.2 = (f32[128,256]{1,0:T(8,128)S(1)}, f32[128,256]{1,0:T(8,128)}, u32[]{:S(2)}) copy-start(f32[128,256]{1,0:T(8,128)} %cotangent.3) | copy-start | bytes 393220
  0.6 39.5 %copy-start = (bf16[1,1,64,128,128]{4,3,2,1,0:T(8,128)(2,1)S(1)}, bf16[1,1,64,128,128]{4,3,2,1,0:T(8,128)(2,1)}, u32[]{:S(2)}) copy-start(bf16[1,1,64,128,128]{4,3,2,1,0:T(8,128)(2,1)} %param.14) | copy-start | bytes 6291460
  2.9 37.3 %all-to-all-start = ((bf16[16,256,128]{2,1,0:T(8,128)(2,1)}), bf16[16,256,128]{2,1,0:T(8,128)(2,1)S(1)}, u32[]{:S(2)}, u32[]{:S(2)}) async-start(bf16[16,256,128]{2,1,0:T(8,128)(2,1)} %first.1), calls=%async_computation | async-start | bytes 2097152 | tf_op jit(solution)/shard_map/all_to_all | solution.py:216
  13.1 0.7 copy-start.8
  13.8 0.9 copy-start.11
  14.7 0.8 copy-start.12
  15.5 0.7 copy-start.13
  16.2 0.7 copy-start.14
  16.8 0.7 copy-start.15
  20.5 0.6 copy-start.4
  21.2 0.6 copy-start.6
  21.8 0.5 copy-start.9
  41.9 6.5 %collective-permute-start = (bf16[16,256,128]{2,1,0:T(8,128)(2,1)S(1)}, bf16[16,256,128]{2,1,0:T(8,128)(2,1)S(1)}, u32[]{:S(2)}, u32[]{:S(2)}) collective-permute-start(bf16[16,256,128]{2,1,0:T(8,128)(2,1)S(1)} %forward1.1), channel_id=1, source_target_pairs={{0,16},{16,0},{1,17},{17,1},{2,18},{18,2},{3,19},{19,3},{4,20},{20... | collective-permute-start | bytes 3145736 | tf_op jit(solution)/shard_map/ppermute | solution.py:212
  48.0 35.6 %copy-start.1 = (f32[256,256]{1,0:T(8,128)S(1)}, f32[256,256]{1,0:T(8,128)}, u32[]{:S(2)}) copy-start(f32[256,256]{1,0:T(8,128)} %weight.3) | copy-start | bytes 786436
  48.0 35.6 %copy-start.10 = (f32[1,128]{1,0:T(1,128)S(1)}, f32[1,128]{1,0:T(1,128)}, u32[]{:S(2)}) copy-start(f32[1,128]{1,0:T(1,128)} %copy-done.9) | copy-start | bytes 1540
  116.5 6.8 %collective-permute-start.1 = (bf16[16,128,256]{2,1,0:T(8,128)(2,1)S(1)}, bf16[16,128,256]{2,1,0:T(8,128)(2,1)S(1)}, u32[]{:S(2)}, u32[]{:S(2)}) collective-permute-start(bf16[16,128,256]{2,1,0:T(8,128)(2,1)S(1)} %all_to_all.36.blocks), channel_id=1, source_target_pairs={{0,16},{16,0},{1,17},{17,1},{2,18},{18,2},{3,19},{19,3},{4,20},{20... | collective-permute-start | bytes 3145736 | tf_op jit(solution)/shard_map/ppermute | solution.py:212
  122.9 32.6 %copy-start.3 = (f32[128,256]{1,0:T(8,128)S(1)}, f32[128,256]{1,0:T(8,128)}, u32[]{:S(2)}) copy-start(f32[128,256]{1,0:T(8,128)} %get-tuple-element.16.states) | copy-start | bytes 393220
  122.9 32.6 %copy-start.5 = (f32[128,128]{1,0:T(8,128)S(1)}, f32[128,128]{1,0:T(8,128)}, u32[]{:S(2)}) copy-start(f32[128,128]{1,0:T(8,128)} %copy-done.4) | copy-start | bytes 196612
  122.9 32.6 %copy-start.7 = (f32[128,128]{1,0:T(8,128)S(1)}, f32[128,128]{1,0:T(8,128)}, u32[]{:S(2)}) copy-start(f32[128,128]{1,0:T(8,128)} %copy-done.6) | copy-start | bytes 196612

commit v5 on v4

v5 whole, which is shorter than its diff:
```python
import functools
import math

import jax
import jax.numpy as jnp
from jax import lax
from jax.experimental import pallas as pl
from jax.experimental.pallas import tpu as pltpu
from jax.sharding import Mesh, PartitionSpec as P


HIGH = lax.Precision.HIGHEST
BF16 = jnp.bfloat16
F32 = jnp.float32
COL = ("xh", "y")
SIDE = ("core", "xh", "y")
ROW = ("xl", "z", "core")
UNROLL = 16
REST = 4
FIRST_MIB = 56
VMEM = pl.BlockSpec(memory_space=pltpu.VMEM)
ANY = pl.BlockSpec(memory_space=pl.ANY)
SMEM = pl.BlockSpec(memory_space=pltpu.SMEM)


def shape(dims, dtype):
    return jax.ShapeDtypeStruct(dims, dtype)


def summed_up(parts, first=0, step=1):
    total = parts[first].astype(F32)
    for q in range(first + step, parts.shape[0], step):
        total += parts[q].astype(F32)
    return total


def first_kernel(state, degrees, out):
    inverse = lax.rsqrt(degrees[...].astype(F32))
    scaled = (jnp.transpose(state[...]) * inverse).astype(BF16)
    half = out.shape[0] // 2
    size = out.shape[1]
    for q in range(half):
        out[q] = scaled[:size, :]
        out[half + q] = scaled[size:, :]


def pack_kernel(rows, cols, live, out):
    for q, x in enumerate((rows, cols, live)):
        out[q : q + 1, :] = x[...]


def prep_kernel(shared, values, degrees, features, input_map, cotangent, inv_row, inv_wide, driving, features_t, cotangent_scaled):
    inverse = lax.rsqrt(degrees[...].astype(F32))
    inv_row[...] = inverse
    wide = jnp.transpose(jnp.broadcast_to(inverse, inv_wide.shape))
    inv_wide[...] = wide
    features_t[...] = jnp.transpose(features[...])
    driving[...] = jnp.dot(
        features[...], input_map[...], precision=HIGH, preferred_element_type=F32
    )
    cotangent_scaled[...] = cotangent[...] * wide[:, :1]


def live_count(places):
    return lax.fori_loop(0, places.shape[1], lambda t, n: n + places[2, t], jnp.int32(0))


def add_tiles(places, core, values, forward, blocks, acc):
    count = live_count(places)
    spare = acc.shape[0] - 1
    start = core * (spare // 2 if not forward else blocks.shape[0] // 2)

    def group(size, begin, g, carry):
        products, slots = [], []
        for u in range(size):
            t = begin + g * size + u
            row, col = start + places[0, t], places[1, t]
            if forward:
                product = jnp.dot(blocks[row], values[t], preferred_element_type=F32)
            else:
                product = jnp.dot(values[t], blocks[col], preferred_element_type=F32)
            products.append(product)
            slots.append(jnp.where(t < count, col if forward else row, spare))
        for slot, product in zip(slots, products):
            acc[slot] += product
        return carry

    full = count // UNROLL
    done = full * UNROLL
    lax.fori_loop(0, full, functools.partial(group, UNROLL, 0), 0)
    lax.fori_loop(0, (count - done + REST - 1) // REST, functools.partial(group, REST, done), 0)


def tiles_kernel(core_ref, places, other_places, values, other_values, blocks, out, acc, held, sem, *, forward):
    core = core_ref[0]
    copy = pltpu.make_async_copy(other_values, held, sem)
    copy.start()
    acc[...] = jnp.zeros_like(acc)
    add_tiles(places, core, values, forward, blocks, acc)
    copy.wait()
    add_tiles(other_places, 1 - core, held, forward, blocks, acc)
    out[...] = acc[0 : out.shape[0]].astype(BF16)


def state_kernel(parts, inv_row, weight, driving, cotangent_scaled, states, summed_t, out):
    total = jnp.concatenate([summed_up(parts, 0, 2), summed_up(parts, 1, 2)], axis=0)
    total = total * inv_row[...]
    summed_t[...] = total
    moved = jnp.dot(jnp.transpose(total), weight[...], precision=HIGH, preferred_element_type=F32)
    state = jnp.tanh(moved + driving[...])
    states[...] = state
    slopes = 1.0 - state * state
    scaled = (slopes * cotangent_scaled[...]).astype(BF16)
    size = out.shape[2]
    for q in range(out.shape[0]):
        out[q] = scaled[:, (q % 2) * size : (q % 2 + 1) * size]


def grad_kernel(
    parts, inv_wide, cotangent, weight, states, summed_t, features_t, adjoint, out, *, factor
):
    middle = parts.shape[0] // 2
    total = jnp.concatenate(
        [summed_up(parts.at[pl.ds(0, middle)]), summed_up(parts.at[pl.ds(middle, middle)])], axis=1
    )
    pulled = total * inv_wide[:, :1]
    moved = lax.dot_general(
        pulled, weight[...], (((1,), (1,)), ((), ())), precision=HIGH, preferred_element_type=F32
    )
    result = cotangent[...] + moved
    adjoint[...] = result
    state = states[...]
    masked = (1.0 - state * state) * result * factor
    weight_part = jnp.dot(summed_t[...], masked, precision=HIGH, preferred_element_type=F32)
    input_part = jnp.dot(features_t[...], masked, precision=HIGH, preferred_element_type=F32)
    half = out.shape[1]
    at = 0
    for side in range(2):
        for part in (weight_part, input_part):
            piece = part[:, side * half : (side + 1) * half]
            out[at : at + piece.shape[0], :] = piece.astype(out.dtype)
            at += piece.shape[0]


def sum_kernel(parts, out):
    total = summed_up(parts).astype(out.dtype)
    for q in range(out.shape[0]):
        out[q] = total


def last_kernel(sums, weight_grad, input_grad):
    half = sums.shape[1]
    at = 0
    for side in range(2):
        for out in (weight_grad, input_grad):
            out[:, side * half : (side + 1) * half] = sums[at : at + out.shape[0], :].astype(F32)
            at += out.shape[0]


def call(kernel, outs, specs, scratch=(), mib=12, flops=10**8, out_specs=None):
    return pl.pallas_call(
        kernel,
        out_shape=outs,
        in_specs=specs,
        out_specs=jax.tree.map(lambda _: VMEM, outs) if out_specs is None else out_specs,
        scratch_shapes=list(scratch),
        compiler_params=pltpu.CompilerParams(vmem_limit_bytes=mib * 2**20),
        cost_estimate=pl.CostEstimate(flops=flops, bytes_accessed=2**21, transcendentals=0),
    )


def swap(x):
    return lax.ppermute(x, "core", [(0, 1), (1, 0)])


def exchange(x, axes):
    return lax.all_to_all(x, axes, 0, 0, tiled=True)


def body(
    starting_state,
    features,
    cotangent,
    degrees,
    tile_values,
    tile_rows,
    tile_cols,
    tile_live,
    weight,
    input_map,
):
    values = tile_values[0, 0]
    nodes, width = starting_state.shape
    inputs = features.shape[1]
    members = lax.axis_size(ROW)
    col_devices = lax.axis_size(COL)
    sides = 2 * col_devices
    core = lax.axis_index("core").astype(jnp.int32).reshape(1)
    degree_row = degrees.reshape(1, nodes)
    block = values.shape[1]
    size = width // 2
    places = call(
        pack_kernel, shape((3, values.shape[0]), jnp.int32), [VMEM] * 3, mib=4
    )(tile_rows[0], tile_cols[0], tile_live[0])

    spread = call(
        first_kernel, shape((sides, size, nodes), BF16), [VMEM] * 2, mib=FIRST_MIB
    )(starting_state, degree_row)
    gathered = exchange(spread, SIDE)
    other_places, other_values = swap(places), swap(values)
    prep = call(
        prep_kernel,
        (
            shape((1, nodes), F32),
            shape((nodes, nodes), F32),
            shape((nodes, width), F32),
            shape((inputs, nodes), F32),
            shape((nodes, width), F32),
        ),
        [ANY] + [VMEM] * 5,
    )
    inv_row, inv_wide, driving, features_t, cotangent_scaled = prep(
        other_values, values, degree_row, features, input_map, cotangent
    )
    order = (core, places, other_places, values, other_values)

    def tile_sums(forward, blocks, count, dims):
        return call(
            functools.partial(tiles_kernel, forward=forward),
            shape((count, *dims), BF16),
            [SMEM] * 3 + [VMEM, ANY, VMEM],
            [
                pltpu.VMEM((count + 1, *dims), F32),
                pltpu.VMEM(values.shape, BF16),
                pltpu.SemaphoreType.DMA,
            ],
            mib=16,
            flops=4 * values.shape[0] * block * block * size,
        )(*order, blocks)

    parts = exchange(tile_sums(True, gathered, members, (size, block)), ROW)
    states, summed_t, spread = call(
        state_kernel,
        (shape((nodes, width), F32), shape((width, nodes), F32), shape((members, nodes, size), BF16)),
        [VMEM] * 5,
    )(parts, inv_row, weight, driving, cotangent_scaled)
    blocks = exchange(spread, ROW)
    parts = exchange(tile_sums(False, blocks, sides, (block, size)), SIDE)
    factor = 1.0 / math.sqrt(nodes * members * col_devices)
    total = width + inputs
    adjoint, sums = call(
        functools.partial(grad_kernel, factor=factor),
        (shape((nodes, width), F32), shape((2 * total, width // 2), BF16)),
        [VMEM] * 7,
    )(parts, inv_wide, cotangent, weight, states, summed_t, features_t)
    piece = (2 * total // members, width // 2)
    parts = exchange(sums.reshape(members, *piece), ROW)
    spread = call(sum_kernel, shape((col_devices, *piece), BF16), [VMEM])(parts)
    parts = exchange(spread, COL)
    spread = call(sum_kernel, shape((members, *piece), BF16), [VMEM])(parts)
    sums = exchange(spread, ROW).reshape(2 * total, width // 2)
    weight_grad, input_grad = call(
        last_kernel, (shape((width, width), F32), shape((inputs, width), F32)), [VMEM]
    )(sums)
    return states, adjoint, weight_grad, input_grad


def solution(mesh):
    sizes = mesh.devices.shape
    fine = Mesh(
        mesh.devices.reshape(2, sizes[0] // 4, 2, 2, sizes[1] // 2),
        ("xl", "z", "core", "xh", "y"),
    )
    every = ROW + COL
    return jax.shard_map(
        body,
        mesh=fine,
        in_specs=(
            P(every, None),
            P(every, None),
            P(every, None),
            P(every),
            P(ROW, COL, None, None, None),
            P(ROW, COL, None),
            P(ROW, COL, None),
            P(ROW, COL, None),
            P(),
            P(),
        ),
        out_specs=(P(every, None), P(every, None), P(), P()),
        check_vma=False,
    )
```

time: 206 us -> 210 us (1.019)
  blocking collectives: 145 us -> 113 us
  waiting for transfers between devices: 18.5 us -> 48.9 us
  starting transfers between devices: 18.9 us -> 27.1 us
  Pallas kernels: 16.1 us -> 12.4 us
    all_to_all x6 -> x5, blocking collectives: 145 us -> 113 us  [exchange(): return lax.all_to_all(x, axes, 0, 0, tiled=True)]
    all_to_all x1 -> x2, waiting for transfers between devices: 17.8 us -> 48 us  [exchange(): return lax.all_to_all(x, axes, 0, 0, tiled=True)]
    all_to_all x1 -> x2, starting transfers between devices: 10.2 us -> 16.1 us  [exchange(): return lax.all_to_all(x, axes, 0, 0, tiled=True)]
    pallas_call x12 -> x10, Pallas kernels: 16.1 us -> 12.4 us  [the longest x2 6.62 us: tile_sums(): call(functools.partial(tiles_kernel, forward=forward), shape((count, *dim...]
    ppermute x2, starting transfers between devices: 8.73 us -> 11 us  [swap(): return lax.ppermute(x, 'core', [(0, 1), (1, 0)])]
    unnamed x32 -> x38, local copies, waits for them, and re-layouts: 6.16 us -> 7.12 us
  transfers between devices with their start and end apart: 3 -> 4, of which waited for: 3 -> 3; matrix products, arithmetic and copies ran while one was open for 0% -> 0% of each run, Pallas kernels for 3% -> 1%
where the time goes in v5:
time: 210 us; the launch traced here: 209 us
  blocking collectives  113 us (54%)
  waiting for transfers between devices  48.9 us (23%)
  starting transfers between devices  27.1 us (13%)
  Pallas kernels  12.4 us (6%)
  local copies, waits for them, and re-layouts  7.12 us (3%)
    all_to_all x5, blocking collectives, exchange(): return lax.all_to_all(x, axes, 0, 0, tiled=True)  113 us
    all_to_all x2, waiting for transfers between devices, exchange(): return lax.all_to_all(x, axes, 0, 0, tiled=True)  48 us
    all_to_all x2, starting transfers between devices, exchange(): return lax.all_to_all(x, axes, 0, 0, tiled=True)  16.1 us
    ppermute x2, starting transfers between devices, swap(): return lax.ppermute(x, 'core', [(0, 1), (1, 0)])  11 us
    unnamed x38, local copies, waits for them, and re-layouts  7.12 us
    pallas_call x2, Pallas kernels, tile_sums(): call(functools.partial(tiles_kernel, forward=forward), shape((count, *dim...  6.62 us
  transfers between devices with their start and end apart: 4, of which 3 were waited for; matrix products, arithmetic and copies ran while one was open for 0% of the time, Pallas kernels for 1%

profile of v5, /device:TPU:1, one launch (start us, length us, event | category | flops | bytes accessed | tf_op | source)
XLA Modules:
  0.0 208.9 jit_solution(11089065767967297907)
XLA Ops:
  0.7 8.9 %collective-permute-start.1 = (bf16[64,128,128]{2,1,0:T(8,128)(2,1)}, bf16[64,128,128]{2,1,0:T(8,128)(2,1)}, u32[]{:S(2)}, u32[]{:S(2)}) collective-permute-start(bf16[64,128,128]{2,1,0:T(8,128)(2,1)} %bitcast.8), channel_id=1, source_target_pairs={{0,16},{16,0},{1,17},{17,1},{2,18},{18,2},{3,19},{19,3},{4,20},{20... | collective-permute-start | bytes 6291464 | tf_op jit(solution)/shard_map/ppermute | solution.py:173
  9.6 2.1 shard_map.130
  11.6 4.5 %all-to-all-start = ((bf16[32,128,128]{2,1,0:T(8,128)(2,1)}), bf16[32,128,128]{2,1,0:T(8,128)(2,1)S(1)}, u32[]{:S(2)}, u32[]{:S(2)}) async-start(bf16[32,128,128]{2,1,0:T(8,128)(2,1)} %shard_map.130), calls=%async_computation | async-start | bytes 2097152 | tf_op jit(solution)/shard_map/all_to_all | solution.py:177
  16.2 2.1 %collective-permute-start = (s32[3,64]{1,0:T(4,128)S(1)}, s32[3,64]{1,0:T(4,128)S(1)}, u32[]{:S(2)}, u32[]{:S(2)}) collective-permute-start(s32[3,64]{1,0:T(4,128)S(1)} %shard_map.129.places), channel_id=1, source_target_pairs={{0,16},{16,0},{1,17},{17,1},{2,18},{18,2},{3,19},{19,3},{4,20},{20... | collective-permute-start | bytes 2312 | tf_op jit(solution)/shard_map/ppermute | solution.py:173
  18.3 0.9 collective-permute-done.other_places
  19.2 26.0 %all-to-all-done.blocks = bf16[32,128,128]{2,1,0:T(8,128)(2,1)S(1)} async-done(((bf16[32,128,128]{2,1,0:T(8,128)(2,1)}), bf16[32,128,128]{2,1,0:T(8,128)(2,1)S(1)}, u32[]{:S(2)}, u32[]{:S(2)}) %all-to-all-start) | async-done | bytes 1048608 | tf_op jit(solution)/shard_map/all_to_all | solution.py:177
  45.3 3.3 %shard_map.131 = bf16[32,128,128]{2,1,0:T(8,128)(2,1)S(1)} custom-call(s32[1]{0:T(128)} %bitcast.core_ref, s32[3,64]{1,0:T(4,128)S(1)} %shard_map.129.places, s32[3,64]{1,0:T(4,128)S(1)} %collective-permute-done.other_places, bf16[64,128,128]{2,1,0:T(8,128)(2,1)S(1)} %bitcast.9, bf16[64,128,128]{2,1,0:T(8,128)(2,1)} %collective-permute-done.1.other_values.shared, ...), custom_call_target="tpu_custom_call" | custom-call | flops 536870912 | bytes 2097152 | tf_op jit(solution)/shard_map/pallas_call | solution.py:228
  48.6 1.0 copy-done.1
  49.6 11.6 %all-to-all-start.1 = ((bf16[32,128,128]{2,1,0:T(8,128)(2,1)}), bf16[32,128,128]{2,1,0:T(8,128)(2,1)S(1)}, u32[]{:S(2)}, u32[]{:S(2)}) async-start(bf16[32,128,128]{2,1,0:T(8,128)(2,1)} %copy-done.1), calls=%async_computation.1 | async-start | bytes 2097152 | tf_op jit(solution)/shard_map/all_to_all | solution.py:177
  61.2 0.9 copy-done.5
  62.1 0.8 copy-done.10
  63.9 0.7 copy-done.8
  65.8 21.9 %all-to-all-done.1.parts = bf16[32,128,128]{2,1,0:T(8,128)(2,1)S(1)} async-done(((bf16[32,128,128]{2,1,0:T(8,128)(2,1)}), bf16[32,128,128]{2,1,0:T(8,128)(2,1)S(1)}, u32[]{:S(2)}, u32[]{:S(2)}) %all-to-all-start.1) | async-done | bytes 1048608 | tf_op jit(solution)/shard_map/all_to_all | solution.py:177
  87.7 0.9 copy-done.7
  88.6 0.9 copy-done.9
  89.5 1.2 shard_map.133
  90.7 32.2 %all_to_all.35.blocks = bf16[32,128,128]{2,1,0:T(8,128)(2,1)S(1)} all-to-all(bf16[32,128,128]{2,1,0:T(8,128)(2,1)S(1)} %get-tuple-element.20), channel_id=1, replica_groups=mesh['xl'=2,'z'=8,'core'=2,'xh'=2,'y'=8] {'xl','z','core'}, dimensions={0} | all-to-all | bytes 2097152 | tf_op jit(solution)/shard_map/all_to_all | solution.py:177
  123.0 3.3 %shard_map.134 = bf16[32,128,128]{2,1,0:T(8,128)(2,1)S(1)} custom-call(s32[1]{0:T(128)} %bitcast.core_ref, s32[3,64]{1,0:T(4,128)S(1)} %shard_map.129.places, s32[3,64]{1,0:T(4,128)S(1)} %collective-permute-done.other_places, bf16[64,128,128]{2,1,0:T(8,128)(2,1)S(1)} %bitcast.11, bf16[64,128,128]{2,1,0:T(8,128)(2,1)} %collective-permute-done.1.other_values.shared, ...), custom_call_target="tpu_custom_call" | custom-call | flops 536870912 | bytes 2097152 | tf_op jit(solution)/shard_map/pallas_call | solution.py:228
  126.3 37.0 %all_to_all.36.parts = bf16[32,128,128]{2,1,0:T(8,128)(2,1)S(1)} all-to-all(bf16[32,128,128]{2,1,0:T(8,128)(2,1)S(1)} %shard_map.134), channel_id=1, replica_groups=mesh['xl'=2,'z'=8,'core'=2,'xh'=2,'y'=8] {'core','xh','y'}, dimensions={0} | all-to-all | bytes 2097152 | tf_op jit(solution)/shard_map/all_to_all | solution.py:177
  163.3 1.4 shard_map.135
  164.7 13.9 %all_to_all.37.parts = bf16[32,24,128]{2,1,0:T(8,128)(2,1)S(1)} all-to-all(bf16[32,24,128]{2,1,0:T(8,128)(2,1)S(1)} %bitcast.12), channel_id=1, replica_groups=mesh['xl'=2,'z'=8,'core'=2,'xh'=2,'y'=8] {'xl','z','core'}, dimensions={0} | all-to-all | bytes 393216 | tf_op jit(solution)/shard_map/all_to_all | solution.py:177
  178.6 13.4 %all_to_all.38.parts = bf16[16,24,128]{2,1,0:T(8,128)(2,1)S(1)} all-to-all(bf16[16,24,128]{2,1,0:T(8,128)(2,1)S(1)} %shard_map.136), channel_id=1, replica_groups=mesh['xl'=2,'z'=8,'core'=2,'xh'=2,'y'=8] {'xh','y'}, dimensions={0} | all-to-all | bytes 196608 | tf_op jit(solution)/shard_map/all_to_all | solution.py:177
  192.0 16.1 %all_to_all.39 = bf16[32,24,128]{2,1,0:T(8,128)(2,1)S(1)} all-to-all(bf16[32,24,128]{2,1,0:T(8,128)(2,1)S(1)} %shard_map.137), channel_id=1, replica_groups=mesh['xl'=2,'z'=8,'core'=2,'xh'=2,'y'=8] {'xl','z','core'}, dimensions={0} | all-to-all | bytes 393216 | tf_op jit(solution)/shard_map/all_to_all | solution.py:177
  208.1 0.8 shard_map.138
  (37 shorter events, 2.3 us)
Async XLA Ops:
  0.6 44.6 %copy-start = (bf16[1,1,64,128,128]{4,3,2,1,0:T(8,128)(2,1)S(1)}, bf16[1,1,64,128,128]{4,3,2,1,0:T(8,128)(2,1)}, u32[]{:S(2)}) copy-start(bf16[1,1,64,128,128]{4,3,2,1,0:T(8,128)(2,1)} %param.14) | copy-start | bytes 6291460
  0.6 15.5 %copy-start.18 = (s32[1,1,64]{2,1,0:T(1,128)S(1)}, s32[1,1,64]{2,1,0:T(1,128)}, u32[]{:S(2)}) copy-start(s32[1,1,64]{2,1,0:T(1,128)} %param.17) | copy-start | bytes 772
  0.7 15.5 %copy-start.17 = (s32[1,1,64]{2,1,0:T(1,128)S(1)}, s32[1,1,64]{2,1,0:T(1,128)}, u32[]{:S(2)}) copy-start(s32[1,1,64]{2,1,0:T(1,128)} %param.16) | copy-start | bytes 772
  0.7 15.5 %copy-start.16 = (s32[1,1,64]{2,1,0:T(1,128)S(1)}, s32[1,1,64]{2,1,0:T(1,128)}, u32[]{:S(2)}) copy-start(s32[1,1,64]{2,1,0:T(1,128)} %param.15) | copy-start | bytes 772
  0.7 44.6 %collective-permute-start.1 = (bf16[64,128,128]{2,1,0:T(8,128)(2,1)}, bf16[64,128,128]{2,1,0:T(8,128)(2,1)}, u32[]{:S(2)}, u32[]{:S(2)}) collective-permute-start(bf16[64,128,128]{2,1,0:T(8,128)(2,1)} %bitcast.8), channel_id=1, source_target_pairs={{0,16},{16,0},{1,17},{17,1},{2,18},{18,2},{3,19},{19,3},{4,20},{20... | collective-permute-start | bytes 6291464 | tf_op jit(solution)/shard_map/ppermute | solution.py:173
  11.6 33.6 %all-to-all-start = ((bf16[32,128,128]{2,1,0:T(8,128)(2,1)}), bf16[32,128,128]{2,1,0:T(8,128)(2,1)S(1)}, u32[]{:S(2)}, u32[]{:S(2)}) async-start(bf16[32,128,128]{2,1,0:T(8,128)(2,1)} %shard_map.130), calls=%async_computation | async-start | bytes 2097152 | tf_op jit(solution)/shard_map/all_to_all | solution.py:177
  16.2 3.1 %collective-permute-start = (s32[3,64]{1,0:T(4,128)S(1)}, s32[3,64]{1,0:T(4,128)S(1)}, u32[]{:S(2)}, u32[]{:S(2)}) collective-permute-start(s32[3,64]{1,0:T(4,128)S(1)} %shard_map.129.places), channel_id=1, source_target_pairs={{0,16},{16,0},{1,17},{17,1},{2,18},{18,2},{3,19},{19,3},{4,20},{20... | collective-permute-start | bytes 2312 | tf_op jit(solution)/shard_map/ppermute | solution.py:173
  48.6 1.0 copy-start.1
  49.6 11.6 %copy-start.3 = (f32[128,256]{1,0:T(8,128)S(1)}, f32[128,256]{1,0:T(8,128)}, u32[]{:S(2)}) copy-start(f32[128,256]{1,0:T(8,128)} %cotangent.3) | copy-start | bytes 393220
  49.6 11.6 %copy-start.15 = (s32[128]{0:T(128)S(1)}, s32[128]{0:T(128)}, u32[]{:S(2)}) copy-start(s32[128]{0:T(128)} %param.13) | copy-start | bytes 1540
  49.6 38.1 %all-to-all-start.1 = ((bf16[32,128,128]{2,1,0:T(8,128)(2,1)}), bf16[32,128,128]{2,1,0:T(8,128)(2,1)S(1)}, u32[]{:S(2)}, u32[]{:S(2)}) async-start(bf16[32,128,128]{2,1,0:T(8,128)(2,1)} %copy-done.1), calls=%async_computation.1 | async-start | bytes 2097152 | tf_op jit(solution)/shard_map/all_to_all | solution.py:177
  61.2 0.9 copy-start.5
  62.1 0.8 copy-start.10
  63.0 24.8 %copy-start.2 = (f32[256,256]{1,0:T(8,128)S(1)}, f32[256,256]{1,0:T(8,128)}, u32[]{:S(2)}) copy-start(f32[256,256]{1,0:T(8,128)} %weight.3) | copy-start | bytes 786436
  63.2 0.7 copy-start.6
  63.9 0.7 copy-start.8
  64.6 0.6 copy-start.11
  65.2 0.6 copy-start.13
  87.7 0.9 copy-start.7
  88.6 0.9 copy-start.9
  126.3 37.0 %copy-start.4 = (f32[128,256]{1,0:T(8,128)S(1)}, f32[128,256]{1,0:T(8,128)}, u32[]{:S(2)}) copy-start(f32[128,256]{1,0:T(8,128)} %get-tuple-element.12.states) | copy-start | bytes 393220
  126.3 37.0 %copy-start.12 = (f32[128,128]{1,0:T(8,128)S(1)}, f32[128,128]{1,0:T(8,128)}, u32[]{:S(2)}) copy-start(f32[128,128]{1,0:T(8,128)} %copy-done.11) | copy-start | bytes 196612
  126.3 37.0 %copy-start.14 = (f32[128,128]{1,0:T(8,128)S(1)}, f32[128,128]{1,0:T(8,128)}, u32[]{:S(2)}) copy-start(f32[128,128]{1,0:T(8,128)} %copy-done.13) | copy-start | bytes 196612

commit v6 on v5

--- a/solution.py
+++ b/solution.py
@@ -15,8 +15,8 @@
 COL = ("xh", "y")
 SIDE = ("core", "xh", "y")
 ROW = ("xl", "z", "core")
-UNROLL = 16
-REST = 4
+UNROLL = 32
+REST = 16
 FIRST_MIB = 56
 VMEM = pl.BlockSpec(memory_space=pltpu.VMEM)
 ANY = pl.BlockSpec(memory_space=pl.ANY)
@@ -45,8 +45,10 @@
 
 
 def pack_kernel(rows, cols, live, out):
-    for q, x in enumerate((rows, cols, live)):
+    for q, x in enumerate((rows, cols)):
         out[q : q + 1, :] = x[...]
+    count = jnp.sum(live[...].astype(F32), axis=1, keepdims=True)
+    out[2:3, :] = jnp.broadcast_to(count, live.shape).astype(jnp.int32)
 
 
 def prep_kernel(shared, values, degrees, features, input_map, cotangent, inv_row, inv_wide, driving, features_t, cotangent_scaled):
@@ -61,12 +63,8 @@
     cotangent_scaled[...] = cotangent[...] * wide[:, :1]
 
 
-def live_count(places):
-    return lax.fori_loop(0, places.shape[1], lambda t, n: n + places[2, t], jnp.int32(0))
-
-
 def add_tiles(places, core, values, forward, blocks, acc):
-    count = live_count(places)
+    count = places[2, 0]
     spare = acc.shape[0] - 1
     start = core * (spare // 2 if not forward else blocks.shape[0] // 2)
 

time: 210 us -> 208 us (level)
  no operation moved by 1% of the time
where the time goes in v6:
time: 208 us; the launch traced here: 207 us
  blocking collectives  112 us (54%)
  waiting for transfers between devices  48.8 us (23%)
  starting transfers between devices  26.7 us (13%)
  Pallas kernels  11.6 us (6%)
  local copies, waits for them, and re-layouts  7.12 us (3%)
    all_to_all x5, blocking collectives, exchange(): return lax.all_to_all(x, axes, 0, 0, tiled=True)  112 us
    all_to_all x2, waiting for transfers between devices, exchange(): return lax.all_to_all(x, axes, 0, 0, tiled=True)  47.9 us
    all_to_all x2, starting transfers between devices, exchange(): return lax.all_to_all(x, axes, 0, 0, tiled=True)  15.7 us
    ppermute x2, starting transfers between devices, swap(): return lax.ppermute(x, 'core', [(0, 1), (1, 0)])  11 us
    unnamed x38, local copies, waits for them, and re-layouts  7.12 us
    pallas_call x2, Pallas kernels, tile_sums(): call(functools.partial(tiles_kernel, forward=forward), shape((count, *dim...  5.82 us
  transfers between devices with their start and end apart: 4, of which 3 were waited for; matrix products, arithmetic and copies ran while one was open for 0% of the time, Pallas kernels for 1%

profile of v6, /device:TPU:1, one launch (start us, length us, event | category | flops | bytes accessed | tf_op | source)
XLA Modules:
  0.0 207.0 jit_solution(7196077818313717951)
XLA Ops:
  0.7 8.9 %collective-permute-start.1 = (bf16[64,128,128]{2,1,0:T(8,128)(2,1)}, bf16[64,128,128]{2,1,0:T(8,128)(2,1)}, u32[]{:S(2)}, u32[]{:S(2)}) collective-permute-start(bf16[64,128,128]{2,1,0:T(8,128)(2,1)} %bitcast.8), channel_id=1, source_target_pairs={{0,16},{16,0},{1,17},{17,1},{2,18},{18,2},{3,19},{19,3},{4,20},{20... | collective-permute-start | bytes 6291464 | tf_op jit(solution)/shard_map/ppermute | solution.py:171
  9.6 2.1 %shard_map.130 = bf16[32,128,128]{2,1,0:T(8,128)(2,1)} custom-call(f32[128,256]{1,0:T(8,128)} %state.1, s32[1,128]{1,0:T(1,128)} %bitcast.14), custom_call_target="tpu_custom_call" | custom-call | flops 100000000 | bytes 2097152 | tf_op jit(solution)/shard_map/pallas_call | solution.py:204
  11.6 4.5 %all-to-all-start = ((bf16[32,128,128]{2,1,0:T(8,128)(2,1)}), bf16[32,128,128]{2,1,0:T(8,128)(2,1)S(1)}, u32[]{:S(2)}, u32[]{:S(2)}) async-start(bf16[32,128,128]{2,1,0:T(8,128)(2,1)} %shard_map.130), calls=%async_computation | async-start | bytes 2097152 | tf_op jit(solution)/shard_map/all_to_all | solution.py:175
  16.3 2.1 %collective-permute-start = (s32[3,64]{1,0:T(4,128)S(1)}, s32[3,64]{1,0:T(4,128)S(1)}, u32[]{:S(2)}, u32[]{:S(2)}) collective-permute-start(s32[3,64]{1,0:T(4,128)S(1)} %shard_map.129.places), channel_id=1, source_target_pairs={{0,16},{16,0},{1,17},{17,1},{2,18},{18,2},{3,19},{19,3},{4,20},{20... | collective-permute-start | bytes 2312 | tf_op jit(solution)/shard_map/ppermute | solution.py:171
  18.4 0.9 collective-permute-done.other_places
  19.3 26.0 %all-to-all-done.blocks = bf16[32,128,128]{2,1,0:T(8,128)(2,1)S(1)} async-done(((bf16[32,128,128]{2,1,0:T(8,128)(2,1)}), bf16[32,128,128]{2,1,0:T(8,128)(2,1)S(1)}, u32[]{:S(2)}, u32[]{:S(2)}) %all-to-all-start) | async-done | bytes 1048608 | tf_op jit(solution)/shard_map/all_to_all | solution.py:175
  45.3 2.9 %shard_map.131 = bf16[32,128,128]{2,1,0:T(8,128)(2,1)S(1)} custom-call(s32[1]{0:T(128)} %bitcast.core_ref, s32[3,64]{1,0:T(4,128)S(1)} %shard_map.129.places, s32[3,64]{1,0:T(4,128)S(1)} %collective-permute-done.other_places, bf16[64,128,128]{2,1,0:T(8,128)(2,1)S(1)} %bitcast.9, bf16[64,128,128]{2,1,0:T(8,128)(2,1)} %collective-permute-done.1.other_values.shared, ...), custom_call_target="tpu_custom_call" | custom-call | flops 536870912 | bytes 2097152 | tf_op jit(solution)/shard_map/pallas_call | solution.py:226
  48.2 1.0 copy-done.1
  49.2 11.2 %all-to-all-start.1 = ((bf16[32,128,128]{2,1,0:T(8,128)(2,1)}), bf16[32,128,128]{2,1,0:T(8,128)(2,1)S(1)}, u32[]{:S(2)}, u32[]{:S(2)}) async-start(bf16[32,128,128]{2,1,0:T(8,128)(2,1)} %copy-done.1), calls=%async_computation.1 | async-start | bytes 2097152 | tf_op jit(solution)/shard_map/all_to_all | solution.py:175
  60.4 0.9 copy-done.5
  61.3 0.8 copy-done.10
  63.1 0.7 copy-done.8
  65.0 21.9 %all-to-all-done.1.parts = bf16[32,128,128]{2,1,0:T(8,128)(2,1)S(1)} async-done(((bf16[32,128,128]{2,1,0:T(8,128)(2,1)}), bf16[32,128,128]{2,1,0:T(8,128)(2,1)S(1)}, u32[]{:S(2)}, u32[]{:S(2)}) %all-to-all-start.1) | async-done | bytes 1048608 | tf_op jit(solution)/shard_map/all_to_all | solution.py:175
  86.9 0.9 copy-done.7
  87.8 0.9 copy-done.9
  88.7 1.2 shard_map.133
  89.9 32.2 %all_to_all.35.blocks = bf16[32,128,128]{2,1,0:T(8,128)(2,1)S(1)} all-to-all(bf16[32,128,128]{2,1,0:T(8,128)(2,1)S(1)} %get-tuple-element.20), channel_id=1, replica_groups=mesh['xl'=2,'z'=8,'core'=2,'xh'=2,'y'=8] {'xl','z','core'}, dimensions={0} | all-to-all | bytes 2097152 | tf_op jit(solution)/shard_map/all_to_all | solution.py:175
  122.1 2.9 %shard_map.134 = bf16[32,128,128]{2,1,0:T(8,128)(2,1)S(1)} custom-call(s32[1]{0:T(128)} %bitcast.core_ref, s32[3,64]{1,0:T(4,128)S(1)} %shard_map.129.places, s32[3,64]{1,0:T(4,128)S(1)} %collective-permute-done.other_places, bf16[64,128,128]{2,1,0:T(8,128)(2,1)S(1)} %bitcast.11, bf16[64,128,128]{2,1,0:T(8,128)(2,1)} %collective-permute-done.1.other_values.shared, ...), custom_call_target="tpu_custom_call" | custom-call | flops 536870912 | bytes 2097152 | tf_op jit(solution)/shard_map/pallas_call | solution.py:226
  125.1 36.6 %all_to_all.36.parts = bf16[32,128,128]{2,1,0:T(8,128)(2,1)S(1)} all-to-all(bf16[32,128,128]{2,1,0:T(8,128)(2,1)S(1)} %shard_map.134), channel_id=1, replica_groups=mesh['xl'=2,'z'=8,'core'=2,'xh'=2,'y'=8] {'core','xh','y'}, dimensions={0} | all-to-all | bytes 2097152 | tf_op jit(solution)/shard_map/all_to_all | solution.py:175
  161.7 1.4 shard_map.135
  163.1 13.7 %all_to_all.37.parts = bf16[32,24,128]{2,1,0:T(8,128)(2,1)S(1)} all-to-all(bf16[32,24,128]{2,1,0:T(8,128)(2,1)S(1)} %bitcast.12), channel_id=1, replica_groups=mesh['xl'=2,'z'=8,'core'=2,'xh'=2,'y'=8] {'xl','z','core'}, dimensions={0} | all-to-all | bytes 393216 | tf_op jit(solution)/shard_map/all_to_all | solution.py:175
  176.9 13.3 %all_to_all.38.parts = bf16[16,24,128]{2,1,0:T(8,128)(2,1)S(1)} all-to-all(bf16[16,24,128]{2,1,0:T(8,128)(2,1)S(1)} %shard_map.136), channel_id=1, replica_groups=mesh['xl'=2,'z'=8,'core'=2,'xh'=2,'y'=8] {'xh','y'}, dimensions={0} | all-to-all | bytes 196608 | tf_op jit(solution)/shard_map/all_to_all | solution.py:175
  190.2 16.1 %all_to_all.39 = bf16[32,24,128]{2,1,0:T(8,128)(2,1)S(1)} all-to-all(bf16[32,24,128]{2,1,0:T(8,128)(2,1)S(1)} %shard_map.137), channel_id=1, replica_groups=mesh['xl'=2,'z'=8,'core'=2,'xh'=2,'y'=8] {'xl','z','core'}, dimensions={0} | all-to-all | bytes 393216 | tf_op jit(solution)/shard_map/all_to_all | solution.py:175
  206.3 0.8 shard_map.138
  (37 shorter events, 2.4 us)
Async XLA Ops:
  0.6 44.6 %copy-start = (bf16[1,1,64,128,128]{4,3,2,1,0:T(8,128)(2,1)S(1)}, bf16[1,1,64,128,128]{4,3,2,1,0:T(8,128)(2,1)}, u32[]{:S(2)}) copy-start(bf16[1,1,64,128,128]{4,3,2,1,0:T(8,128)(2,1)} %param.14) | copy-start | bytes 6291460
  0.6 15.5 %copy-start.18 = (s32[1,1,64]{2,1,0:T(1,128)S(1)}, s32[1,1,64]{2,1,0:T(1,128)}, u32[]{:S(2)}) copy-start(s32[1,1,64]{2,1,0:T(1,128)} %param.17) | copy-start | bytes 772
  0.7 15.5 %copy-start.17 = (s32[1,1,64]{2,1,0:T(1,128)S(1)}, s32[1,1,64]{2,1,0:T(1,128)}, u32[]{:S(2)}) copy-start(s32[1,1,64]{2,1,0:T(1,128)} %param.16) | copy-start | bytes 772
  0.7 15.5 %copy-start.16 = (s32[1,1,64]{2,1,0:T(1,128)S(1)}, s32[1,1,64]{2,1,0:T(1,128)}, u32[]{:S(2)}) copy-start(s32[1,1,64]{2,1,0:T(1,128)} %param.15) | copy-start | bytes 772
  0.7 44.6 %collective-permute-start.1 = (bf16[64,128,128]{2,1,0:T(8,128)(2,1)}, bf16[64,128,128]{2,1,0:T(8,128)(2,1)}, u32[]{:S(2)}, u32[]{:S(2)}) collective-permute-start(bf16[64,128,128]{2,1,0:T(8,128)(2,1)} %bitcast.8), channel_id=1, source_target_pairs={{0,16},{16,0},{1,17},{17,1},{2,18},{18,2},{3,19},{19,3},{4,20},{20... | collective-permute-start | bytes 6291464 | tf_op jit(solution)/shard_map/ppermute | solution.py:171
  11.6 33.6 %all-to-all-start = ((bf16[32,128,128]{2,1,0:T(8,128)(2,1)}), bf16[32,128,128]{2,1,0:T(8,128)(2,1)S(1)}, u32[]{:S(2)}, u32[]{:S(2)}) async-start(bf16[32,128,128]{2,1,0:T(8,128)(2,1)} %shard_map.130), calls=%async_computation | async-start | bytes 2097152 | tf_op jit(solution)/shard_map/all_to_all | solution.py:175
  16.3 3.0 %collective-permute-start = (s32[3,64]{1,0:T(4,128)S(1)}, s32[3,64]{1,0:T(4,128)S(1)}, u32[]{:S(2)}, u32[]{:S(2)}) collective-permute-start(s32[3,64]{1,0:T(4,128)S(1)} %shard_map.129.places), channel_id=1, source_target_pairs={{0,16},{16,0},{1,17},{17,1},{2,18},{18,2},{3,19},{19,3},{4,20},{20... | collective-permute-start | bytes 2312 | tf_op jit(solution)/shard_map/ppermute | solution.py:171
  48.2 1.0 copy-start.1
  49.2 11.2 %copy-start.3 = (f32[128,256]{1,0:T(8,128)S(1)}, f32[128,256]{1,0:T(8,128)}, u32[]{:S(2)}) copy-start(f32[128,256]{1,0:T(8,128)} %cotangent.3) | copy-start | bytes 393220
  49.2 11.2 %copy-start.15 = (s32[128]{0:T(128)S(1)}, s32[128]{0:T(128)}, u32[]{:S(2)}) copy-start(s32[128]{0:T(128)} %param.13) | copy-start | bytes 1540
  49.2 37.7 %all-to-all-start.1 = ((bf16[32,128,128]{2,1,0:T(8,128)(2,1)}), bf16[32,128,128]{2,1,0:T(8,128)(2,1)S(1)}, u32[]{:S(2)}, u32[]{:S(2)}) async-start(bf16[32,128,128]{2,1,0:T(8,128)(2,1)} %copy-done.1), calls=%async_computation.1 | async-start | bytes 2097152 | tf_op jit(solution)/shard_map/all_to_all | solution.py:175
  60.4 0.9 copy-start.5
  61.3 0.8 copy-start.10
  62.2 24.8 %copy-start.2 = (f32[256,256]{1,0:T(8,128)S(1)}, f32[256,256]{1,0:T(8,128)}, u32[]{:S(2)}) copy-start(f32[256,256]{1,0:T(8,128)} %weight.3) | copy-start | bytes 786436
  62.4 0.7 copy-start.6
  63.1 0.7 copy-start.8
  63.7 0.6 copy-start.11
  64.4 0.6 copy-start.13
  86.9 0.9 copy-start.7
  87.8 0.9 copy-start.9
  125.1 36.6 %copy-start.4 = (f32[128,256]{1,0:T(8,128)S(1)}, f32[128,256]{1,0:T(8,128)}, u32[]{:S(2)}) copy-start(f32[128,256]{1,0:T(8,128)} %get-tuple-element.12.states) | copy-start | bytes 393220
  125.1 36.6 %copy-start.12 = (f32[128,128]{1,0:T(8,128)S(1)}, f32[128,128]{1,0:T(8,128)}, u32[]{:S(2)}) copy-start(f32[128,128]{1,0:T(8,128)} %copy-done.11) | copy-start | bytes 196612
  125.1 36.6 %copy-start.14 = (f32[128,128]{1,0:T(8,128)S(1)}, f32[128,128]{1,0:T(8,128)}, u32[]{:S(2)}) copy-start(f32[128,128]{1,0:T(8,128)} %copy-done.13) | copy-start | bytes 196612

commit v7 on v6

--- a/solution.py
+++ b/solution.py
@@ -63,40 +63,55 @@
     cotangent_scaled[...] = cotangent[...] * wide[:, :1]
 
 
-def add_tiles(places, core, values, forward, blocks, acc):
-    count = places[2, 0]
+def add_group(size, begin, places, start, count, values, forward, blocks, acc):
     spare = acc.shape[0] - 1
-    start = core * (spare // 2 if not forward else blocks.shape[0] // 2)
-
-    def group(size, begin, g, carry):
-        products, slots = [], []
-        for u in range(size):
-            t = begin + g * size + u
-            row, col = start + places[0, t], places[1, t]
-            if forward:
-                product = jnp.dot(blocks[row], values[t], preferred_element_type=F32)
-            else:
-                product = jnp.dot(values[t], blocks[col], preferred_element_type=F32)
-            products.append(product)
-            slots.append(jnp.where(t < count, col if forward else row, spare))
-        for slot, product in zip(slots, products):
-            acc[slot] += product
+    products, slots = [], []
+    for u in range(size):
+        t = begin + u
+        row, col = start + places[0, t], places[1, t]
+        if forward:
+            product = jnp.dot(blocks[row], values[t], preferred_element_type=F32)
+        else:
+            product = jnp.dot(values[t], blocks[col], preferred_element_type=F32)
+        products.append(product)
+        slots.append(jnp.where(t < count, col if forward else row, spare))
+    for slot, product in zip(slots, products):
+        acc[slot] += product
+
+
+def tiles_kernel(core_ref, places, other_places, values, other_values, blocks, out, acc, held, sems, *, forward):
+    core = core_ref[0]
+    mine, theirs = places[2, 0], other_places[2, 0]
+    step = blocks.shape[0] // 2 if forward else out.shape[0] // 2
+    pieces = held.shape[0] // REST
+    copies = []
+    for j in range(pieces):
+        part = pl.ds(j * REST, REST)
+        copies.append(pltpu.make_async_copy(other_values.at[part], held.at[part], sems.at[j]))
+
+        @pl.when(theirs > j * REST)
+        def _(j=j):
+            copies[j].start()
+
+    acc[...] = jnp.zeros_like(acc)
+
+    def own(size, first, g, carry):
+        add_group(size, first + g * size, places, core * step, mine, values, forward, blocks, acc)
         return carry
 
-    full = count // UNROLL
+    full = mine // UNROLL
     done = full * UNROLL
-    lax.fori_loop(0, full, functools.partial(group, UNROLL, 0), 0)
-    lax.fori_loop(0, (count - done + REST - 1) // REST, functools.partial(group, REST, done), 0)
-
-
-def tiles_kernel(core_ref, places, other_places, values, other_values, blocks, out, acc, held, sem, *, forward):
-    core = core_ref[0]
-    copy = pltpu.make_async_copy(other_values, held, sem)
-    copy.start()
-    acc[...] = jnp.zeros_like(acc)
-    add_tiles(places, core, values, forward, blocks, acc)
-    copy.wait()
-    add_tiles(other_places, 1 - core, held, forward, blocks, acc)
+    lax.fori_loop(0, full, functools.partial(own, UNROLL, 0), 0)
+    lax.fori_loop(0, (mine - done + REST - 1) // REST, functools.partial(own, REST, done), 0)
+    for j in range(pieces):
+
+        @pl.when(theirs > j * REST)
+        def _(j=j):
+            copies[j].wait()
+            add_group(
+                REST, j * REST, other_places, (1 - core) * step, theirs, held, forward, blocks, acc
+            )
+
     out[...] = acc[0 : out.shape[0]].astype(BF16)
 
 
@@ -195,7 +210,7 @@
     sides = 2 * col_devices
     core = lax.axis_index("core").astype(jnp.int32).reshape(1)
     degree_row = degrees.reshape(1, nodes)
-    block = values.shape[1]
+    slots, block = values.shape[:2]
     size = width // 2
     places = call(
         pack_kernel, shape((3, values.shape[0]), jnp.int32), [VMEM] * 3, mib=4
@@ -230,7 +245,7 @@
             [
                 pltpu.VMEM((count + 1, *dims), F32),
                 pltpu.VMEM(values.shape, BF16),
-                pltpu.SemaphoreType.DMA,
+                pltpu.SemaphoreType.DMA((slots // REST,)),
             ],
             mib=16,
             flops=4 * values.shape[0] * block * block * size,

time: 208 us -> 207 us (level)
  no operation moved by 1% of the time
where the time goes in v7:
time: 207 us; the launch traced here: 206 us
  blocking collectives  112 us (54%)
  waiting for transfers between devices  48.8 us (24%)
  starting transfers between devices  26.8 us (13%)
  Pallas kernels  10.6 us (5%)
  local copies, waits for them, and re-layouts  7.12 us (3%)
    all_to_all x5, blocking collectives, exchange(): return lax.all_to_all(x, axes, 0, 0, tiled=True)  112 us
    all_to_all x2, waiting for transfers between devices, exchange(): return lax.all_to_all(x, axes, 0, 0, tiled=True)  47.9 us
    all_to_all x2, starting transfers between devices, exchange(): return lax.all_to_all(x, axes, 0, 0, tiled=True)  15.8 us
    ppermute x2, starting transfers between devices, swap(): return lax.ppermute(x, 'core', [(0, 1), (1, 0)])  11 us
    unnamed x38, local copies, waits for them, and re-layouts  7.12 us
    pallas_call x2, Pallas kernels, tile_sums(): call(functools.partial(tiles_kernel, forward=forward), shape((count, *dim...  4.8 us
  transfers between devices with their start and end apart: 4, of which 3 were waited for; matrix products, arithmetic and copies ran while one was open for 0% of the time, Pallas kernels for 1%

profile of v7, /device:TPU:1, one launch (start us, length us, event | category | flops | bytes accessed | tf_op | source)
XLA Modules:
  0.0 206.2 jit_solution(10795601257785349640)
XLA Ops:
  0.7 8.9 %collective-permute-start.1 = (bf16[64,128,128]{2,1,0:T(8,128)(2,1)}, bf16[64,128,128]{2,1,0:T(8,128)(2,1)}, u32[]{:S(2)}, u32[]{:S(2)}) collective-permute-start(bf16[64,128,128]{2,1,0:T(8,128)(2,1)} %bitcast.8), channel_id=1, source_target_pairs={{0,16},{16,0},{1,17},{17,1},{2,18},{18,2},{3,19},{19,3},{4,20},{20... | collective-permute-start | bytes 6291464 | tf_op jit(solution)/shard_map/ppermute | solution.py:186
  9.6 2.1 %shard_map.130 = bf16[32,128,128]{2,1,0:T(8,128)(2,1)} custom-call(f32[128,256]{1,0:T(8,128)} %state.1, s32[1,128]{1,0:T(1,128)} %bitcast.14), custom_call_target="tpu_custom_call" | custom-call | flops 100000000 | bytes 2097152 | tf_op jit(solution)/shard_map/pallas_call | solution.py:219
  11.6 4.5 %all-to-all-start = ((bf16[32,128,128]{2,1,0:T(8,128)(2,1)}), bf16[32,128,128]{2,1,0:T(8,128)(2,1)S(1)}, u32[]{:S(2)}, u32[]{:S(2)}) async-start(bf16[32,128,128]{2,1,0:T(8,128)(2,1)} %shard_map.130), calls=%async_computation | async-start | bytes 2097152 | tf_op jit(solution)/shard_map/all_to_all | solution.py:190
  16.3 2.1 %collective-permute-start = (s32[3,64]{1,0:T(4,128)S(1)}, s32[3,64]{1,0:T(4,128)S(1)}, u32[]{:S(2)}, u32[]{:S(2)}) collective-permute-start(s32[3,64]{1,0:T(4,128)S(1)} %shard_map.129.places), channel_id=1, source_target_pairs={{0,16},{16,0},{1,17},{17,1},{2,18},{18,2},{3,19},{19,3},{4,20},{20... | collective-permute-start | bytes 2312 | tf_op jit(solution)/shard_map/ppermute | solution.py:186
  18.4 0.9 collective-permute-done.other_places
  19.3 26.0 %all-to-all-done.blocks = bf16[32,128,128]{2,1,0:T(8,128)(2,1)S(1)} async-done(((bf16[32,128,128]{2,1,0:T(8,128)(2,1)}), bf16[32,128,128]{2,1,0:T(8,128)(2,1)S(1)}, u32[]{:S(2)}, u32[]{:S(2)}) %all-to-all-start) | async-done | bytes 1048608 | tf_op jit(solution)/shard_map/all_to_all | solution.py:190
  45.3 2.4 %shard_map.131 = bf16[32,128,128]{2,1,0:T(8,128)(2,1)S(1)} custom-call(s32[1]{0:T(128)} %bitcast.core_ref, s32[3,64]{1,0:T(4,128)S(1)} %shard_map.129.places, s32[3,64]{1,0:T(4,128)S(1)} %collective-permute-done.other_places, bf16[64,128,128]{2,1,0:T(8,128)(2,1)S(1)} %bitcast.9, bf16[64,128,128]{2,1,0:T(8,128)(2,1)} %collective-permute-done.1.other_values.shared, ...), custom_call_target="tpu_custom_call" | custom-call | flops 536870912 | bytes 2097152 | tf_op jit(solution)/shard_map/pallas_call | solution.py:241
  47.7 1.0 copy-done.1
  48.7 11.3 %all-to-all-start.1 = ((bf16[32,128,128]{2,1,0:T(8,128)(2,1)}), bf16[32,128,128]{2,1,0:T(8,128)(2,1)S(1)}, u32[]{:S(2)}, u32[]{:S(2)}) async-start(bf16[32,128,128]{2,1,0:T(8,128)(2,1)} %copy-done.1), calls=%async_computation.1 | async-start | bytes 2097152 | tf_op jit(solution)/shard_map/all_to_all | solution.py:190
  60.0 0.9 copy-done.5
  60.9 0.8 copy-done.10
  62.7 0.7 copy-done.8
  64.6 21.9 %all-to-all-done.1.parts = bf16[32,128,128]{2,1,0:T(8,128)(2,1)S(1)} async-done(((bf16[32,128,128]{2,1,0:T(8,128)(2,1)}), bf16[32,128,128]{2,1,0:T(8,128)(2,1)S(1)}, u32[]{:S(2)}, u32[]{:S(2)}) %all-to-all-start.1) | async-done | bytes 1048608 | tf_op jit(solution)/shard_map/all_to_all | solution.py:190
  86.5 0.9 copy-done.7
  87.4 0.9 copy-done.9
  88.3 1.2 shard_map.133
  89.5 32.2 %all_to_all.35.blocks = bf16[32,128,128]{2,1,0:T(8,128)(2,1)S(1)} all-to-all(bf16[32,128,128]{2,1,0:T(8,128)(2,1)S(1)} %get-tuple-element.20), channel_id=1, replica_groups=mesh['xl'=2,'z'=8,'core'=2,'xh'=2,'y'=8] {'xl','z','core'}, dimensions={0} | all-to-all | bytes 2097152 | tf_op jit(solution)/shard_map/all_to_all | solution.py:190
  121.8 2.4 %shard_map.134 = bf16[32,128,128]{2,1,0:T(8,128)(2,1)S(1)} custom-call(s32[1]{0:T(128)} %bitcast.core_ref, s32[3,64]{1,0:T(4,128)S(1)} %shard_map.129.places, s32[3,64]{1,0:T(4,128)S(1)} %collective-permute-done.other_places, bf16[64,128,128]{2,1,0:T(8,128)(2,1)S(1)} %bitcast.11, bf16[64,128,128]{2,1,0:T(8,128)(2,1)} %collective-permute-done.1.other_values.shared, ...), custom_call_target="tpu_custom_call" | custom-call | flops 536870912 | bytes 2097152 | tf_op jit(solution)/shard_map/pallas_call | solution.py:241
  124.2 36.6 %all_to_all.36.parts = bf16[32,128,128]{2,1,0:T(8,128)(2,1)S(1)} all-to-all(bf16[32,128,128]{2,1,0:T(8,128)(2,1)S(1)} %shard_map.134), channel_id=1, replica_groups=mesh['xl'=2,'z'=8,'core'=2,'xh'=2,'y'=8] {'core','xh','y'}, dimensions={0} | all-to-all | bytes 2097152 | tf_op jit(solution)/shard_map/all_to_all | solution.py:190
  160.8 1.4 shard_map.135
  162.1 13.7 %all_to_all.37.parts = bf16[32,24,128]{2,1,0:T(8,128)(2,1)S(1)} all-to-all(bf16[32,24,128]{2,1,0:T(8,128)(2,1)S(1)} %bitcast.12), channel_id=1, replica_groups=mesh['xl'=2,'z'=8,'core'=2,'xh'=2,'y'=8] {'xl','z','core'}, dimensions={0} | all-to-all | bytes 393216 | tf_op jit(solution)/shard_map/all_to_all | solution.py:190
  175.9 13.4 %all_to_all.38.parts = bf16[16,24,128]{2,1,0:T(8,128)(2,1)S(1)} all-to-all(bf16[16,24,128]{2,1,0:T(8,128)(2,1)S(1)} %shard_map.136), channel_id=1, replica_groups=mesh['xl'=2,'z'=8,'core'=2,'xh'=2,'y'=8] {'xh','y'}, dimensions={0} | all-to-all | bytes 196608 | tf_op jit(solution)/shard_map/all_to_all | solution.py:190
  189.4 16.1 %all_to_all.39 = bf16[32,24,128]{2,1,0:T(8,128)(2,1)S(1)} all-to-all(bf16[32,24,128]{2,1,0:T(8,128)(2,1)S(1)} %shard_map.137), channel_id=1, replica_groups=mesh['xl'=2,'z'=8,'core'=2,'xh'=2,'y'=8] {'xl','z','core'}, dimensions={0} | all-to-all | bytes 393216 | tf_op jit(solution)/shard_map/all_to_all | solution.py:190
  205.5 0.8 shard_map.138
  (37 shorter events, 2.4 us)
Async XLA Ops:
  0.6 44.6 %copy-start = (bf16[1,1,64,128,128]{4,3,2,1,0:T(8,128)(2,1)S(1)}, bf16[1,1,64,128,128]{4,3,2,1,0:T(8,128)(2,1)}, u32[]{:S(2)}) copy-start(bf16[1,1,64,128,128]{4,3,2,1,0:T(8,128)(2,1)} %param.14) | copy-start | bytes 6291460
  0.6 15.5 %copy-start.18 = (s32[1,1,64]{2,1,0:T(1,128)S(1)}, s32[1,1,64]{2,1,0:T(1,128)}, u32[]{:S(2)}) copy-start(s32[1,1,64]{2,1,0:T(1,128)} %param.17) | copy-start | bytes 772
  0.7 15.5 %copy-start.17 = (s32[1,1,64]{2,1,0:T(1,128)S(1)}, s32[1,1,64]{2,1,0:T(1,128)}, u32[]{:S(2)}) copy-start(s32[1,1,64]{2,1,0:T(1,128)} %param.16) | copy-start | bytes 772
  0.7 15.5 %copy-start.16 = (s32[1,1,64]{2,1,0:T(1,128)S(1)}, s32[1,1,64]{2,1,0:T(1,128)}, u32[]{:S(2)}) copy-start(s32[1,1,64]{2,1,0:T(1,128)} %param.15) | copy-start | bytes 772
  0.7 44.6 %collective-permute-start.1 = (bf16[64,128,128]{2,1,0:T(8,128)(2,1)}, bf16[64,128,128]{2,1,0:T(8,128)(2,1)}, u32[]{:S(2)}, u32[]{:S(2)}) collective-permute-start(bf16[64,128,128]{2,1,0:T(8,128)(2,1)} %bitcast.8), channel_id=1, source_target_pairs={{0,16},{16,0},{1,17},{17,1},{2,18},{18,2},{3,19},{19,3},{4,20},{20... | collective-permute-start | bytes 6291464 | tf_op jit(solution)/shard_map/ppermute | solution.py:186
  11.6 33.6 %all-to-all-start = ((bf16[32,128,128]{2,1,0:T(8,128)(2,1)}), bf16[32,128,128]{2,1,0:T(8,128)(2,1)S(1)}, u32[]{:S(2)}, u32[]{:S(2)}) async-start(bf16[32,128,128]{2,1,0:T(8,128)(2,1)} %shard_map.130), calls=%async_computation | async-start | bytes 2097152 | tf_op jit(solution)/shard_map/all_to_all | solution.py:190
  16.3 3.0 %collective-permute-start = (s32[3,64]{1,0:T(4,128)S(1)}, s32[3,64]{1,0:T(4,128)S(1)}, u32[]{:S(2)}, u32[]{:S(2)}) collective-permute-start(s32[3,64]{1,0:T(4,128)S(1)} %shard_map.129.places), channel_id=1, source_target_pairs={{0,16},{16,0},{1,17},{17,1},{2,18},{18,2},{3,19},{19,3},{4,20},{20... | collective-permute-start | bytes 2312 | tf_op jit(solution)/shard_map/ppermute | solution.py:186
  47.7 1.0 copy-start.1
  48.7 11.3 %copy-start.3 = (f32[128,256]{1,0:T(8,128)S(1)}, f32[128,256]{1,0:T(8,128)}, u32[]{:S(2)}) copy-start(f32[128,256]{1,0:T(8,128)} %cotangent.3) | copy-start | bytes 393220
  48.7 11.3 %copy-start.15 = (s32[128]{0:T(128)S(1)}, s32[128]{0:T(128)}, u32[]{:S(2)}) copy-start(s32[128]{0:T(128)} %param.13) | copy-start | bytes 1540
  48.7 37.8 %all-to-all-start.1 = ((bf16[32,128,128]{2,1,0:T(8,128)(2,1)}), bf16[32,128,128]{2,1,0:T(8,128)(2,1)S(1)}, u32[]{:S(2)}, u32[]{:S(2)}) async-start(bf16[32,128,128]{2,1,0:T(8,128)(2,1)} %copy-done.1), calls=%async_computation.1 | async-start | bytes 2097152 | tf_op jit(solution)/shard_map/all_to_all | solution.py:190
  60.0 0.9 copy-start.5
  60.9 0.8 copy-start.10
  61.8 24.8 %copy-start.2 = (f32[256,256]{1,0:T(8,128)S(1)}, f32[256,256]{1,0:T(8,128)}, u32[]{:S(2)}) copy-start(f32[256,256]{1,0:T(8,128)} %weight.3) | copy-start | bytes 786436
  62.0 0.7 copy-start.6
  62.7 0.7 copy-start.8
  63.3 0.6 copy-start.11
  64.0 0.6 copy-start.13
  86.5 0.9 copy-start.7
  87.4 0.9 copy-start.9
  124.1 36.6 %copy-start.4 = (f32[128,256]{1,0:T(8,128)S(1)}, f32[128,256]{1,0:T(8,128)}, u32[]{:S(2)}) copy-start(f32[128,256]{1,0:T(8,128)} %get-tuple-element.12.states) | copy-start | bytes 393220
  124.2 36.6 %copy-start.12 = (f32[128,128]{1,0:T(8,128)S(1)}, f32[128,128]{1,0:T(8,128)}, u32[]{:S(2)}) copy-start(f32[128,128]{1,0:T(8,128)} %copy-done.11) | copy-start | bytes 196612
  124.2 36.6 %copy-start.14 = (f32[128,128]{1,0:T(8,128)S(1)}, f32[128,128]{1,0:T(8,128)}, u32[]{:S(2)}) copy-start(f32[128,128]{1,0:T(8,128)} %copy-done.13) | copy-start | bytes 196612

commit v8 on v7

--- a/solution.py
+++ b/solution.py
@@ -13,7 +13,7 @@
 BF16 = jnp.bfloat16
 F32 = jnp.float32
 COL = ("xh", "y")
-SIDE = ("core", "xh", "y")
+SIDE = ("xh", "y", "core")
 ROW = ("xl", "z", "core")
 UNROLL = 32
 REST = 16
@@ -37,11 +37,9 @@
 def first_kernel(state, degrees, out):
     inverse = lax.rsqrt(degrees[...].astype(F32))
     scaled = (jnp.transpose(state[...]) * inverse).astype(BF16)
-    half = out.shape[0] // 2
     size = out.shape[1]
-    for q in range(half):
-        out[q] = scaled[:size, :]
-        out[half + q] = scaled[size:, :]
+    for q in range(out.shape[0]):
+        out[q] = scaled[(q % 2) * size : (q % 2 + 1) * size, :]
 
 
 def pack_kernel(rows, cols, live, out):
@@ -63,12 +61,12 @@
     cotangent_scaled[...] = cotangent[...] * wide[:, :1]
 
 
-def add_group(size, begin, places, start, count, values, forward, blocks, acc):
+def add_group(size, begin, places, side, count, values, forward, blocks, acc):
     spare = acc.shape[0] - 1
     products, slots = [], []
     for u in range(size):
         t = begin + u
-        row, col = start + places[0, t], places[1, t]
+        row, col = 2 * places[0, t] + side, places[1, t]
         if forward:
             product = jnp.dot(blocks[row], values[t], preferred_element_type=F32)
         else:
@@ -82,7 +80,6 @@
 def tiles_kernel(core_ref, places, other_places, values, other_values, blocks, out, acc, held, sems, *, forward):
     core = core_ref[0]
     mine, theirs = places[2, 0], other_places[2, 0]
-    step = blocks.shape[0] // 2 if forward else out.shape[0] // 2
     pieces = held.shape[0] // REST
     copies = []
     for j in range(pieces):
@@ -96,7 +93,7 @@
     acc[...] = jnp.zeros_like(acc)
 
     def own(size, first, g, carry):
-        add_group(size, first + g * size, places, core * step, mine, values, forward, blocks, acc)
+        add_group(size, first + g * size, places, core, mine, values, forward, blocks, acc)
         return carry
 
     full = mine // UNROLL
@@ -109,7 +106,7 @@
         def _(j=j):
             copies[j].wait()
             add_group(
-                REST, j * REST, other_places, (1 - core) * step, theirs, held, forward, blocks, acc
+                REST, j * REST, other_places, 1 - core, theirs, held, forward, blocks, acc
             )
 
     out[...] = acc[0 : out.shape[0]].astype(BF16)
@@ -132,10 +129,7 @@
 def grad_kernel(
     parts, inv_wide, cotangent, weight, states, summed_t, features_t, adjoint, out, *, factor
 ):
-    middle = parts.shape[0] // 2
-    total = jnp.concatenate(
-        [summed_up(parts.at[pl.ds(0, middle)]), summed_up(parts.at[pl.ds(middle, middle)])], axis=1
-    )
+    total = jnp.concatenate([summed_up(parts, 0, 2), summed_up(parts, 1, 2)], axis=1)
     pulled = total * inv_wide[:, :1]
     moved = lax.dot_general(
         pulled, weight[...], (((1,), (1,)), ((), ())), precision=HIGH, preferred_element_type=F32

time: 207 us -> 207 us (level)
  starting transfers between devices: 26.8 us -> 29.3 us
    all_to_all x2, starting transfers between devices: 15.8 us -> 18.3 us  [exchange(): return lax.all_to_all(x, axes, 0, 0, tiled=True)]
where the time goes in v8:
time: 207 us; the launch traced here: 206 us
  blocking collectives  112 us (54%)
  waiting for transfers between devices  47 us (23%)
  starting transfers between devices  29.3 us (14%)
  Pallas kernels  10.6 us (5%)
  local copies, waits for them, and re-layouts  7.12 us (3%)
    all_to_all x5, blocking collectives, exchange(): return lax.all_to_all(x, axes, 0, 0, tiled=True)  112 us
    all_to_all x2, waiting for transfers between devices, exchange(): return lax.all_to_all(x, axes, 0, 0, tiled=True)  46.1 us
    all_to_all x2, starting transfers between devices, exchange(): return lax.all_to_all(x, axes, 0, 0, tiled=True)  18.3 us
    ppermute x2, starting transfers between devices, swap(): return lax.ppermute(x, 'core', [(0, 1), (1, 0)])  11 us
    unnamed x38, local copies, waits for them, and re-layouts  7.12 us
    pallas_call x2, Pallas kernels, tile_sums(): call(functools.partial(tiles_kernel, forward=forward), shape((count, *dim...  4.8 us
  transfers between devices with their start and end apart: 4, of which 3 were waited for; matrix products, arithmetic and copies ran while one was open for 0% of the time, Pallas kernels for 1%

profile of v8, /device:TPU:1, one launch (start us, length us, event | category | flops | bytes accessed | tf_op | source)
XLA Modules:
  0.0 206.4 jit_solution(11682587983102047160)
XLA Ops:
  0.7 8.9 %collective-permute-start.1 = (bf16[64,128,128]{2,1,0:T(8,128)(2,1)}, bf16[64,128,128]{2,1,0:T(8,128)(2,1)}, u32[]{:S(2)}, u32[]{:S(2)}) collective-permute-start(bf16[64,128,128]{2,1,0:T(8,128)(2,1)} %bitcast.8), channel_id=1, source_target_pairs={{0,16},{16,0},{1,17},{17,1},{2,18},{18,2},{3,19},{19,3},{4,20},{20... | collective-permute-start | bytes 6291464 | tf_op jit(solution)/shard_map/ppermute | solution.py:180
  9.6 2.1 %shard_map.130 = bf16[32,128,128]{2,1,0:T(8,128)(2,1)} custom-call(f32[128,256]{1,0:T(8,128)} %state.1, s32[1,128]{1,0:T(1,128)} %bitcast.14), custom_call_target="tpu_custom_call" | custom-call | flops 100000000 | bytes 2097152 | tf_op jit(solution)/shard_map/pallas_call | solution.py:213
  11.6 4.5 %all-to-all-start = ((bf16[32,128,128]{2,1,0:T(8,128)(2,1)}), bf16[32,128,128]{2,1,0:T(8,128)(2,1)S(1)}, u32[]{:S(2)}, u32[]{:S(2)}) async-start(bf16[32,128,128]{2,1,0:T(8,128)(2,1)} %shard_map.130), calls=%async_computation | async-start | bytes 2097152 | tf_op jit(solution)/shard_map/all_to_all | solution.py:184
  16.2 2.1 %collective-permute-start = (s32[3,64]{1,0:T(4,128)S(1)}, s32[3,64]{1,0:T(4,128)S(1)}, u32[]{:S(2)}, u32[]{:S(2)}) collective-permute-start(s32[3,64]{1,0:T(4,128)S(1)} %shard_map.129.places), channel_id=1, source_target_pairs={{0,16},{16,0},{1,17},{17,1},{2,18},{18,2},{3,19},{19,3},{4,20},{20... | collective-permute-start | bytes 2312 | tf_op jit(solution)/shard_map/ppermute | solution.py:180
  18.4 0.9 collective-permute-done.other_places
  19.3 24.2 %all-to-all-done.blocks = bf16[32,128,128]{2,1,0:T(8,128)(2,1)S(1)} async-done(((bf16[32,128,128]{2,1,0:T(8,128)(2,1)}), bf16[32,128,128]{2,1,0:T(8,128)(2,1)S(1)}, u32[]{:S(2)}, u32[]{:S(2)}) %all-to-all-start) | async-done | bytes 1048608 | tf_op jit(solution)/shard_map/all_to_all | solution.py:184
  43.5 2.4 %shard_map.131 = bf16[32,128,128]{2,1,0:T(8,128)(2,1)S(1)} custom-call(s32[1]{0:T(128)} %bitcast.core_ref, s32[3,64]{1,0:T(4,128)S(1)} %shard_map.129.places, s32[3,64]{1,0:T(4,128)S(1)} %collective-permute-done.other_places, bf16[64,128,128]{2,1,0:T(8,128)(2,1)S(1)} %bitcast.9, bf16[64,128,128]{2,1,0:T(8,128)(2,1)} %collective-permute-done.1.other_values.shared, ...), custom_call_target="tpu_custom_call" | custom-call | flops 536870912 | bytes 2097152 | tf_op jit(solution)/shard_map/pallas_call | solution.py:235
  45.9 1.0 copy-done.1
  46.9 13.8 %all-to-all-start.1 = ((bf16[32,128,128]{2,1,0:T(8,128)(2,1)}), bf16[32,128,128]{2,1,0:T(8,128)(2,1)S(1)}, u32[]{:S(2)}, u32[]{:S(2)}) async-start(bf16[32,128,128]{2,1,0:T(8,128)(2,1)} %copy-done.1), calls=%async_computation.1 | async-start | bytes 2097152 | tf_op jit(solution)/shard_map/all_to_all | solution.py:184
  60.7 0.9 copy-done.5
  61.6 0.8 copy-done.10
  63.4 0.7 copy-done.8
  65.3 21.9 %all-to-all-done.1.parts = bf16[32,128,128]{2,1,0:T(8,128)(2,1)S(1)} async-done(((bf16[32,128,128]{2,1,0:T(8,128)(2,1)}), bf16[32,128,128]{2,1,0:T(8,128)(2,1)S(1)}, u32[]{:S(2)}, u32[]{:S(2)}) %all-to-all-start.1) | async-done | bytes 1048608 | tf_op jit(solution)/shard_map/all_to_all | solution.py:184
  87.2 0.9 copy-done.7
  88.1 0.9 copy-done.9
  89.0 1.2 shard_map.133
  90.2 32.2 %all_to_all.35.blocks = bf16[32,128,128]{2,1,0:T(8,128)(2,1)S(1)} all-to-all(bf16[32,128,128]{2,1,0:T(8,128)(2,1)S(1)} %get-tuple-element.20), channel_id=1, replica_groups=mesh['xl'=2,'z'=8,'core'=2,'xh'=2,'y'=8] {'xl','z','core'}, dimensions={0} | all-to-all | bytes 2097152 | tf_op jit(solution)/shard_map/all_to_all | solution.py:184
  122.4 2.4 %shard_map.134 = bf16[32,128,128]{2,1,0:T(8,128)(2,1)S(1)} custom-call(s32[1]{0:T(128)} %bitcast.core_ref, s32[3,64]{1,0:T(4,128)S(1)} %shard_map.129.places, s32[3,64]{1,0:T(4,128)S(1)} %collective-permute-done.other_places, bf16[64,128,128]{2,1,0:T(8,128)(2,1)S(1)} %bitcast.11, bf16[64,128,128]{2,1,0:T(8,128)(2,1)} %collective-permute-done.1.other_values.shared, ...), custom_call_target="tpu_custom_call" | custom-call | flops 536870912 | bytes 2097152 | tf_op jit(solution)/shard_map/pallas_call | solution.py:235
  124.9 34.0 %all_to_all.36.parts = bf16[32,128,128]{2,1,0:T(8,128)(2,1)S(1)} all-to-all(bf16[32,128,128]{2,1,0:T(8,128)(2,1)S(1)} %shard_map.134), channel_id=1, replica_groups=mesh['xl'=2,'z'=8,'core'=2,'xh'=2,'y'=8] {'xh','y','core'}, dimensions={0} | all-to-all | bytes 2097152 | tf_op jit(solution)/shard_map/all_to_all | solution.py:184
  158.9 1.4 shard_map.135
  160.3 16.8 %all_to_all.37.parts = bf16[32,24,128]{2,1,0:T(8,128)(2,1)S(1)} all-to-all(bf16[32,24,128]{2,1,0:T(8,128)(2,1)S(1)} %bitcast.12), channel_id=1, replica_groups=mesh['xl'=2,'z'=8,'core'=2,'xh'=2,'y'=8] {'xl','z','core'}, dimensions={0} | all-to-all | bytes 393216 | tf_op jit(solution)/shard_map/all_to_all | solution.py:184
  177.1 12.4 %all_to_all.38.parts = bf16[16,24,128]{2,1,0:T(8,128)(2,1)S(1)} all-to-all(bf16[16,24,128]{2,1,0:T(8,128)(2,1)S(1)} %shard_map.136), channel_id=1, replica_groups=mesh['xl'=2,'z'=8,'core'=2,'xh'=2,'y'=8] {'xh','y'}, dimensions={0} | all-to-all | bytes 196608 | tf_op jit(solution)/shard_map/all_to_all | solution.py:184
  189.5 16.1 %all_to_all.39 = bf16[32,24,128]{2,1,0:T(8,128)(2,1)S(1)} all-to-all(bf16[32,24,128]{2,1,0:T(8,128)(2,1)S(1)} %shard_map.137), channel_id=1, replica_groups=mesh['xl'=2,'z'=8,'core'=2,'xh'=2,'y'=8] {'xl','z','core'}, dimensions={0} | all-to-all | bytes 393216 | tf_op jit(solution)/shard_map/all_to_all | solution.py:184
  205.7 0.8 shard_map.138
  (37 shorter events, 2.4 us)
Async XLA Ops:
  0.6 42.9 %copy-start = (bf16[1,1,64,128,128]{4,3,2,1,0:T(8,128)(2,1)S(1)}, bf16[1,1,64,128,128]{4,3,2,1,0:T(8,128)(2,1)}, u32[]{:S(2)}) copy-start(bf16[1,1,64,128,128]{4,3,2,1,0:T(8,128)(2,1)} %param.14) | copy-start | bytes 6291460
  0.6 15.5 %copy-start.18 = (s32[1,1,64]{2,1,0:T(1,128)S(1)}, s32[1,1,64]{2,1,0:T(1,128)}, u32[]{:S(2)}) copy-start(s32[1,1,64]{2,1,0:T(1,128)} %param.17) | copy-start | bytes 772
  0.7 15.5 %copy-start.17 = (s32[1,1,64]{2,1,0:T(1,128)S(1)}, s32[1,1,64]{2,1,0:T(1,128)}, u32[]{:S(2)}) copy-start(s32[1,1,64]{2,1,0:T(1,128)} %param.16) | copy-start | bytes 772
  0.7 15.5 %copy-start.16 = (s32[1,1,64]{2,1,0:T(1,128)S(1)}, s32[1,1,64]{2,1,0:T(1,128)}, u32[]{:S(2)}) copy-start(s32[1,1,64]{2,1,0:T(1,128)} %param.15) | copy-start | bytes 772
  0.7 42.8 %collective-permute-start.1 = (bf16[64,128,128]{2,1,0:T(8,128)(2,1)}, bf16[64,128,128]{2,1,0:T(8,128)(2,1)}, u32[]{:S(2)}, u32[]{:S(2)}) collective-permute-start(bf16[64,128,128]{2,1,0:T(8,128)(2,1)} %bitcast.8), channel_id=1, source_target_pairs={{0,16},{16,0},{1,17},{17,1},{2,18},{18,2},{3,19},{19,3},{4,20},{20... | collective-permute-start | bytes 6291464 | tf_op jit(solution)/shard_map/ppermute | solution.py:180
  11.6 31.9 %all-to-all-start = ((bf16[32,128,128]{2,1,0:T(8,128)(2,1)}), bf16[32,128,128]{2,1,0:T(8,128)(2,1)S(1)}, u32[]{:S(2)}, u32[]{:S(2)}) async-start(bf16[32,128,128]{2,1,0:T(8,128)(2,1)} %shard_map.130), calls=%async_computation | async-start | bytes 2097152 | tf_op jit(solution)/shard_map/all_to_all | solution.py:184
  16.2 3.0 %collective-permute-start = (s32[3,64]{1,0:T(4,128)S(1)}, s32[3,64]{1,0:T(4,128)S(1)}, u32[]{:S(2)}, u32[]{:S(2)}) collective-permute-start(s32[3,64]{1,0:T(4,128)S(1)} %shard_map.129.places), channel_id=1, source_target_pairs={{0,16},{16,0},{1,17},{17,1},{2,18},{18,2},{3,19},{19,3},{4,20},{20... | collective-permute-start | bytes 2312 | tf_op jit(solution)/shard_map/ppermute | solution.py:180
  45.9 1.0 copy-start.1
  46.9 13.8 %copy-start.3 = (f32[128,256]{1,0:T(8,128)S(1)}, f32[128,256]{1,0:T(8,128)}, u32[]{:S(2)}) copy-start(f32[128,256]{1,0:T(8,128)} %cotangent.3) | copy-start | bytes 393220
  46.9 13.8 %copy-start.15 = (s32[128]{0:T(128)S(1)}, s32[128]{0:T(128)}, u32[]{:S(2)}) copy-start(s32[128]{0:T(128)} %param.13) | copy-start | bytes 1540
  46.9 40.3 %all-to-all-start.1 = ((bf16[32,128,128]{2,1,0:T(8,128)(2,1)}), bf16[32,128,128]{2,1,0:T(8,128)(2,1)S(1)}, u32[]{:S(2)}, u32[]{:S(2)}) async-start(bf16[32,128,128]{2,1,0:T(8,128)(2,1)} %copy-done.1), calls=%async_computation.1 | async-start | bytes 2097152 | tf_op jit(solution)/shard_map/all_to_all | solution.py:184
  60.7 0.9 copy-start.5
  61.6 0.8 copy-start.10
  62.5 24.8 %copy-start.2 = (f32[256,256]{1,0:T(8,128)S(1)}, f32[256,256]{1,0:T(8,128)}, u32[]{:S(2)}) copy-start(f32[256,256]{1,0:T(8,128)} %weight.3) | copy-start | bytes 786436
  62.7 0.7 copy-start.6
  63.4 0.7 copy-start.8
  64.0 0.6 copy-start.11
  64.7 0.6 copy-start.13
  87.2 0.9 copy-start.7
  88.1 0.9 copy-start.9
  124.8 34.1 %copy-start.4 = (f32[128,256]{1,0:T(8,128)S(1)}, f32[128,256]{1,0:T(8,128)}, u32[]{:S(2)}) copy-start(f32[128,256]{1,0:T(8,128)} %get-tuple-element.12.states) | copy-start | bytes 393220
  124.9 34.1 %copy-start.12 = (f32[128,128]{1,0:T(8,128)S(1)}, f32[128,128]{1,0:T(8,128)}, u32[]{:S(2)}) copy-start(f32[128,128]{1,0:T(8,128)} %copy-done.11) | copy-start | bytes 196612
  124.9 34.1 %copy-start.14 = (f32[128,128]{1,0:T(8,128)S(1)}, f32[128,128]{1,0:T(8,128)}, u32[]{:S(2)}) copy-start(f32[128,128]{1,0:T(8,128)} %copy-done.13) | copy-start | bytes 196612
